TPU v7x, 512 devices: a whole 4x8x8 slice. The times are simulated.
512 devices in a mesh: gx: 4 (over y_lo), gy: 128 (over z, y_hi, x, core).
Axes of the slice: x: 4, y: 8 (y_hi: 2, y_lo: 4; y = y_hi * 4 + y_lo), z: 8, core: 2. Of those that a mesh axis runs over, the one named last changes fastest.
Arguments:
- traces: bfloat16 [8, 256, 128, 256], P('gx', 'gy'), may hold values from -6 to 6
- aperture: int32 [8, 256, 9], P('gx', 'gy'), may hold values 0 or 1
- geometry: int32 [8, 256, 3, 128], P('gx', 'gy'), may hold values from 0 to 1023, as said below
- trace_weight: bfloat16 [8, 256, 128], P('gx', 'gy'), may hold values from 0.0087890625 to 0.03515625
- class_weight: float32 [14], replicated, may hold values from 0.3 to 1.5
- traveltime: int32 [14, 256], replicated, may hold values from 0 to 1114
Outputs:
- image: float32 [64, 1024, 256], P('gx', 'gy')
Inputs may be any that keep to these rules, and one draw needn't show every extreme that they name: Row 0 of a trace's geometry is an inline midpoint among the 16 image columns of its block's tile, row 1 a crossline midpoint among its tile's 8 columns, row 2 an offset class below 8.
All inputs are finite; a program needn't handle non-finite values. No bound on the sum of `aperture` on one device may be relied on, other than what follows from the above.
Results may differ from a plain program's by a relative error of at most 0.0029.
Values may be sent and summed in bfloat16 or wider, within the bound.
No kernel may reach another device: no remote copies, remote signals or barrier semaphores. Data moves between devices by JAX's collectives and lax.ppermute only.
A program may use at most 64 MiB of HBM per device.

v0:
```python
import jax
import jax.numpy as jnp
from jax import lax
from jax.sharding import PartitionSpec as P

NS = 256
NTIME = 256
PX = 16
PY = 8
DSTEP = 8


def padded(cells, sides, width):
    for axis, dim in sides:
        count = lax.axis_size(axis)
        ends = count - 1
        head = lax.slice_in_dim(cells, 0, width, axis=dim)
        tail = lax.slice_in_dim(cells, cells.shape[dim] - width, cells.shape[dim], axis=dim)
        cells = jnp.concatenate(
            [
                lax.ppermute(tail, axis, [(i, (i + 1) % count) for i in range(ends)]),
                cells,
                lax.ppermute(head, axis, [((i + 1) % count, i) for i in range(ends)]),
            ],
            axis=dim,
        )
    return cells


def migrate(samples_in, live_weights, geometry, tile_x, tile_y, traveltime, class_weight):
    points = jnp.arange(PX * PY, dtype=jnp.int32)
    point_x = tile_x * PX + points // PY
    point_y = tile_y * PY + points % PY
    distance = jnp.abs(point_x[:, None] - geometry[0][None, :]) + jnp.abs(
        point_y[:, None] - geometry[1][None, :]
    )
    classes = geometry[2][None, :] + distance // DSTEP
    sample_ids = jnp.arange(NS, dtype=jnp.int32)[:, None]

    def add_class(level, image):
        scaled = (live_weights * class_weight[level]).astype(jnp.bfloat16)
        amplitude = jnp.where(classes == level, scaled[None, :], jnp.zeros((), jnp.bfloat16))
        stacked = jnp.dot(amplitude, samples_in, preferred_element_type=jnp.float32)
        quarter = traveltime[level]
        first_sample = quarter // 4
        fraction = (quarter % 4).astype(jnp.float32) * 0.25
        interp = jnp.where(
            sample_ids == first_sample[None, :], 1.0 - fraction[None, :], 0.0
        ) + jnp.where(sample_ids == first_sample[None, :] + 1, fraction[None, :], 0.0)
        return image + jnp.dot(
            stacked, interp, precision=lax.Precision.HIGHEST, preferred_element_type=jnp.float32
        )

    return lax.fori_loop(
        0, class_weight.shape[0], add_class, jnp.zeros((PX * PY, NTIME), jnp.float32)
    )


def per_device(traces, aperture, geometry, trace_weight, class_weight, traveltime):
    blocks = traces.shape[0]
    tile_x = lax.axis_index("gx")
    tile_y = lax.axis_index("gy")
    near_traces, near_weight = (
        padded(traces, (("gx", 0), ("gy", 1)), blocks),
        padded(trace_weight, (("gx", 0), ("gy", 1)), blocks),
    )
    near_aperture, near_geometry = (
        padded(aperture, (("gx", 0), ("gy", 1)), blocks),
        padded(geometry, (("gx", 0), ("gy", 1)), blocks),
    )
    offset = jnp.arange(3 * blocks, dtype=jnp.int32) // blocks - 1
    wanted = (1 - offset)[:, None] * 3 + (1 - offset)[None, :]
    choose = (jnp.arange(9, dtype=jnp.int32)[None, None, :] == wanted[:, :, None]).astype(jnp.int32)
    live_block = jnp.sum(near_aperture * choose, axis=2)
    live = jnp.broadcast_to(live_block[:, :, None], near_weight.shape).reshape(-1)
    live_weights = near_weight.reshape(-1).astype(jnp.float32) * live.astype(jnp.float32)
    flat_geometry = jnp.moveaxis(near_geometry, 2, 0).reshape(3, -1)
    image = migrate(
        near_traces.reshape(-1, NS),
        live_weights,
        flat_geometry,
        tile_x,
        tile_y,
        traveltime,
        class_weight,
    )
    return image.reshape(PX, PY, NTIME)


def solution(mesh):
    return jax.shard_map(
        per_device,
        mesh=mesh,
        in_specs=(
            P("gx", "gy", None, None),
            P("gx", "gy", None),
            P("gx", "gy", None, None),
            P("gx", "gy", None),
            P(),
            P(),
        ),
        out_specs=P("gx", "gy", None),
        check_vma=False,
    )
```

profile of v0, /device:TPU:255, one launch (start us, length us, event | category | flops | bytes accessed | tf_op | source)
XLA Modules:
  0.0 170.8 jit_solution(3702176358756328754)
XLA Ops:
  1.3 4.0 %collective-permute-start.9 = (s32[2,2,9]{2,1,0:T(2,128)}, s32[2,2,9]{2,1,0:T(2,128)S(1)}, u32[]{:S(2)}, u32[]{:S(2)}) collective-permute-start(s32[2,2,9]{2,1,0:T(2,128)} %param.9), channel_id=1, source_target_pairs={{128,0},{256,128},{384,256},{129,1},{257,129},{385,257},{130,2},{2... | collective-permute-start | bytes 440 | tf_op jit(solution)/shard_map/ppermute | solution.py:23
  5.3 1.3 collective-permute-start.4
  6.6 4.0 %collective-permute-start.5 = (bf16[2,2,128]{2,1,0:T(2,128)(2,1)}, bf16[2,2,128]{2,1,0:T(2,128)(2,1)S(1)}, u32[]{:S(2)}, u32[]{:S(2)}) collective-permute-start(bf16[2,2,128]{2,1,0:T(2,128)(2,1)} %param.11), channel_id=1, source_target_pairs={{128,0},{256,128},{384,256},{129,1},{257,129},{385,257},{130,2},{2... | collective-permute-start | bytes 3080 | tf_op jit(solution)/shard_map/ppermute | solution.py:23
  10.6 1.3 collective-permute-start
  12.7 9.0 %collective-permute-start.10 = (s32[6,2,9]{2,1,0:T(2,128)S(1)}, s32[6,2,9]{2,1,0:T(2,128)S(1)}, u32[]{:S(2)}, u32[]{:S(2)}) collective-permute-start(s32[6,2,9]{2,1,0:T(2,128)S(1)} %constant_dynamic-update-slice_fusion.3), channel_id=1, source_target_pairs={{0,1},{1,2},{2,3},{3,4},{4,5},{5,6},{6,7},{7,8},{8,9},{9,10},{10,1... | collective-permute-start | bytes 1304 | tf_op jit(solution)/shard_map/ppermute | solution.py:21
  21.7 1.9 %collective-permute-start.11 = (s32[6,2,9]{2,1,0:T(2,128)S(1)}, s32[6,2,9]{2,1,0:T(2,128)S(1)}, u32[]{:S(2)}, u32[]{:S(2)}) collective-permute-start(s32[6,2,9]{2,1,0:T(2,128)S(1)} %constant_dynamic-update-slice_fusion.3), channel_id=1, source_target_pairs={{1,0},{2,1},{3,2},{4,3},{5,4},{6,5},{7,6},{8,7},{9,8},{10,9},{11,1... | collective-permute-start | bytes 1304 | tf_op jit(solution)/shard_map/ppermute | solution.py:23
  23.7 4.3 %collective-permute-start.1 = (s32[2,2,3,128]{3,1,2,0:T(2,128)}, s32[2,2,3,128]{3,1,2,0:T(2,128)S(1)}, u32[]{:S(2)}, u32[]{:S(2)}) collective-permute-start(s32[2,2,3,128]{3,1,2,0:T(2,128)} %param.10), channel_id=1, source_target_pairs={{128,0},{256,128},{384,256},{129,1},{257,129},{385,257},{130,2},{2... | collective-permute-start | bytes 18440 | tf_op jit(solution)/shard_map/ppermute | solution.py:23
  28.0 6.8 %collective-permute-done.11 = s32[6,2,9]{2,1,0:T(2,128)S(1)} collective-permute-done((s32[6,2,9]{2,1,0:T(2,128)S(1)}, s32[6,2,9]{2,1,0:T(2,128)S(1)}, u32[]{:S(2)}, u32[]{:S(2)}) %collective-permute-start.11) | collective-permute-done | bytes 464 | tf_op jit(solution)/shard_map/ppermute | solution.py:23
  36.4 4.9 %collective-permute-start.13 = (bf16[2,2,128,256]{3,2,1,0:T(8,128)(2,1)}, bf16[2,2,128,256]{3,2,1,0:T(8,128)(2,1)S(1)}, u32[]{:S(2)}, u32[]{:S(2)}) collective-permute-start(bf16[2,2,128,256]{3,2,1,0:T(8,128)(2,1)} %param.8), channel_id=1, source_target_pairs={{128,0},{256,128},{384,256},{129,1},{257,129},{385,257},{130,2},{2... | collective-permute-start | bytes 786440 | tf_op jit(solution)/shard_map/ppermute | solution.py:23
  42.0 4.9 %collective-permute-start.6 = (bf16[6,2,128]{2,1,0:T(2,128)(2,1)S(1)}, bf16[6,2,128]{2,1,0:T(2,128)(2,1)S(1)}, u32[]{:S(2)}, u32[]{:S(2)}) collective-permute-start(bf16[6,2,128]{2,1,0:T(2,128)(2,1)S(1)} %constant_dynamic-update-slice_fusion), channel_id=1, source_target_pairs={{0,1},{1,2},{2,3},{3,4},{4,5},{5,6},{6,7},{7,8},{8,9},{9,10},{10,1... | collective-permute-start | bytes 9224 | tf_op jit(solution)/shard_map/ppermute | solution.py:21
  46.9 1.9 %collective-permute-start.7 = (bf16[6,2,128]{2,1,0:T(2,128)(2,1)S(1)}, bf16[6,2,128]{2,1,0:T(2,128)(2,1)S(1)}, u32[]{:S(2)}, u32[]{:S(2)}) collective-permute-start(bf16[6,2,128]{2,1,0:T(2,128)(2,1)S(1)} %constant_dynamic-update-slice_fusion), channel_id=1, source_target_pairs={{1,0},{2,1},{3,2},{4,3},{5,4},{6,5},{7,6},{8,7},{9,8},{10,9},{11,1... | collective-permute-start | bytes 9224 | tf_op jit(solution)/shard_map/ppermute | solution.py:23
  49.9 11.8 %collective-permute-start.14 = (bf16[6,2,128,256]{3,2,1,0:T(8,128)(2,1)S(1)}, bf16[6,2,128,256]{3,2,1,0:T(8,128)(2,1)S(1)}, u32[]{:S(2)}, u32[]{:S(2)}) collective-permute-start(bf16[6,2,128,256]{3,2,1,0:T(8,128)(2,1)S(1)} %constant_dynamic-update-slice_fusion.6), channel_id=1, source_target_pairs={{0,1},{1,2},{2,3},{3,4},{4,5},{5,6},{6,7},{7,8},{8,9},{9,10},{10,1... | collective-permute-start | bytes 2359304 | tf_op jit(solution)/shard_map/ppermute | solution.py:21
  61.7 1.9 %collective-permute-start.15 = (bf16[6,2,128,256]{3,2,1,0:T(8,128)(2,1)S(1)}, bf16[6,2,128,256]{3,2,1,0:T(8,128)(2,1)}, u32[]{:S(2)}, u32[]{:S(2)}) collective-permute-start(bf16[6,2,128,256]{3,2,1,0:T(8,128)(2,1)S(1)} %constant_dynamic-update-slice_fusion.6), channel_id=1, source_target_pairs={{1,0},{2,1},{3,2},{4,3},{5,4},{6,5},{7,6},{8,7},{9,8},{10,9},{11,1... | collective-permute-start | bytes 2359304 | tf_op jit(solution)/shard_map/ppermute | solution.py:23
  64.3 11.8 %collective-permute-start.2 = (s32[6,2,3,128]{3,1,2,0:T(2,128)S(1)}, s32[6,2,3,128]{3,1,2,0:T(2,128)S(1)}, u32[]{:S(2)}, u32[]{:S(2)}) collective-permute-start(s32[6,2,3,128]{3,1,2,0:T(2,128)S(1)} %constant_dynamic-update-slice_fusion.9), channel_id=1, source_target_pairs={{0,1},{1,2},{2,3},{3,4},{4,5},{5,6},{6,7},{7,8},{8,9},{9,10},{10,1... | collective-permute-start | bytes 55304 | tf_op jit(solution)/shard_map/ppermute | solution.py:21
  76.1 1.9 %collective-permute-start.3 = (s32[6,2,3,128]{3,1,2,0:T(2,128)S(1)}, s32[6,2,3,128]{3,1,2,0:T(2,128)S(1)}, u32[]{:S(2)}, u32[]{:S(2)}) collective-permute-start(s32[6,2,3,128]{3,1,2,0:T(2,128)S(1)} %constant_dynamic-update-slice_fusion.9), channel_id=1, source_target_pairs={{1,0},{2,1},{3,2},{4,3},{5,4},{6,5},{7,6},{8,7},{9,8},{10,9},{11,1... | collective-permute-start | bytes 55304 | tf_op jit(solution)/shard_map/ppermute | solution.py:23
  79.1 12.6 %collective-permute-done.3 = s32[6,2,3,128]{3,1,2,0:T(2,128)S(1)} collective-permute-done((s32[6,2,3,128]{3,1,2,0:T(2,128)S(1)}, s32[6,2,3,128]{3,1,2,0:T(2,128)S(1)}, u32[]{:S(2)}, u32[]{:S(2)}) %collective-permute-start.3) | collective-permute-done | bytes 18464 | tf_op jit(solution)/shard_map/ppermute | solution.py:23
  92.7 1.6 pad_maximum_fusion
  94.3 75.8 %while.17 = (s32[]{:T(128)}, f32[128,256]{1,0:T(8,128)S(1)}, f32[14]{0:T(128)S(1)}, f32[4608]{0:T(1024)S(1)}, bf16[4608,256]{1,0:T(8,128)(2,1)S(1)}, /*index=5*/...) while((s32[]{:T(128)}, f32[128,256]{1,0:T(8,128)S(1)}, ...), condition=%wide.region_2.3_spmd.clone.clone, body=%wide.region_1.2_spmd.clone.clone.sunk | while | flops 416628480 | bytes 2989219 | solution.py:54
  95.6 2.3 %fusion.60 = f32[128,256]{1,0:T(8,128)S(1)} fusion(bf16[4608,256]{1,0:T(8,128)(2,1)S(1)} %get-tuple-element.416, s32[4608]{0:T(1024)S(1)} %get-tuple-element.420, s32[128]{0:T(128)S(1)} %get-tuple-element.421, s32[4608]{0:T(1024)S(1)} %get-tuple-element.418, s32[128]{0:T(128)S(1)} %get-tuple-element.419, s32[4608]{0:T(1024)S(1)} %get-tuple-element.422, ...), kind=kOutput, calls=%fused_computation.14.clone.1 | convolution fusion | flops 315555840 | bytes 2555908 | tf_op jit(solution)/shard_map/while/body/eval_jaxpr/dot_general | solution.py:43
  101.0 2.3 %fusion.60 = f32[128,256]{1,0:T(8,128)S(1)} fusion(bf16[4608,256]{1,0:T(8,128)(2,1)S(1)} %get-tuple-element.416, s32[4608]{0:T(1024)S(1)} %get-tuple-element.420, s32[128]{0:T(128)S(1)} %get-tuple-element.421, s32[4608]{0:T(1024)S(1)} %get-tuple-element.418, s32[128]{0:T(128)S(1)} %get-tuple-element.419, s32[4608]{0:T(1024)S(1)} %get-tuple-element.422, ...), kind=kOutput, calls=%fused_computation.14.clone.1 | convolution fusion | flops 315555840 | bytes 2555908 | tf_op jit(solution)/shard_map/while/body/eval_jaxpr/dot_general | solution.py:43
  106.4 2.3 %fusion.60 = f32[128,256]{1,0:T(8,128)S(1)} fusion(bf16[4608,256]{1,0:T(8,128)(2,1)S(1)} %get-tuple-element.416, s32[4608]{0:T(1024)S(1)} %get-tuple-element.420, s32[128]{0:T(128)S(1)} %get-tuple-element.421, s32[4608]{0:T(1024)S(1)} %get-tuple-element.418, s32[128]{0:T(128)S(1)} %get-tuple-element.419, s32[4608]{0:T(1024)S(1)} %get-tuple-element.422, ...), kind=kOutput, calls=%fused_computation.14.clone.1 | convolution fusion | flops 315555840 | bytes 2555908 | tf_op jit(solution)/shard_map/while/body/eval_jaxpr/dot_general | solution.py:43
  111.9 2.3 %fusion.60 = f32[128,256]{1,0:T(8,128)S(1)} fusion(bf16[4608,256]{1,0:T(8,128)(2,1)S(1)} %get-tuple-element.416, s32[4608]{0:T(1024)S(1)} %get-tuple-element.420, s32[128]{0:T(128)S(1)} %get-tuple-element.421, s32[4608]{0:T(1024)S(1)} %get-tuple-element.418, s32[128]{0:T(128)S(1)} %get-tuple-element.419, s32[4608]{0:T(1024)S(1)} %get-tuple-element.422, ...), kind=kOutput, calls=%fused_computation.14.clone.1 | convolution fusion | flops 315555840 | bytes 2555908 | tf_op jit(solution)/shard_map/while/body/eval_jaxpr/dot_general | solution.py:43
  117.3 2.3 %fusion.60 = f32[128,256]{1,0:T(8,128)S(1)} fusion(bf16[4608,256]{1,0:T(8,128)(2,1)S(1)} %get-tuple-element.416, s32[4608]{0:T(1024)S(1)} %get-tuple-element.420, s32[128]{0:T(128)S(1)} %get-tuple-element.421, s32[4608]{0:T(1024)S(1)} %get-tuple-element.418, s32[128]{0:T(128)S(1)} %get-tuple-element.419, s32[4608]{0:T(1024)S(1)} %get-tuple-element.422, ...), kind=kOutput, calls=%fused_computation.14.clone.1 | convolution fusion | flops 315555840 | bytes 2555908 | tf_op jit(solution)/shard_map/while/body/eval_jaxpr/dot_general | solution.py:43
  122.7 2.3 %fusion.60 = f32[128,256]{1,0:T(8,128)S(1)} fusion(bf16[4608,256]{1,0:T(8,128)(2,1)S(1)} %get-tuple-element.416, s32[4608]{0:T(1024)S(1)} %get-tuple-element.420, s32[128]{0:T(128)S(1)} %get-tuple-element.421, s32[4608]{0:T(1024)S(1)} %get-tuple-element.418, s32[128]{0:T(128)S(1)} %get-tuple-element.419, s32[4608]{0:T(1024)S(1)} %get-tuple-element.422, ...), kind=kOutput, calls=%fused_computation.14.clone.1 | convolution fusion | flops 315555840 | bytes 2555908 | tf_op jit(solution)/shard_map/while/body/eval_jaxpr/dot_general | solution.py:43
  128.1 2.3 %fusion.60 = f32[128,256]{1,0:T(8,128)S(1)} fusion(bf16[4608,256]{1,0:T(8,128)(2,1)S(1)} %get-tuple-element.416, s32[4608]{0:T(1024)S(1)} %get-tuple-element.420, s32[128]{0:T(128)S(1)} %get-tuple-element.421, s32[4608]{0:T(1024)S(1)} %get-tuple-element.418, s32[128]{0:T(128)S(1)} %get-tuple-element.419, s32[4608]{0:T(1024)S(1)} %get-tuple-element.422, ...), kind=kOutput, calls=%fused_computation.14.clone.1 | convolution fusion | flops 315555840 | bytes 2555908 | tf_op jit(solution)/shard_map/while/body/eval_jaxpr/dot_general | solution.py:43
  133.5 2.3 %fusion.60 = f32[128,256]{1,0:T(8,128)S(1)} fusion(bf16[4608,256]{1,0:T(8,128)(2,1)S(1)} %get-tuple-element.416, s32[4608]{0:T(1024)S(1)} %get-tuple-element.420, s32[128]{0:T(128)S(1)} %get-tuple-element.421, s32[4608]{0:T(1024)S(1)} %get-tuple-element.418, s32[128]{0:T(128)S(1)} %get-tuple-element.419, s32[4608]{0:T(1024)S(1)} %get-tuple-element.422, ...), kind=kOutput, calls=%fused_computation.14.clone.1 | convolution fusion | flops 315555840 | bytes 2555908 | tf_op jit(solution)/shard_map/while/body/eval_jaxpr/dot_general | solution.py:43
  139.0 2.3 %fusion.60 = f32[128,256]{1,0:T(8,128)S(1)} fusion(bf16[4608,256]{1,0:T(8,128)(2,1)S(1)} %get-tuple-element.416, s32[4608]{0:T(1024)S(1)} %get-tuple-element.420, s32[128]{0:T(128)S(1)} %get-tuple-element.421, s32[4608]{0:T(1024)S(1)} %get-tuple-element.418, s32[128]{0:T(128)S(1)} %get-tuple-element.419, s32[4608]{0:T(1024)S(1)} %get-tuple-element.422, ...), kind=kOutput, calls=%fused_computation.14.clone.1 | convolution fusion | flops 315555840 | bytes 2555908 | tf_op jit(solution)/shard_map/while/body/eval_jaxpr/dot_general | solution.py:43
  144.4 2.3 %fusion.60 = f32[128,256]{1,0:T(8,128)S(1)} fusion(bf16[4608,256]{1,0:T(8,128)(2,1)S(1)} %get-tuple-element.416, s32[4608]{0:T(1024)S(1)} %get-tuple-element.420, s32[128]{0:T(128)S(1)} %get-tuple-element.421, s32[4608]{0:T(1024)S(1)} %get-tuple-element.418, s32[128]{0:T(128)S(1)} %get-tuple-element.419, s32[4608]{0:T(1024)S(1)} %get-tuple-element.422, ...), kind=kOutput, calls=%fused_computation.14.clone.1 | convolution fusion | flops 315555840 | bytes 2555908 | tf_op jit(solution)/shard_map/while/body/eval_jaxpr/dot_general | solution.py:43
  149.8 2.3 %fusion.60 = f32[128,256]{1,0:T(8,128)S(1)} fusion(bf16[4608,256]{1,0:T(8,128)(2,1)S(1)} %get-tuple-element.416, s32[4608]{0:T(1024)S(1)} %get-tuple-element.420, s32[128]{0:T(128)S(1)} %get-tuple-element.421, s32[4608]{0:T(1024)S(1)} %get-tuple-element.418, s32[128]{0:T(128)S(1)} %get-tuple-element.419, s32[4608]{0:T(1024)S(1)} %get-tuple-element.422, ...), kind=kOutput, calls=%fused_computation.14.clone.1 | convolution fusion | flops 315555840 | bytes 2555908 | tf_op jit(solution)/shard_map/while/body/eval_jaxpr/dot_general | solution.py:43
  155.2 2.3 %fusion.60 = f32[128,256]{1,0:T(8,128)S(1)} fusion(bf16[4608,256]{1,0:T(8,128)(2,1)S(1)} %get-tuple-element.416, s32[4608]{0:T(1024)S(1)} %get-tuple-element.420, s32[128]{0:T(128)S(1)} %get-tuple-element.421, s32[4608]{0:T(1024)S(1)} %get-tuple-element.418, s32[128]{0:T(128)S(1)} %get-tuple-element.419, s32[4608]{0:T(1024)S(1)} %get-tuple-element.422, ...), kind=kOutput, calls=%fused_computation.14.clone.1 | convolution fusion | flops 315555840 | bytes 2555908 | tf_op jit(solution)/shard_map/while/body/eval_jaxpr/dot_general | solution.py:43
  160.6 2.3 %fusion.60 = f32[128,256]{1,0:T(8,128)S(1)} fusion(bf16[4608,256]{1,0:T(8,128)(2,1)S(1)} %get-tuple-element.416, s32[4608]{0:T(1024)S(1)} %get-tuple-element.420, s32[128]{0:T(128)S(1)} %get-tuple-element.421, s32[4608]{0:T(1024)S(1)} %get-tuple-element.418, s32[128]{0:T(128)S(1)} %get-tuple-element.419, s32[4608]{0:T(1024)S(1)} %get-tuple-element.422, ...), kind=kOutput, calls=%fused_computation.14.clone.1 | convolution fusion | flops 315555840 | bytes 2555908 | tf_op jit(solution)/shard_map/while/body/eval_jaxpr/dot_general | solution.py:43
  166.0 2.3 %fusion.60 = f32[128,256]{1,0:T(8,128)S(1)} fusion(bf16[4608,256]{1,0:T(8,128)(2,1)S(1)} %get-tuple-element.416, s32[4608]{0:T(1024)S(1)} %get-tuple-element.420, s32[128]{0:T(128)S(1)} %get-tuple-element.421, s32[4608]{0:T(1024)S(1)} %get-tuple-element.418, s32[128]{0:T(128)S(1)} %get-tuple-element.419, s32[4608]{0:T(1024)S(1)} %get-tuple-element.422, ...), kind=kOutput, calls=%fused_computation.14.clone.1 | convolution fusion | flops 315555840 | bytes 2555908 | tf_op jit(solution)/shard_map/while/body/eval_jaxpr/dot_general | solution.py:43
  (117 shorter events, 51.8 us)
Async XLA Ops:
  0.0 12.0 %collective-permute-start.8 = (s32[2,2,9]{2,1,0:T(2,128)}, s32[2,2,9]{2,1,0:T(2,128)S(1)}, u32[]{:S(2)}, u32[]{:S(2)}) collective-permute-start(s32[2,2,9]{2,1,0:T(2,128)} %param.9), channel_id=1, source_target_pairs={{0,128},{128,256},{256,384},{1,129},{129,257},{257,385},{2,130},{1... | collective-permute-start | bytes 440 | tf_op jit(solution)/shard_map/ppermute | solution.py:21
  1.3 11.4 %collective-permute-start.9 = (s32[2,2,9]{2,1,0:T(2,128)}, s32[2,2,9]{2,1,0:T(2,128)S(1)}, u32[]{:S(2)}, u32[]{:S(2)}) collective-permute-start(s32[2,2,9]{2,1,0:T(2,128)} %param.9), channel_id=1, source_target_pairs={{128,0},{256,128},{384,256},{129,1},{257,129},{385,257},{130,2},{2... | collective-permute-start | bytes 440 | tf_op jit(solution)/shard_map/ppermute | solution.py:23
  5.3 31.1 %collective-permute-start.4 = (bf16[2,2,128]{2,1,0:T(2,128)(2,1)}, bf16[2,2,128]{2,1,0:T(2,128)(2,1)S(1)}, u32[]{:S(2)}, u32[]{:S(2)}) collective-permute-start(bf16[2,2,128]{2,1,0:T(2,128)(2,1)} %param.11), channel_id=1, source_target_pairs={{0,128},{128,256},{256,384},{1,129},{129,257},{257,385},{2,130},{1... | collective-permute-start | bytes 3080 | tf_op jit(solution)/shard_map/ppermute | solution.py:21
  6.6 35.4 %collective-permute-start.5 = (bf16[2,2,128]{2,1,0:T(2,128)(2,1)}, bf16[2,2,128]{2,1,0:T(2,128)(2,1)S(1)}, u32[]{:S(2)}, u32[]{:S(2)}) collective-permute-start(bf16[2,2,128]{2,1,0:T(2,128)(2,1)} %param.11), channel_id=1, source_target_pairs={{128,0},{256,128},{384,256},{129,1},{257,129},{385,257},{130,2},{2... | collective-permute-start | bytes 3080 | tf_op jit(solution)/shard_map/ppermute | solution.py:23
  10.6 36.3 %collective-permute-start = (s32[2,2,3,128]{3,1,2,0:T(2,128)}, s32[2,2,3,128]{3,1,2,0:T(2,128)S(1)}, u32[]{:S(2)}, u32[]{:S(2)}) collective-permute-start(s32[2,2,3,128]{3,1,2,0:T(2,128)} %param.10), channel_id=1, source_target_pairs={{0,128},{128,256},{256,384},{1,129},{129,257},{257,385},{2,130},{1... | collective-permute-start | bytes 18440 | tf_op jit(solution)/shard_map/ppermute | solution.py:21
  12.7 11.0 %collective-permute-start.10 = (s32[6,2,9]{2,1,0:T(2,128)S(1)}, s32[6,2,9]{2,1,0:T(2,128)S(1)}, u32[]{:S(2)}, u32[]{:S(2)}) collective-permute-start(s32[6,2,9]{2,1,0:T(2,128)S(1)} %constant_dynamic-update-slice_fusion.3), channel_id=1, source_target_pairs={{0,1},{1,2},{2,3},{3,4},{4,5},{5,6},{6,7},{7,8},{8,9},{9,10},{10,1... | collective-permute-start | bytes 1304 | tf_op jit(solution)/shard_map/ppermute | solution.py:21
  21.7 13.1 %collective-permute-start.11 = (s32[6,2,9]{2,1,0:T(2,128)S(1)}, s32[6,2,9]{2,1,0:T(2,128)S(1)}, u32[]{:S(2)}, u32[]{:S(2)}) collective-permute-start(s32[6,2,9]{2,1,0:T(2,128)S(1)} %constant_dynamic-update-slice_fusion.3), channel_id=1, source_target_pairs={{1,0},{2,1},{3,2},{4,3},{5,4},{6,5},{7,6},{8,7},{9,8},{10,9},{11,1... | collective-permute-start | bytes 1304 | tf_op jit(solution)/shard_map/ppermute | solution.py:23
  23.7 40.6 %collective-permute-start.1 = (s32[2,2,3,128]{3,1,2,0:T(2,128)}, s32[2,2,3,128]{3,1,2,0:T(2,128)S(1)}, u32[]{:S(2)}, u32[]{:S(2)}) collective-permute-start(s32[2,2,3,128]{3,1,2,0:T(2,128)} %param.10), channel_id=1, source_target_pairs={{128,0},{256,128},{384,256},{129,1},{257,129},{385,257},{130,2},{2... | collective-permute-start | bytes 18440 | tf_op jit(solution)/shard_map/ppermute | solution.py:23
  34.8 14.0 %collective-permute-start.12 = (bf16[2,2,128,256]{3,2,1,0:T(8,128)(2,1)}, bf16[2,2,128,256]{3,2,1,0:T(8,128)(2,1)S(1)}, u32[]{:S(2)}, u32[]{:S(2)}) collective-permute-start(bf16[2,2,128,256]{3,2,1,0:T(8,128)(2,1)} %param.8), channel_id=1, source_target_pairs={{0,128},{128,256},{256,384},{1,129},{129,257},{257,385},{2,130},{1... | collective-permute-start | bytes 786440 | tf_op jit(solution)/shard_map/ppermute | solution.py:21
  36.4 13.5 %collective-permute-start.13 = (bf16[2,2,128,256]{3,2,1,0:T(8,128)(2,1)}, bf16[2,2,128,256]{3,2,1,0:T(8,128)(2,1)S(1)}, u32[]{:S(2)}, u32[]{:S(2)}) collective-permute-start(bf16[2,2,128,256]{3,2,1,0:T(8,128)(2,1)} %param.8), channel_id=1, source_target_pairs={{128,0},{256,128},{384,256},{129,1},{257,129},{385,257},{130,2},{2... | collective-permute-start | bytes 786440 | tf_op jit(solution)/shard_map/ppermute | solution.py:23
  42.0 34.1 %collective-permute-start.6 = (bf16[6,2,128]{2,1,0:T(2,128)(2,1)S(1)}, bf16[6,2,128]{2,1,0:T(2,128)(2,1)S(1)}, u32[]{:S(2)}, u32[]{:S(2)}) collective-permute-start(bf16[6,2,128]{2,1,0:T(2,128)(2,1)S(1)} %constant_dynamic-update-slice_fusion), channel_id=1, source_target_pairs={{0,1},{1,2},{2,3},{3,4},{4,5},{5,6},{6,7},{7,8},{8,9},{9,10},{10,1... | collective-permute-start | bytes 9224 | tf_op jit(solution)/shard_map/ppermute | solution.py:21
  46.9 31.1 %collective-permute-start.7 = (bf16[6,2,128]{2,1,0:T(2,128)(2,1)S(1)}, bf16[6,2,128]{2,1,0:T(2,128)(2,1)S(1)}, u32[]{:S(2)}, u32[]{:S(2)}) collective-permute-start(bf16[6,2,128]{2,1,0:T(2,128)(2,1)S(1)} %constant_dynamic-update-slice_fusion), channel_id=1, source_target_pairs={{1,0},{2,1},{3,2},{4,3},{5,4},{6,5},{7,6},{8,7},{9,8},{10,9},{11,1... | collective-permute-start | bytes 9224 | tf_op jit(solution)/shard_map/ppermute | solution.py:23
  49.9 41.9 %collective-permute-start.14 = (bf16[6,2,128,256]{3,2,1,0:T(8,128)(2,1)S(1)}, bf16[6,2,128,256]{3,2,1,0:T(8,128)(2,1)S(1)}, u32[]{:S(2)}, u32[]{:S(2)}) collective-permute-start(bf16[6,2,128,256]{3,2,1,0:T(8,128)(2,1)S(1)} %constant_dynamic-update-slice_fusion.6), channel_id=1, source_target_pairs={{0,1},{1,2},{2,3},{3,4},{4,5},{5,6},{6,7},{7,8},{8,9},{9,10},{10,1... | collective-permute-start | bytes 2359304 | tf_op jit(solution)/shard_map/ppermute | solution.py:21
  61.7 31.0 %collective-permute-start.15 = (bf16[6,2,128,256]{3,2,1,0:T(8,128)(2,1)S(1)}, bf16[6,2,128,256]{3,2,1,0:T(8,128)(2,1)}, u32[]{:S(2)}, u32[]{:S(2)}) collective-permute-start(bf16[6,2,128,256]{3,2,1,0:T(8,128)(2,1)S(1)} %constant_dynamic-update-slice_fusion.6), channel_id=1, source_target_pairs={{1,0},{2,1},{3,2},{4,3},{5,4},{6,5},{7,6},{8,7},{9,8},{10,9},{11,1... | collective-permute-start | bytes 2359304 | tf_op jit(solution)/shard_map/ppermute | solution.py:23
  64.3 14.8 %collective-permute-start.2 = (s32[6,2,3,128]{3,1,2,0:T(2,128)S(1)}, s32[6,2,3,128]{3,1,2,0:T(2,128)S(1)}, u32[]{:S(2)}, u32[]{:S(2)}) collective-permute-start(s32[6,2,3,128]{3,1,2,0:T(2,128)S(1)} %constant_dynamic-update-slice_fusion.9), channel_id=1, source_target_pairs={{0,1},{1,2},{2,3},{3,4},{4,5},{5,6},{6,7},{7,8},{8,9},{9,10},{10,1... | collective-permute-start | bytes 55304 | tf_op jit(solution)/shard_map/ppermute | solution.py:21
  76.1 15.6 %collective-permute-start.3 = (s32[6,2,3,128]{3,1,2,0:T(2,128)S(1)}, s32[6,2,3,128]{3,1,2,0:T(2,128)S(1)}, u32[]{:S(2)}, u32[]{:S(2)}) collective-permute-start(s32[6,2,3,128]{3,1,2,0:T(2,128)S(1)} %constant_dynamic-update-slice_fusion.9), channel_id=1, source_target_pairs={{1,0},{2,1},{3,2},{4,3},{5,4},{6,5},{7,6},{8,7},{9,8},{10,9},{11,1... | collective-permute-start | bytes 55304 | tf_op jit(solution)/shard_map/ppermute | solution.py:23
  91.8 2.6 %copy-start.1 = (f32[14]{0:T(128)S(1)}, f32[14]{0:T(128)}, u32[]{:S(2)}) copy-start(f32[14]{0:T(128)} %param.12) | copy-start | bytes 172
  91.8 0.9 copy-start
  170.2 0.7 copy-start.2
where the time goes:
time: 173 us; the launch traced here: 171 us
  starting transfers between devices  67.4 us (39%)
  matrix products  37.4 us (22%)
  other arithmetic  31.2 us (18%)
  waiting for transfers between devices  20.4 us (12%)
  local copies, waits for them, and re-layouts  13.4 us (8%)
    ppermute x8, starting transfers between devices, padded(): lax.ppermute(tail, axis, [(i, (i + 1) % count) for i in range(ends)])  42.6 us
    dot_general x14, matrix products, add_class(): stacked = jnp.dot(amplitude, samples_in, preferred_element_type=jnp.float32)  32.2 us
    ppermute x8, starting transfers between devices, padded(): lax.ppermute(head, axis, [((i + 1) % count, i) for i in range(ends)])  24.9 us
    ppermute x8, waiting for transfers between devices, padded(): lax.ppermute(head, axis, [((i + 1) % count, i) for i in range(ends)])  19.4 us
    sub x14, other arithmetic, add_class(): 1.0 - fraction[None, :]  10.3 us
    add x14, other arithmetic, add_class(): first_sample[None, :] + 1  10 us
    convert_element_type x14, other arithmetic, add_class(): scaled = (live_weights * class_weight[level]).astype(jnp.bfloat16)  8.83 us
    dynamic_slice x14, local copies, waits for them, and re-layouts, add_class(): scaled = (live_weights * class_weight[level]).astype(jnp.bfloat16)  8.68 us
  transfers between devices with their start and end apart: 16, of which 3 were waited for; matrix products, arithmetic and copies ran while one was open for 2% of the time, Pallas kernels for 0%

commit v1 on v0

v1 whole, which is shorter than its diff:
```python
import jax
import jax.numpy as jnp
from jax import lax
from jax.experimental import pallas as pl
from jax.experimental.pallas import tpu as pltpu
from jax.sharding import PartitionSpec as P

NS = 256
NTIME = 256
PX = 16
PY = 8
DSTEP = 8
TR = 128
NH = 8
NC = 14
COLS = PX * PY
NJ = 4 * TR
NQ = (2 * PX - 1 + 2 * PY - 1) // DSTEP + 1
NQ_MID = (PX - 1 + 2 * PY - 1) // DSTEP + 1
LEVEL = 129.0
BF = jnp.bfloat16
F32 = jnp.float32


def row_of(parts):
    return jnp.concatenate(parts, axis=1)


def geometry_rows(geom_ref):
    def part(kind):
        return row_of([geom_ref[i, kind, k : k + 1, :] for i in range(2) for k in range(2)])

    return part(0), part(1), part(2)


def partners():
    dx = 1 - 2 * (lax.axis_index("gx") % 2)
    dy = 1 - 2 * (lax.axis_index("gy") % 2)
    return dx, dy


def inline_distance(dx, mx):
    px = lax.broadcasted_iota(jnp.int32, (PX, NJ), 0)
    ax = jnp.abs(px + PX * dx - (mx & (PX - 1)))
    ax = (2 * ax - (DSTEP - 1)).astype(F32) * (0.5 / DSTEP)
    ax = jnp.broadcast_to(ax[:, None, :], (PX, PY, NJ)).reshape(COLS, NJ)
    return ax.astype(BF).reshape(COLS // 16, 16, NJ)


def crossline_distance(dy, my):
    py = lax.broadcasted_iota(jnp.int32, (16, NJ), 0) % PY
    ay = jnp.abs(py + PY * dy - (my & (PY - 1)))
    return (ay.astype(F32) * (1.0 / DSTEP)).astype(BF)[None]


def class_scales(h, w_ref, cw_ref):
    w = row_of([w_ref[i, k : k + 1, :] for i in range(2) for k in range(2)]).astype(F32)
    scales = []
    for q in range(NQ):
        cw = jnp.full(h.shape, cw_ref[q], F32)
        for k in range(1, NH):
            cw = jnp.where(h == k, cw_ref[k + q], cw)
        scales.append((w * cw).astype(BF).astype(F32))
    return scales


def live_row(ap_ref, dx, dy):
    entry = (dx + 1) * 3 + dy + 1
    return row_of([jnp.full((1, TR), ap_ref[i, k, entry].astype(F32), F32) for i in range(2) for k in range(2)])


def fill_amplitudes(a_ref, at, ax, ay, scales, live, n_q):
    level = (ax + ay) + jnp.asarray(LEVEL, BF)
    for q in range(n_q):
        scale = jnp.broadcast_to(scales[q] * live, (16, NJ)).astype(BF)[None]
        a = jnp.where(level == jnp.asarray(LEVEL + q, BF), scale, jnp.zeros((), BF))
        a_ref[at : at + COLS, q * NJ : (q + 1) * NJ] = a.reshape(COLS, NJ)


def outer_kernel(ap_ref, cw_ref, traces_ref, geom_ref, w_ref, tt_ref, first_ref, second_ref, tq_ref, t_ref, a_ref):
    mx, my, h = geometry_rows(geom_ref)
    dx, dy = partners()
    sample = lax.broadcasted_iota(jnp.int32, (NS, NTIME), 0).astype(F32)
    traces = traces_ref[...]
    for c in range(NC):
        at = tt_ref[c : c + 1, :].astype(F32) * 0.25
        interp = jnp.maximum(1.0 - jnp.abs(sample - at), 0.0).astype(BF)
        t_ref[c] = jnp.dot(traces, interp, preferred_element_type=F32).astype(BF)
    hf = h.astype(F32)
    for b in range(4):
        rows = slice(b * TR, (b + 1) * TR)
        hcol = jnp.broadcast_to(hf[:, rows], (TR, TR)).T
        hcol = jnp.concatenate([hcol, hcol], axis=1).astype(BF)
        masks = [hcol == jnp.asarray(k, BF) for k in range(NH)]
        for q in range(NQ):
            picked = t_ref[q, rows, :]
            for k in range(1, NH):
                picked = jnp.where(masks[k], t_ref[k + q, rows, :], picked)
            tq_ref[q * NJ + b * TR : q * NJ + (b + 1) * TR, :] = picked
    scales = class_scales(h, w_ref, cw_ref)
    tiles_y = (-dy, dy, 0)
    ays = [crossline_distance(t, my) for t in tiles_y]
    for n, tx in enumerate((dx, -dx)):
        ax = inline_distance(tx, mx)
        for m, ty in enumerate(tiles_y):
            fill_amplitudes(a_ref, (3 * n + m) * COLS, ax, ays[m], scales, live_row(ap_ref, tx, ty), NQ)
    out = jnp.dot(a_ref[...], tq_ref[...], preferred_element_type=F32).astype(BF)
    first_ref[...] = out[: 3 * COLS]
    second_ref[...] = out[3 * COLS :]


def inner_kernel(ap_ref, cw_ref, geom_ref, w_ref, tq_ref, own_ref, a_ref):
    mx, my, h = geometry_rows(geom_ref)
    _, dy = partners()
    scales = class_scales(h, w_ref, cw_ref)
    ax = inline_distance(0, mx)
    for m, ty in enumerate((-dy, dy, 0)):
        fill_amplitudes(a_ref, m * COLS, ax, crossline_distance(ty, my), scales, live_row(ap_ref, 0, ty), NQ_MID)
    own_ref[...] = jnp.dot(a_ref[...], tq_ref[: NQ_MID * NJ, :], preferred_element_type=F32)


def swaps(axis, odd):
    n = lax.axis_size(axis)
    lower = range(1 if odd else 0, n - 1, 2)
    return [p for i in lower for p in ((i, i + 1), (i + 1, i))]


SMEM = pl.BlockSpec(memory_space=pltpu.SMEM)
VMEM = pl.BlockSpec(memory_space=pltpu.VMEM)


def per_device(traces, aperture, geometry, trace_weight, class_weight, traveltime):
    geom = jnp.transpose(geometry, (0, 2, 1, 3))
    first, second, tq = pl.pallas_call(
        outer_kernel,
        out_shape=(
            jax.ShapeDtypeStruct((3 * COLS, NTIME), BF),
            jax.ShapeDtypeStruct((3 * COLS, NTIME), BF),
            jax.ShapeDtypeStruct((NQ * NJ, NTIME), BF),
        ),
        in_specs=[SMEM, SMEM, VMEM, VMEM, VMEM, VMEM],
        out_specs=(VMEM, VMEM, VMEM),
        scratch_shapes=[pltpu.VMEM((NC, NJ, NTIME), BF), pltpu.VMEM((6 * COLS, NQ * NJ), BF)],
        name="outer",
    )(aperture, class_weight, traces.reshape(NJ, NS), geom, trace_weight, traveltime)
    from_first = lax.ppermute(first, "gx", swaps("gx", False))
    from_second = lax.ppermute(second, "gx", swaps("gx", True))
    own = pl.pallas_call(
        inner_kernel,
        out_shape=jax.ShapeDtypeStruct((3 * COLS, NTIME), F32),
        in_specs=[SMEM, SMEM, VMEM, VMEM, VMEM],
        out_specs=VMEM,
        scratch_shapes=[pltpu.VMEM((3 * COLS, NQ_MID * NJ), BF)],
        name="inner",
    )(aperture, class_weight, geom, trace_weight, tq)
    total = own + from_first.astype(F32) + from_second.astype(F32)
    odd = lax.ppermute(total[:COLS].astype(BF), "gy", swaps("gy", True))
    even = lax.ppermute(total[COLS : 2 * COLS].astype(BF), "gy", swaps("gy", False))
    image = total[2 * COLS :] + odd.astype(F32) + even.astype(F32)
    return image.reshape(PX, PY, NTIME)


def solution(mesh):
    return jax.shard_map(
        per_device,
        mesh=mesh,
        in_specs=(
            P("gx", "gy", None, None),
            P("gx", "gy", None),
            P("gx", "gy", None, None),
            P("gx", "gy", None),
            P(),
            P(),
        ),
        out_specs=P("gx", "gy", None),
        check_vma=False,
    )
```

time: 173 us -> 32.7 us (0.19)
  the two profiles are of different devices: /device:TPU:255 before, /device:TPU:272 now
where the time goes in v1:
time: 32.7 us; the launch traced here: 32.4 us
  starting transfers between devices  12.5 us (38%)
  waiting for transfers between devices  10.3 us (31%)
  Pallas kernels  7.85 us (24%)
  other arithmetic  1.73 us (5%)
    ppermute x1, waiting for transfers between devices, per_device(): odd = lax.ppermute(total[:COLS].astype(BF), 'gy', swaps('gy', True))  6.58 us
    ppermute x1, starting transfers between devices, per_device(): odd = lax.ppermute(total[:COLS].astype(BF), 'gy', swaps('gy', True))  5.2 us
    pallas_call x1, Pallas kernels, per_device(): pl.pallas_call(outer_kernel, out_shape=(jax.ShapeDtypeStruct((3 * COLS, N...  5.02 us
    ppermute x1, starting transfers between devices, per_device(): from_first = lax.ppermute(first, 'gx', swaps('gx', False))  3.47 us
    ppermute x1, waiting for transfers between devices, per_device(): from_second = lax.ppermute(second, 'gx', swaps('gx', True))  3.21 us
    pallas_call x1, Pallas kernels, per_device(): pl.pallas_call(inner_kernel, out_shape=jax.ShapeDtypeStruct((3 * COLS, NT...  2.83 us
    ppermute x1, starting transfers between devices, per_device(): lax.ppermute(total[COLS:2 * COLS].astype(BF), 'gy', swaps('gy', False))  1.92 us
    ppermute x1, starting transfers between devices, per_device(): from_second = lax.ppermute(second, 'gx', swaps('gx', True))  1.92 us
  transfers between devices with their start and end apart: 4, of which 3 were waited for; matrix products, arithmetic and copies ran while one was open for 0% of the time, Pallas kernels for 9%

profile of v1, /device:TPU:272, one launch (start us, length us, event | category | flops | bytes accessed | tf_op | source)
XLA Modules:
  0.0 32.4 jit_solution(1200509410077913020)
XLA Ops:
  0.0 5.0 %outer.1 = (bf16[384,256]{1,0:T(8,128)(2,1)}, bf16[384,256]{1,0:T(8,128)(2,1)}, bf16[3072,256]{1,0:T(8,128)(2,1)}) custom-call(s32[2,2,9]{2,1,0:T(2,128)} %ap_ref.3, f32[14]{0:T(128)} %cw_ref.3, bf16[512,256]{1,0:T(8,128)(2,1)} %bitcast.4, s32[2,3,2,128]{3,2,1,0:T(2,128)} %bitcast.5, bf16[2,2,128]{2,1,0:T(2,128)(2,1)} %w_ref.3, s32[14,256]{1,0:T(8,128)} %tt_ref.1), custom_call_target="tpu_custom_call" | custom-call | tf_op jit(solution)/shard_map/outer/pallas_call | solution.py:134
  5.0 3.5 %collective-permute-start = (bf16[384,256]{1,0:T(8,128)(2,1)}, bf16[384,256]{1,0:T(8,128)(2,1)S(1)}, u32[]{:S(2)}, u32[]{:S(2)}) collective-permute-start(bf16[384,256]{1,0:T(8,128)(2,1)} %get-tuple-element.9), channel_id=1, source_target_pairs={{0,128},{128,0},{256,384},{384,256},{1,129},{129,1},{257,385},{385... | collective-permute-start | bytes 589832 | tf_op jit(solution)/shard_map/ppermute | solution.py:146
  8.5 1.9 %collective-permute-start.1 = (bf16[384,256]{1,0:T(8,128)(2,1)}, bf16[384,256]{1,0:T(8,128)(2,1)S(1)}, u32[]{:S(2)}, u32[]{:S(2)}) collective-permute-start(bf16[384,256]{1,0:T(8,128)(2,1)} %get-tuple-element.10), channel_id=1, source_target_pairs={{128,256},{256,128},{129,257},{257,129},{130,258},{258,130},{131,2... | collective-permute-start | bytes 589832 | tf_op jit(solution)/shard_map/ppermute | solution.py:147
  10.4 2.8 %inner.1 = f32[384,256]{1,0:T(8,128)} custom-call(s32[2,2,9]{2,1,0:T(2,128)} %ap_ref.3, f32[14]{0:T(128)} %cw_ref.3, s32[2,3,2,128]{3,2,1,0:T(2,128)} %bitcast.6, bf16[2,2,128]{2,1,0:T(2,128)(2,1)} %w_ref.3, bf16[3072,256]{1,0:T(8,128)(2,1)} %get-tuple-element.8.tq_ref), custom_call_target="tpu_custom_call" | custom-call | tf_op jit(solution)/shard_map/inner/pallas_call | solution.py:148
  13.3 0.5 %collective-permute-done = bf16[384,256]{1,0:T(8,128)(2,1)S(1)} collective-permute-done((bf16[384,256]{1,0:T(8,128)(2,1)}, bf16[384,256]{1,0:T(8,128)(2,1)S(1)}, u32[]{:S(2)}, u32[]{:S(2)}) %collective-permute-start) | collective-permute-done | bytes 196640 | tf_op jit(solution)/shard_map/ppermute | solution.py:146
  13.7 3.2 %collective-permute-done.1 = bf16[384,256]{1,0:T(8,128)(2,1)S(1)} collective-permute-done((bf16[384,256]{1,0:T(8,128)(2,1)}, bf16[384,256]{1,0:T(8,128)(2,1)S(1)}, u32[]{:S(2)}, u32[]{:S(2)}) %collective-permute-start.1) | collective-permute-done | bytes 196640 | tf_op jit(solution)/shard_map/ppermute | solution.py:147
  17.0 1.1 %fusion.2 = (bf16[384,256]{1,0:T(8,128)(2,1)S(1)}, f32[384,256]{1,0:T(8,128)S(1)}) fusion(bf16[384,256]{1,0:T(8,128)(2,1)S(1)} %collective-permute-done.1, f32[384,256]{1,0:T(8,128)} %inner.1, bf16[384,256]{1,0:T(8,128)(2,1)S(1)} %collective-permute-done), kind=kLoop, calls=%fused_computation.4 | loop fusion | flops 491520 | bytes 1376256 | tf_op jit(solution)/shard_map/convert.1
  18.0 5.2 %collective-permute-start.2 = (bf16[128,256]{1,0:T(8,128)(2,1)S(1)}, bf16[128,256]{1,0:T(8,128)(2,1)S(1)}, u32[]{:S(2)}, u32[]{:S(2)}) collective-permute-start(bf16[128,256]{1,0:T(8,128)(2,1)S(1)} %get-tuple-element.13), channel_id=1, source_target_pairs={{1,2},{2,1},{3,4},{4,3},{5,6},{6,5},{7,8},{8,7},{9,10},{10,9},{11,... | collective-permute-start | bytes 196616 | tf_op jit(solution)/shard_map/ppermute | solution.py:157
  23.2 1.9 %collective-permute-start.3 = (bf16[128,256]{1,0:T(8,128)(2,1)S(1)}, bf16[128,256]{1,0:T(8,128)(2,1)S(1)}, u32[]{:S(2)}, u32[]{:S(2)}) collective-permute-start(bf16[128,256]{1,0:T(8,128)(2,1)S(1)} %get-tuple-element.14), channel_id=1, source_target_pairs={{0,1},{1,0},{2,3},{3,2},{4,5},{5,4},{6,7},{7,6},{8,9},{9,8},{10,11... | collective-permute-start | bytes 196616 | tf_op jit(solution)/shard_map/ppermute | solution.py:158
  25.2 6.6 %collective-permute-done.2 = bf16[128,256]{1,0:T(8,128)(2,1)S(1)} collective-permute-done((bf16[128,256]{1,0:T(8,128)(2,1)S(1)}, bf16[128,256]{1,0:T(8,128)(2,1)S(1)}, u32[]{:S(2)}, u32[]{:S(2)}) %collective-permute-start.2) | collective-permute-done | bytes 65568 | tf_op jit(solution)/shard_map/ppermute | solution.py:157
  31.7 0.0 collective-permute-done.3
  31.8 0.7 %fusion.1 = f32[16,8,256]{2,1,0:T(8,128)} fusion(f32[384,256]{1,0:T(8,128)S(1)} %get-tuple-element.12, bf16[128,256]{1,0:T(8,128)(2,1)S(1)} %collective-permute-done.3, bf16[128,256]{1,0:T(8,128)(2,1)S(1)} %collective-permute-done.2), kind=kLoop, calls=%fused_computation.3 | loop fusion | flops 131072 | bytes 393216 | tf_op jit(solution)/shard_map/reshape | solution.py:160
  (1 shorter events, 0.0 us)
Async XLA Ops:
  5.0 8.7 %collective-permute-start = (bf16[384,256]{1,0:T(8,128)(2,1)}, bf16[384,256]{1,0:T(8,128)(2,1)S(1)}, u32[]{:S(2)}, u32[]{:S(2)}) collective-permute-start(bf16[384,256]{1,0:T(8,128)(2,1)} %get-tuple-element.9), channel_id=1, source_target_pairs={{0,128},{128,0},{256,384},{384,256},{1,129},{129,1},{257,385},{385... | collective-permute-start | bytes 589832 | tf_op jit(solution)/shard_map/ppermute | solution.py:146
  8.5 8.5 %collective-permute-start.1 = (bf16[384,256]{1,0:T(8,128)(2,1)}, bf16[384,256]{1,0:T(8,128)(2,1)S(1)}, u32[]{:S(2)}, u32[]{:S(2)}) collective-permute-start(bf16[384,256]{1,0:T(8,128)(2,1)} %get-tuple-element.10), channel_id=1, source_target_pairs={{128,256},{256,128},{129,257},{257,129},{130,258},{258,130},{131,2... | collective-permute-start | bytes 589832 | tf_op jit(solution)/shard_map/ppermute | solution.py:147
  18.0 13.7 %collective-permute-start.2 = (bf16[128,256]{1,0:T(8,128)(2,1)S(1)}, bf16[128,256]{1,0:T(8,128)(2,1)S(1)}, u32[]{:S(2)}, u32[]{:S(2)}) collective-permute-start(bf16[128,256]{1,0:T(8,128)(2,1)S(1)} %get-tuple-element.13), channel_id=1, source_target_pairs={{1,2},{2,1},{3,4},{4,3},{5,6},{6,5},{7,8},{8,7},{9,10},{10,9},{11,... | collective-permute-start | bytes 196616 | tf_op jit(solution)/shard_map/ppermute | solution.py:157
  23.2 8.5 %collective-permute-start.3 = (bf16[128,256]{1,0:T(8,128)(2,1)S(1)}, bf16[128,256]{1,0:T(8,128)(2,1)S(1)}, u32[]{:S(2)}, u32[]{:S(2)}) collective-permute-start(bf16[128,256]{1,0:T(8,128)(2,1)S(1)} %get-tuple-element.14), channel_id=1, source_target_pairs={{0,1},{1,0},{2,3},{3,2},{4,5},{5,4},{6,7},{7,6},{8,9},{9,8},{10,11... | collective-permute-start | bytes 196616 | tf_op jit(solution)/shard_map/ppermute | solution.py:158

commit v2 on v1

v2 whole, which is shorter than its diff:
```python
import jax
import jax.numpy as jnp
from jax import lax
from jax.experimental import pallas as pl
from jax.experimental.pallas import tpu as pltpu
from jax.sharding import PartitionSpec as P


NS = 256
NTIME = 256
PX = 16
PY = 8
DSTEP = 8
TR = 128
NH = 8
NC = 14
COLS = PX * PY
NJ = 4 * TR
NQ = (2 * PX - 1 + 2 * PY - 1) // DSTEP + 1
LEVEL = 129.0
BF = jnp.bfloat16
F32 = jnp.float32


NB = 4
ROW_X, ROW_Y, ROW_SCALE, ROW_LIVE = 0, 1, 2, 2 + NQ


def row_of(parts):
    return jnp.concatenate(parts, axis=1)


def blocks(piece):
    return row_of([piece(i, k) for i in range(2) for k in range(2)])


def partners():
    dx = 1 - 2 * (lax.axis_index("gx") % 2)
    dy = 1 - 2 * (lax.axis_index("gy") % 2)
    return dx, dy


def inline_distance(dx, mx):
    px = (lax.broadcasted_iota(jnp.int32, (PX, NJ), 0) + PX * dx).astype(F32)
    ax = (2.0 * jnp.abs(px - mx) - (DSTEP - 1)) * (0.5 / DSTEP)
    ax = jnp.broadcast_to(ax[:, None, :], (PX, PY, NJ)).reshape(COLS, NJ)
    return ax.astype(BF).reshape(COLS // 16, 16, NJ)


def crossline_distance(dy, my):
    py = (lax.broadcasted_iota(jnp.int32, (16, NJ), 0) % PY + PY * dy).astype(F32)
    return (jnp.abs(py - my) * (1.0 / DSTEP)).astype(BF)[None]


def class_scales(h, w, cw_ref):
    scales = []
    for q in range(NQ):
        cw = jnp.full(h.shape, cw_ref[q], F32)
        for k in range(1, NH):
            cw = jnp.where(h == k, cw_ref[k + q], cw)
        scales.append((w * cw).astype(BF).astype(F32))
    return scales


def live_row(ap_ref, dx, dy):
    entry = (dx + 1) * 3 + dy + 1
    return blocks(lambda i, k: jnp.full((1, TR), ap_ref[i, k, entry].astype(F32), F32))


def fill_amplitudes(a_ref, at, ax, ay, scales, live, n_q):
    level = (ax + ay) + jnp.asarray(LEVEL, BF)
    for q in range(n_q):
        scale = jnp.broadcast_to(scales[q] * live, (16, NJ)).astype(BF)[None]
        a = jnp.where(level == jnp.asarray(LEVEL + q, BF), scale, jnp.zeros((), BF))
        a_ref[at : at + COLS, q * NJ : (q + 1) * NJ] = a.reshape(COLS, NJ)


def outer_kernel(
    traces_hbm, geom_hbm, w_hbm, tt_hbm, ap_hbm, cw_hbm,
    first_ref, second_ref, tq_ref, table_ref,
    traces_ref, geom_ref, w_ref, tt_ref, ap_ref, cw_ref, sems, t_ref, a_ref,
):
    pairs = (
        (tt_hbm, tt_ref), (traces_hbm, traces_ref), (geom_hbm, geom_ref),
        (w_hbm, w_ref), (cw_hbm, cw_ref), (ap_hbm, ap_ref),
    )
    copies = [pltpu.make_async_copy(a, b, sems.at[n]) for n, (a, b) in enumerate(pairs)]
    for copy in copies:
        copy.start()
    dx, dy = partners()
    sample = lax.broadcasted_iota(jnp.int32, (NS, NTIME), 0).astype(F32)
    for copy in copies:
        copy.wait()
    h = blocks(lambda i, k: geom_ref[i, 2, k : k + 1, :])
    mx = blocks(lambda i, k: geom_ref[i, 0, k : k + 1, :] & (PX - 1)).astype(F32)
    my = blocks(lambda i, k: geom_ref[i, 1, k : k + 1, :] & (PY - 1)).astype(F32)
    w = blocks(lambda i, k: w_ref[i, k : k + 1, :]).astype(F32)
    scales = class_scales(h, w, cw_ref)
    tiles = ((dx, -dy), (-dx, -dy))
    ay = crossline_distance(-dy, my)
    for n, (tx, ty) in enumerate(tiles):
        fill_amplitudes(a_ref, n * COLS, inline_distance(tx, mx), ay, scales, live_row(ap_ref, tx, ty), NQ)
    traces = traces_ref[...]
    for c in range(NC):
        at = tt_ref[c : c + 1, :].astype(F32) * 0.25
        interp = jnp.maximum(1.0 - jnp.abs(sample - at), 0.0).astype(BF)
        t_ref[c] = jnp.dot(traces, interp, preferred_element_type=F32).astype(BF)
    hf = h.astype(F32)
    for b in range(NB):
        rows = slice(b * TR, (b + 1) * TR)
        hcol = jnp.broadcast_to(hf[:, rows], (TR, TR)).T
        hcol = jnp.concatenate([hcol, hcol], axis=1).astype(BF)
        masks = [hcol == jnp.asarray(k, BF) for k in range(NH)]
        for q in range(NQ):
            picked = t_ref[q, rows, :]
            for k in range(1, NH):
                picked = jnp.where(masks[k], t_ref[k + q, rows, :], picked)
            tq_ref[q * NJ + b * TR : q * NJ + (b + 1) * TR, :] = picked
    out = jnp.dot(a_ref[...], tq_ref[...], preferred_element_type=F32).astype(BF)
    first_ref[...] = out[:COLS]
    second_ref[...] = out[COLS:]
    table_ref[ROW_X : ROW_X + 1, :] = mx
    table_ref[ROW_Y : ROW_Y + 1, :] = my
    for q in range(NQ):
        table_ref[ROW_SCALE + q : ROW_SCALE + q + 1, :] = scales[q]
    for n, (tx, ty, _) in enumerate(inner_tiles(dx, dy)):
        table_ref[ROW_LIVE + n : ROW_LIVE + n + 1, :] = live_row(ap_ref, tx, ty)


def inner_tiles(dx, dy):
    return ((dx, dy, 6), (-dx, dy, 6), (dx, 0, 5), (-dx, 0, 5), (0, -dy, 4), (0, dy, 4), (0, 0, 3))


def inner_kernel(tq_ref, table_ref, slow_ref, pair_ref, own_ref, a_ref):
    dx, dy = partners()
    tiles = inner_tiles(dx, dy)
    mx, my = table_ref[ROW_X : ROW_X + 1, :], table_ref[ROW_Y : ROW_Y + 1, :]
    scales = [table_ref[ROW_SCALE + q : ROW_SCALE + q + 1, :] for q in range(NQ)]
    axs = [inline_distance(t, mx) for t in (dx, -dx, 0)]
    ays = [crossline_distance(t, my) for t in (-dy, dy, 0)]
    which = ((0, 1), (1, 1), (0, 2), (1, 2), (2, 0), (2, 1), (2, 2))
    for n, (_, _, n_q) in enumerate(tiles):
        live = table_ref[ROW_LIVE + n : ROW_LIVE + n + 1, :]
        fill_amplitudes(a_ref, n * COLS, axs[which[n][0]], ays[which[n][1]], scales, live, n_q)

    def part(first, last, low, high):
        a = a_ref[first * COLS : last * COLS, low * NJ : high * NJ]
        return jnp.dot(a, tq_ref[low * NJ : high * NJ, :], preferred_element_type=F32)

    x = part(0, 2, 0, 6)
    pair_ref[: 2 * COLS] = x
    x = part(2, 4, 0, 5)
    own_ref[: 2 * COLS] = x
    x = part(4, 6, 0, 4)
    slow_ref[...] = x[:COLS]
    pair_ref[2 * COLS :] = x[COLS:]
    own_ref[2 * COLS :] = part(6, 7, 0, 3)


def swaps(axis, odd):
    n = lax.axis_size(axis)
    lower = range(1 if odd else 0, n - 1, 2)
    return [p for i in lower for p in ((i, i + 1), (i + 1, i))]


HBM = pl.BlockSpec(memory_space=pltpu.HBM)
VMEM = pl.BlockSpec(memory_space=pltpu.VMEM)
INNER_COST = pl.CostEstimate(flops=2 * 33 * COLS * NJ * NTIME, bytes_accessed=1 << 21, transcendentals=0)
PARAMS = pltpu.CompilerParams(vmem_limit_bytes=24 << 20)


def in_hbm(x):
    return pltpu.with_memory_space_constraint(x, pltpu.HBM)


def per_device(traces, aperture, geometry, trace_weight, class_weight, traveltime):
    geom = jnp.transpose(geometry, (0, 2, 1, 3))
    first, second, tq, table = pl.pallas_call(
        outer_kernel,
        out_shape=(
            jax.ShapeDtypeStruct((COLS, NTIME), BF),
            jax.ShapeDtypeStruct((COLS, NTIME), BF),
            jax.ShapeDtypeStruct((NQ * NJ, NTIME), BF),
            jax.ShapeDtypeStruct((16, NJ), F32),
        ),
        in_specs=[HBM] * 6,
        out_specs=(VMEM,) * 4,
        scratch_shapes=[
            pltpu.VMEM((NJ, NS), BF),
            pltpu.VMEM((2, 3, 2, TR), jnp.int32),
            pltpu.VMEM((2, 2, TR), BF),
            pltpu.VMEM((NC, NTIME), jnp.int32),
            pltpu.SMEM((2, 2, 9), jnp.int32),
            pltpu.SMEM((NC,), F32),
            pltpu.SemaphoreType.DMA((6,)),
            pltpu.VMEM((NC, NJ, NTIME), BF),
            pltpu.VMEM((2 * COLS, NQ * NJ), BF),
        ],
        compiler_params=PARAMS,
        name="outer",
    )(*(in_hbm(x) for x in (traces.reshape(NJ, NS), geom, trace_weight, traveltime, aperture, class_weight)))
    corner_first = lax.ppermute(first, "gx", swaps("gx", False))
    corner_second = lax.ppermute(second, "gx", swaps("gx", True))
    slow, pair, own = pl.pallas_call(
        inner_kernel,
        out_shape=(
            jax.ShapeDtypeStruct((COLS, NTIME), F32),
            jax.ShapeDtypeStruct((3 * COLS, NTIME), F32),
            jax.ShapeDtypeStruct((3 * COLS, NTIME), F32),
        ),
        in_specs=[VMEM] * 2,
        out_specs=(VMEM,) * 3,
        scratch_shapes=[pltpu.VMEM((7 * COLS, NQ * NJ), BF)],
        compiler_params=PARAMS,
        cost_estimate=INNER_COST,
        name="inner",
    )(tq, table)
    near = lax.ppermute(pair, "gy", swaps("gy", False))
    slow = slow + corner_first.astype(F32) + corner_second.astype(F32)
    far = lax.ppermute(slow.astype(BF), "gy", swaps("gy", True))
    own = own + near
    side_first = lax.ppermute(own[:COLS].astype(BF), "gx", swaps("gx", False))
    side_second = lax.ppermute(own[COLS : 2 * COLS].astype(BF), "gx", swaps("gx", True))
    image = own[2 * COLS :] + side_first.astype(F32) + side_second.astype(F32) + far.astype(F32)
    return image.reshape(PX, PY, NTIME)


def solution(mesh):
    return jax.shard_map(
        per_device,
        mesh=mesh,
        in_specs=(
            P("gx", "gy", None, None),
            P("gx", "gy", None),
            P("gx", "gy", None, None),
            P("gx", "gy", None),
            P(),
            P(),
        ),
        out_specs=P("gx", "gy", None),
        check_vma=False,
    )
```

time: 32.7 us -> 33.2 us (1.015)
  the two profiles are of different devices: /device:TPU:272 before, /device:TPU:328 now
where the time goes in v2:
time: 33.2 us; the launch traced here: 32.8 us
  starting transfers between devices  21.2 us (64%)
  waiting for transfers between devices  5.88 us (18%)
  Pallas kernels  4.88 us (15%)
  other arithmetic  0.76 us (2%)
    ppermute x1, starting transfers between devices, per_device(): far = lax.ppermute(slow.astype(BF), 'gy', swaps('gy', True))  7.67 us
    ppermute x1, starting transfers between devices, per_device(): corner_second = lax.ppermute(second, 'gx', swaps('gx', True))  4.61 us
    pallas_call x1, Pallas kernels, per_device(): pl.pallas_call(outer_kernel, out_shape=(jax.ShapeDtypeStruct((COLS, NTIME...  3.57 us
    ppermute x1, starting transfers between devices, per_device(): lax.ppermute(own[COLS:2 * COLS].astype(BF), 'gx', swaps('gx', True))  2.72 us
    ppermute x1, waiting for transfers between devices, per_device(): corner_second = lax.ppermute(second, 'gx', swaps('gx', True))  2.45 us
    ppermute x1, starting transfers between devices, per_device(): corner_first = lax.ppermute(first, 'gx', swaps('gx', False))  2.36 us
    ppermute x1, waiting for transfers between devices, per_device(): lax.ppermute(own[COLS:2 * COLS].astype(BF), 'gx', swaps('gx', True))  1.93 us
    ppermute x1, starting transfers between devices, per_device(): near = lax.ppermute(pair, 'gy', swaps('gy', False))  1.92 us
  transfers between devices with their start and end apart: 6, of which 4 were waited for; matrix products, arithmetic and copies ran while one was open for 0% of the time, Pallas kernels for 0%

profile of v2, /device:TPU:328, one launch (start us, length us, event | category | flops | bytes accessed | tf_op | source)
XLA Modules:
  0.0 32.8 jit_solution(6220369792290323068)
XLA Ops:
  0.0 3.6 %outer.1 = (bf16[128,256]{1,0:T(8,128)(2,1)S(1)}, bf16[128,256]{1,0:T(8,128)(2,1)S(1)}, bf16[3072,256]{1,0:T(8,128)(2,1)S(1)}, f32[16,512]{1,0:T(8,128)S(1)}) custom-call(bf16[512,256]{1,0:T(8,128)(2,1)} %bitcast.4, s32[2,3,2,128]{3,2,1,0:T(2,128)} %bitcast.5, bf16[2,2,128]{2,1,0:T(2,128)(2,1)} %w_hbm.1, s32[14,256]{1,0:T(8,128)} %tt_hbm.1, ...), custom_call_target="tpu_custom_call" | custom-call | tf_op jit(solution)/shard_map/outer/pallas_call | solution.py:178
  3.6 1.3 %inner.1 = (f32[128,256]{1,0:T(8,128)S(1)}, f32[384,256]{1,0:T(8,128)S(1)}, f32[384,256]{1,0:T(8,128)S(1)}) custom-call(bf16[3072,256]{1,0:T(8,128)(2,1)S(1)} %get-tuple-element.12.tq_ref, f32[16,512]{1,0:T(8,128)S(1)} %get-tuple-element.13.table_ref), custom_call_target="tpu_custom_call" | custom-call | flops 1107296256 | bytes 2097152 | tf_op jit(solution)/shard_map/inner/pallas_call | solution.py:204
  4.9 1.9 %collective-permute-start = (f32[384,256]{1,0:T(8,128)S(1)}, f32[384,256]{1,0:T(8,128)S(1)}, u32[]{:S(2)}, u32[]{:S(2)}) collective-permute-start(f32[384,256]{1,0:T(8,128)S(1)} %get-tuple-element.15), channel_id=1, source_target_pairs={{0,1},{1,0},{2,3},{3,2},{4,5},{5,4},{6,7},{7,6},{8,9},{9,8},{10,11... | collective-permute-start | bytes 1179656 | tf_op jit(solution)/shard_map/ppermute | solution.py:218
  6.8 2.4 %collective-permute-start.3 = (bf16[128,256]{1,0:T(8,128)(2,1)S(1)}, bf16[128,256]{1,0:T(8,128)(2,1)S(1)}, u32[]{:S(2)}, u32[]{:S(2)}) collective-permute-start(bf16[128,256]{1,0:T(8,128)(2,1)S(1)} %get-tuple-element.17), channel_id=1, source_target_pairs={{0,128},{128,0},{256,384},{384,256},{1,129},{129,1},{257,385},{385... | collective-permute-start | bytes 196616 | tf_op jit(solution)/shard_map/ppermute | solution.py:202
  9.2 4.6 %collective-permute-start.4 = (bf16[128,256]{1,0:T(8,128)(2,1)S(1)}, bf16[128,256]{1,0:T(8,128)(2,1)S(1)}, u32[]{:S(2)}, u32[]{:S(2)}) collective-permute-start(bf16[128,256]{1,0:T(8,128)(2,1)S(1)} %get-tuple-element.18), channel_id=1, source_target_pairs={{128,256},{256,128},{129,257},{257,129},{130,258},{258,130},{131,2... | collective-permute-start | bytes 196616 | tf_op jit(solution)/shard_map/ppermute | solution.py:203
  13.8 0.0 collective-permute-done.3
  13.8 2.4 %collective-permute-done.4 = bf16[128,256]{1,0:T(8,128)(2,1)S(1)} collective-permute-done((bf16[128,256]{1,0:T(8,128)(2,1)S(1)}, bf16[128,256]{1,0:T(8,128)(2,1)S(1)}, u32[]{:S(2)}, u32[]{:S(2)}) %collective-permute-start.4) | collective-permute-done | bytes 65568 | tf_op jit(solution)/shard_map/ppermute | solution.py:203
  16.3 7.7 %collective-permute-start.5 = (bf16[128,256]{1,0:T(8,128)(2,1)S(1)}, bf16[128,256]{1,0:T(8,128)(2,1)S(1)}, u32[]{:S(2)}, u32[]{:S(2)}) collective-permute-start(bf16[128,256]{1,0:T(8,128)(2,1)S(1)} %add_convert_fusion), channel_id=1, source_target_pairs={{1,2},{2,1},{3,4},{4,3},{5,6},{6,5},{7,8},{8,7},{9,10},{10,9},{11,... | collective-permute-start | bytes 196616 | tf_op jit(solution)/shard_map/ppermute | solution.py:220
  24.0 0.0 collective-permute-done
  24.0 0.1 fusion.3
  24.1 1.9 %collective-permute-start.1 = (bf16[128,256]{1,0:T(8,128)(2,1)S(1)}, bf16[128,256]{1,0:T(8,128)(2,1)S(1)}, u32[]{:S(2)}, u32[]{:S(2)}) collective-permute-start(bf16[128,256]{1,0:T(8,128)(2,1)S(1)} %get-tuple-element.21), channel_id=1, source_target_pairs={{0,128},{128,0},{256,384},{384,256},{1,129},{129,1},{257,385},{385... | collective-permute-start | bytes 196616 | tf_op jit(solution)/shard_map/ppermute | solution.py:222
  26.0 2.7 %collective-permute-start.2 = (bf16[128,256]{1,0:T(8,128)(2,1)S(1)}, bf16[128,256]{1,0:T(8,128)(2,1)S(1)}, u32[]{:S(2)}, u32[]{:S(2)}) collective-permute-start(bf16[128,256]{1,0:T(8,128)(2,1)S(1)} %get-tuple-element.22), channel_id=1, source_target_pairs={{128,256},{256,128},{129,257},{257,129},{130,258},{258,130},{131,2... | collective-permute-start | bytes 196616 | tf_op jit(solution)/shard_map/ppermute | solution.py:223
  28.7 0.2 collective-permute-done.5
  28.9 1.3 %collective-permute-done.1 = bf16[128,256]{1,0:T(8,128)(2,1)S(1)} collective-permute-done((bf16[128,256]{1,0:T(8,128)(2,1)S(1)}, bf16[128,256]{1,0:T(8,128)(2,1)S(1)}, u32[]{:S(2)}, u32[]{:S(2)}) %collective-permute-start.1) | collective-permute-done | bytes 65568 | tf_op jit(solution)/shard_map/ppermute | solution.py:222
  30.2 1.9 %collective-permute-done.2 = bf16[128,256]{1,0:T(8,128)(2,1)S(1)} collective-permute-done((bf16[128,256]{1,0:T(8,128)(2,1)S(1)}, bf16[128,256]{1,0:T(8,128)(2,1)S(1)}, u32[]{:S(2)}, u32[]{:S(2)}) %collective-permute-start.2) | collective-permute-done | bytes 65568 | tf_op jit(solution)/shard_map/ppermute | solution.py:223
  32.2 0.7 %fusion.2 = f32[16,8,256]{2,1,0:T(8,128)} fusion(f32[384,256]{1,0:T(8,128)S(1)} %get-tuple-element.20, bf16[128,256]{1,0:T(8,128)(2,1)S(1)} %collective-permute-done.5, bf16[128,256]{1,0:T(8,128)(2,1)S(1)} %collective-permute-done.2, bf16[128,256]{1,0:T(8,128)(2,1)S(1)} %collective-permute-done.1), kind=kLoop, calls=%fused_computation.3 | loop fusion | flops 196608 | bytes 458752 | tf_op jit(solution)/shard_map/reshape | solution.py:225
  (2 shorter events, 0.0 us)
Async XLA Ops:
  4.9 19.1 %collective-permute-start = (f32[384,256]{1,0:T(8,128)S(1)}, f32[384,256]{1,0:T(8,128)S(1)}, u32[]{:S(2)}, u32[]{:S(2)}) collective-permute-start(f32[384,256]{1,0:T(8,128)S(1)} %get-tuple-element.15), channel_id=1, source_target_pairs={{0,1},{1,0},{2,3},{3,2},{4,5},{5,4},{6,7},{7,6},{8,9},{9,8},{10,11... | collective-permute-start | bytes 1179656 | tf_op jit(solution)/shard_map/ppermute | solution.py:218
  6.8 7.0 %collective-permute-start.3 = (bf16[128,256]{1,0:T(8,128)(2,1)S(1)}, bf16[128,256]{1,0:T(8,128)(2,1)S(1)}, u32[]{:S(2)}, u32[]{:S(2)}) collective-permute-start(bf16[128,256]{1,0:T(8,128)(2,1)S(1)} %get-tuple-element.17), channel_id=1, source_target_pairs={{0,128},{128,0},{256,384},{384,256},{1,129},{129,1},{257,385},{385... | collective-permute-start | bytes 196616 | tf_op jit(solution)/shard_map/ppermute | solution.py:202
  9.2 7.1 %collective-permute-start.4 = (bf16[128,256]{1,0:T(8,128)(2,1)S(1)}, bf16[128,256]{1,0:T(8,128)(2,1)S(1)}, u32[]{:S(2)}, u32[]{:S(2)}) collective-permute-start(bf16[128,256]{1,0:T(8,128)(2,1)S(1)} %get-tuple-element.18), channel_id=1, source_target_pairs={{128,256},{256,128},{129,257},{257,129},{130,258},{258,130},{131,2... | collective-permute-start | bytes 196616 | tf_op jit(solution)/shard_map/ppermute | solution.py:203
  16.3 12.6 %collective-permute-start.5 = (bf16[128,256]{1,0:T(8,128)(2,1)S(1)}, bf16[128,256]{1,0:T(8,128)(2,1)S(1)}, u32[]{:S(2)}, u32[]{:S(2)}) collective-permute-start(bf16[128,256]{1,0:T(8,128)(2,1)S(1)} %add_convert_fusion), channel_id=1, source_target_pairs={{1,2},{2,1},{3,4},{4,3},{5,6},{6,5},{7,8},{8,7},{9,10},{10,9},{11,... | collective-permute-start | bytes 196616 | tf_op jit(solution)/shard_map/ppermute | solution.py:220
  24.1 6.2 %collective-permute-start.1 = (bf16[128,256]{1,0:T(8,128)(2,1)S(1)}, bf16[128,256]{1,0:T(8,128)(2,1)S(1)}, u32[]{:S(2)}, u32[]{:S(2)}) collective-permute-start(bf16[128,256]{1,0:T(8,128)(2,1)S(1)} %get-tuple-element.21), channel_id=1, source_target_pairs={{0,128},{128,0},{256,384},{384,256},{1,129},{129,1},{257,385},{385... | collective-permute-start | bytes 196616 | tf_op jit(solution)/shard_map/ppermute | solution.py:222
  26.0 6.2 %collective-permute-start.2 = (bf16[128,256]{1,0:T(8,128)(2,1)S(1)}, bf16[128,256]{1,0:T(8,128)(2,1)S(1)}, u32[]{:S(2)}, u32[]{:S(2)}) collective-permute-start(bf16[128,256]{1,0:T(8,128)(2,1)S(1)} %get-tuple-element.22), channel_id=1, source_target_pairs={{128,256},{256,128},{129,257},{257,129},{130,258},{258,130},{131,2... | collective-permute-start | bytes 196616 | tf_op jit(solution)/shard_map/ppermute | solution.py:223

commit v3 on v2

v3 whole, which is shorter than its diff:
```python
import jax
import jax.numpy as jnp
from jax import lax
from jax.experimental import pallas as pl
from jax.experimental.pallas import tpu as pltpu
from jax.sharding import PartitionSpec as P


NS = 256
NTIME = 256
PX = 16
PY = 8
DSTEP = 8
TR = 128
NH = 8
NC = 14
COLS = PX * PY
NJ = 4 * TR
NQ = (2 * PX - 1 + 2 * PY - 1) // DSTEP + 1
LEVEL = 129.0
BF = jnp.bfloat16
F32 = jnp.float32


NB = 4
NREACH = NH + NQ - 1
PICK_UNROLL = 4
GROUPS = (0, 4, 7, 10, NREACH)
ROW_X, ROW_Y, ROW_SCALE, ROW_LIVE = 0, 1, 2, 2 + NQ


def row_of(parts):
    return jnp.concatenate(parts, axis=1)


def blocks(piece):
    return row_of([piece(i, k) for i in range(2) for k in range(2)])


def partners():
    dx = 1 - 2 * (lax.axis_index("gx") % 2)
    dy = 1 - 2 * (lax.axis_index("gy") % 2)
    return dx, dy


def inline_distance(dx, mx):
    px = (lax.broadcasted_iota(jnp.int32, (PX, NJ), 0) + PX * dx).astype(F32)
    ax = (2.0 * jnp.abs(px - mx) - (DSTEP - 1)) * (0.5 / DSTEP)
    ax = jnp.broadcast_to(ax[:, None, :], (PX, PY, NJ)).reshape(COLS, NJ)
    return ax.astype(BF).reshape(COLS // 16, 16, NJ)


def crossline_distance(dy, my):
    py = (lax.broadcasted_iota(jnp.int32, (16, NJ), 0) % PY + PY * dy).astype(F32)
    return (jnp.abs(py - my) * (1.0 / DSTEP)).astype(BF)[None]


def class_scales(h, w, cw_ref):
    scales = []
    for q in range(NQ):
        cw = jnp.full(h.shape, cw_ref[q], F32)
        for k in range(1, NH):
            cw = jnp.where(h == k, cw_ref[k + q], cw)
        scales.append((w * cw).astype(BF).astype(F32))
    return scales


def live_row(ap_ref, dx, dy):
    entry = (dx + 1) * 3 + dy + 1
    return blocks(lambda i, k: jnp.full((1, TR), ap_ref[i, k, entry].astype(F32), F32))


def fill_amplitudes(a_ref, at, ax, ay, scales, live, n_q):
    level = (ax + ay) + jnp.asarray(LEVEL, BF)
    for q in range(n_q):
        scale = jnp.broadcast_to(scales[q] * live, (16, NJ)).astype(BF)[None]
        a = jnp.where(level == jnp.asarray(LEVEL + q, BF), scale, jnp.zeros((), BF))
        a_ref[at : at + COLS, q * NJ : (q + 1) * NJ] = a.reshape(COLS, NJ)


def outer_kernel(
    traces_hbm, geom_hbm, w_hbm, tt_hbm, ap_hbm, cw_hbm,
    first_ref, corner_ref, tq_ref, table_ref,
    traces_ref, geom_ref, w_ref, tt_ref, ap_ref, cw_ref, sems, class_ref, interp_ref, t_ref, a_ref,
):
    pairs = (
        (tt_hbm, tt_ref), (traces_hbm, traces_ref), (geom_hbm, geom_ref),
        (w_hbm, w_ref), (cw_hbm, cw_ref), (ap_hbm, ap_ref),
    )
    copies = [pltpu.make_async_copy(a, b, sems.at[n]) for n, (a, b) in enumerate(pairs)]
    for copy in copies:
        copy.start()
    dx, dy = partners()
    for copy in copies:
        copy.wait()
    h = blocks(lambda i, k: geom_ref[i, 2, k : k + 1, :])
    mx = blocks(lambda i, k: geom_ref[i, 0, k : k + 1, :] & (PX - 1)).astype(F32)
    my = blocks(lambda i, k: geom_ref[i, 1, k : k + 1, :] & (PY - 1)).astype(F32)
    w = blocks(lambda i, k: w_ref[i, k : k + 1, :]).astype(F32)
    scales = class_scales(h, w, cw_ref)
    hf = h.astype(F32)

    for b in range(NB):
        column = jnp.broadcast_to(hf[:, b * TR : (b + 1) * TR], (TR, TR)).T
        class_ref[b * TR : (b + 1) * TR, :] = column.astype(BF)
    ays = [crossline_distance(t, my) for t in (-dy, 0, dy)]
    axs = [inline_distance(t, mx) for t in (dx, -dx)]
    sample = lax.broadcasted_iota(jnp.int32, (NS, NTIME), 0).astype(F32).astype(BF).reshape(NS // 16, 16, NTIME)
    for n, (tx, ty, n_q) in enumerate(outer_tiles(dx, dy)):
        classes = range(GROUPS[n], GROUPS[n + 1])
        for c in classes:
            quarter = tt_ref[c : c + 1, :]
            whole = jnp.minimum(quarter >> 2, NS).astype(F32)
            part = (quarter & 3).astype(F32) * 0.25
            whole = jnp.broadcast_to(whole, (16, NTIME)).astype(BF)[None]
            part = jnp.broadcast_to(part, (16, NTIME)).astype(BF)[None]
            away = jnp.abs((sample - whole) - part)
            interp = jnp.maximum(jnp.asarray(1.0, BF) - away, jnp.asarray(0.0, BF))
            interp_ref[:, c * NTIME : (c + 1) * NTIME] = interp.reshape(NS, NTIME)
        lanes = slice(classes[0] * NTIME, (classes[-1] + 1) * NTIME)
        t_ref[:, lanes] = jnp.dot(traces_ref[...], interp_ref[:, lanes], preferred_element_type=F32).astype(BF)
        fill_amplitudes(a_ref, n * COLS, axs[n // 3], ays[n % 3], scales, live_row(ap_ref, tx, ty), n_q)

    def pick(n, carry):
        rows = pl.ds(pl.multiple_of(n * 16, 16), 16)
        k = class_ref[rows, :]
        bit4 = k >= jnp.asarray(4.0, BF)
        k = jnp.where(bit4, k - jnp.asarray(4.0, BF), k)
        bit2 = k >= jnp.asarray(2.0, BF)
        k = jnp.where(bit2, k - jnp.asarray(2.0, BF), k)
        bit1 = k >= jnp.asarray(1.0, BF)
        for lane in (0, 128):
            t = [t_ref[rows, c * NTIME + lane : c * NTIME + lane + 128] for c in range(NREACH)]
            for bit, shift in ((bit1, 1), (bit2, 2), (bit4, 4)):
                t = [jnp.where(bit, t[c + shift], t[c]) for c in range(len(t) - shift)]
            for q in range(NQ):
                tq_ref[pl.ds(pl.multiple_of(q * NJ + n * 16, 16), 16), lane : lane + 128] = t[q]
        return carry

    lax.fori_loop(0, NJ // 16, pick, 0, unroll=PICK_UNROLL)
    for n in range(2):
        rows = slice(2 * n * COLS, 2 * (n + 1) * COLS)
        out = jnp.dot(a_ref[rows, :], tq_ref[...], preferred_element_type=F32).astype(BF)
        if n == 0:
            first_ref[: 2 * COLS] = out
        else:
            first_ref[2 * COLS :] = out[:COLS]
            corner_ref[...] = out[COLS:]
    table_ref[ROW_X : ROW_X + 1, :] = mx
    table_ref[ROW_Y : ROW_Y + 1, :] = my
    for q in range(NQ):
        table_ref[ROW_SCALE + q : ROW_SCALE + q + 1, :] = scales[q]
    for n, (tx, ty, _) in enumerate(inner_tiles(dx, dy)):
        table_ref[ROW_LIVE + n : ROW_LIVE + n + 1, :] = live_row(ap_ref, tx, ty)


def outer_tiles(dx, dy):
    return ((dx, -dy, 6), (dx, 0, 6), (dx, dy, 6), (-dx, -dy, 6))


def inner_tiles(dx, dy):
    return ((-dx, dy, 6), (-dx, 0, 6), (0, -dy, 4), (0, dy, 4), (0, 0, 3))


def inner_kernel(tq_ref, table_ref, slow_ref, second_ref, own_ref, a_ref):
    dx, dy = partners()
    tiles = inner_tiles(dx, dy)
    mx, my = table_ref[ROW_X : ROW_X + 1, :], table_ref[ROW_Y : ROW_Y + 1, :]
    scales = [table_ref[ROW_SCALE + q : ROW_SCALE + q + 1, :] for q in range(NQ)]
    axs = [inline_distance(t, mx) for t in (-dx, 0)]
    ays = [crossline_distance(t, my) for t in (-dy, dy, 0)]
    which = ((0, 1), (0, 2), (1, 0), (1, 1), (1, 2))
    for n, (_, _, n_q) in enumerate(tiles):
        live = table_ref[ROW_LIVE + n : ROW_LIVE + n + 1, :]
        fill_amplitudes(a_ref, n * COLS, axs[which[n][0]], ays[which[n][1]], scales, live, n_q)

    def part(first, last, n_q):
        a = a_ref[first * COLS : last * COLS, : n_q * NJ]
        return jnp.dot(a, tq_ref[: n_q * NJ, :], preferred_element_type=F32)

    x = part(0, 2, 6).astype(BF)
    second_ref[COLS:] = x[:COLS]
    second_ref[:COLS] = x[COLS:]
    x = part(2, 4, 4)
    slow_ref[...] = x[:COLS]
    own_ref[COLS:] = x[COLS:]
    own_ref[:COLS] = part(4, 5, 3)


def swaps(axis, odd):
    n = lax.axis_size(axis)
    lower = range(1 if odd else 0, n - 1, 2)
    return [p for i in lower for p in ((i, i + 1), (i + 1, i))]


HBM = pl.BlockSpec(memory_space=pltpu.HBM)
VMEM = pl.BlockSpec(memory_space=pltpu.VMEM)
INNER_COST = pl.CostEstimate(flops=2 * 23 * COLS * NJ * NTIME, bytes_accessed=1 << 21, transcendentals=0)
PARAMS = pltpu.CompilerParams(vmem_limit_bytes=24 << 20)


def in_hbm(x):
    return pltpu.with_memory_space_constraint(x, pltpu.HBM)


def per_device(traces, aperture, geometry, trace_weight, class_weight, traveltime):
    geom = jnp.transpose(geometry, (0, 2, 1, 3))
    first, corner, tq, table = pl.pallas_call(
        outer_kernel,
        out_shape=(
            jax.ShapeDtypeStruct((3 * COLS, NTIME), BF),
            jax.ShapeDtypeStruct((COLS, NTIME), BF),
            jax.ShapeDtypeStruct((NQ * NJ, NTIME), BF),
            jax.ShapeDtypeStruct((16, NJ), F32),
        ),
        in_specs=[HBM] * 6,
        out_specs=(VMEM,) * 4,
        scratch_shapes=[
            pltpu.VMEM((NJ, NS), BF),
            pltpu.VMEM((2, 3, 2, TR), jnp.int32),
            pltpu.VMEM((2, 2, TR), BF),
            pltpu.VMEM((NC, NTIME), jnp.int32),
            pltpu.SMEM((2, 2, 9), jnp.int32),
            pltpu.SMEM((NC,), F32),
            pltpu.SemaphoreType.DMA((6,)),
            pltpu.VMEM((NJ, TR), BF),
            pltpu.VMEM((NS, NREACH * NTIME), BF),
            pltpu.VMEM((NJ, NREACH * NTIME), BF),
            pltpu.VMEM((4 * COLS, NQ * NJ), BF),
        ],
        compiler_params=PARAMS,
        name="outer",
    )(*(in_hbm(x) for x in (traces.reshape(NJ, NS), geom, trace_weight, traveltime, aperture, class_weight)))
    from_first = lax.ppermute(first, "gx", swaps("gx", False))
    from_corner = lax.ppermute(corner, "gx", swaps("gx", True))
    slow, second, own = pl.pallas_call(
        inner_kernel,
        out_shape=(
            jax.ShapeDtypeStruct((COLS, NTIME), F32),
            jax.ShapeDtypeStruct((2 * COLS, NTIME), BF),
            jax.ShapeDtypeStruct((2 * COLS, NTIME), F32),
        ),
        in_specs=[VMEM] * 2,
        out_specs=(VMEM,) * 3,
        scratch_shapes=[pltpu.VMEM((5 * COLS, NQ * NJ), BF)],
        compiler_params=PARAMS,
        cost_estimate=INNER_COST,
        name="inner",
    )(tq, table)
    from_second = lax.ppermute(second, "gx", swaps("gx", True))
    slow = slow + from_first[:COLS].astype(F32) + from_corner.astype(F32)
    far = lax.ppermute(slow.astype(BF), "gy", swaps("gy", True))
    own = own + from_first[COLS:].astype(F32) + from_second.astype(F32)
    near = lax.ppermute(own[COLS:], "gy", swaps("gy", False))
    image = own[:COLS] + near + far.astype(F32)
    return image.reshape(PX, PY, NTIME)


def solution(mesh):
    return jax.shard_map(
        per_device,
        mesh=mesh,
        in_specs=(
            P("gx", "gy", None, None),
            P("gx", "gy", None),
            P("gx", "gy", None, None),
            P("gx", "gy", None),
            P(),
            P(),
        ),
        out_specs=P("gx", "gy", None),
        check_vma=False,
    )
```

time: 33.2 us -> 33.6 us (1.012)
  the two profiles are of different devices: /device:TPU:328 before, /device:TPU:239 now
where the time goes in v3:
time: 33.6 us; the launch traced here: 33.3 us
  starting transfers between devices  18.8 us (56%)
  waiting for transfers between devices  8.34 us (25%)
  Pallas kernels  5.36 us (16%)
  other arithmetic  0.74 us (2%)
    ppermute x1, waiting for transfers between devices, per_device(): far = lax.ppermute(slow.astype(BF), 'gy', swaps('gy', True))  7.91 us
    ppermute x1, starting transfers between devices, per_device(): far = lax.ppermute(slow.astype(BF), 'gy', swaps('gy', True))  5.79 us
    ppermute x1, starting transfers between devices, per_device(): near = lax.ppermute(own[COLS:], 'gy', swaps('gy', False))  4.72 us
    pallas_call x1, Pallas kernels, per_device(): pl.pallas_call(outer_kernel, out_shape=(jax.ShapeDtypeStruct((3 * COLS, N...  4.38 us
    ppermute x1, starting transfers between devices, per_device(): from_corner = lax.ppermute(corner, 'gx', swaps('gx', True))  3.36 us
    ppermute x1, starting transfers between devices, per_device(): from_first = lax.ppermute(first, 'gx', swaps('gx', False))  2.98 us
    ppermute x1, starting transfers between devices, per_device(): from_second = lax.ppermute(second, 'gx', swaps('gx', True))  1.92 us
    pallas_call x1, Pallas kernels, per_device(): pl.pallas_call(inner_kernel, out_shape=(jax.ShapeDtypeStruct((COLS, NTIME...  0.98 us
  transfers between devices with their start and end apart: 5, of which 2 were waited for; matrix products, arithmetic and copies ran while one was open for 0% of the time, Pallas kernels for 3%

profile of v3, /device:TPU:239, one launch (start us, length us, event | category | flops | bytes accessed | tf_op | source)
XLA Modules:
  0.0 33.3 jit_solution(12414453528879410392)
XLA Ops:
  0.0 4.4 %outer.1 = (bf16[384,256]{1,0:T(8,128)(2,1)S(1)}, bf16[128,256]{1,0:T(8,128)(2,1)S(1)}, bf16[3072,256]{1,0:T(8,128)(2,1)S(1)}, f32[16,512]{1,0:T(8,128)S(1)}) custom-call(bf16[512,256]{1,0:T(8,128)(2,1)} %bitcast.4, s32[2,3,2,128]{3,2,1,0:T(2,128)} %bitcast.5, bf16[2,2,128]{2,1,0:T(2,128)(2,1)} %w_hbm.1, s32[14,256]{1,0:T(8,128)} %tt_hbm.1, ...), custom_call_target="tpu_custom_call" | custom-call | tf_op jit(solution)/shard_map/outer/pallas_call | solution.py:208
  4.4 3.0 %collective-permute-start = (bf16[384,256]{1,0:T(8,128)(2,1)S(1)}, bf16[384,256]{1,0:T(8,128)(2,1)S(1)}, u32[]{:S(2)}, u32[]{:S(2)}) collective-permute-start(bf16[384,256]{1,0:T(8,128)(2,1)S(1)} %get-tuple-element.15), channel_id=1, source_target_pairs={{0,128},{128,0},{256,384},{384,256},{1,129},{129,1},{257,385},{385... | collective-permute-start | bytes 589832 | tf_op jit(solution)/shard_map/ppermute | solution.py:234
  7.4 1.0 %inner.1 = (f32[128,256]{1,0:T(8,128)S(1)}, bf16[256,256]{1,0:T(8,128)(2,1)S(1)}, f32[256,256]{1,0:T(8,128)S(1)}) custom-call(bf16[3072,256]{1,0:T(8,128)(2,1)S(1)} %get-tuple-element.12.tq_ref, f32[16,512]{1,0:T(8,128)S(1)} %get-tuple-element.13.table_ref), custom_call_target="tpu_custom_call" | custom-call | flops 771751936 | bytes 2097152 | tf_op jit(solution)/shard_map/inner/pallas_call | solution.py:236
  8.4 1.9 %collective-permute-start.1 = (bf16[256,256]{1,0:T(8,128)(2,1)S(1)}, bf16[256,256]{1,0:T(8,128)(2,1)S(1)}, u32[]{:S(2)}, u32[]{:S(2)}) collective-permute-start(bf16[256,256]{1,0:T(8,128)(2,1)S(1)} %get-tuple-element.16), channel_id=1, source_target_pairs={{128,256},{256,128},{129,257},{257,129},{130,258},{258,130},{131,2... | collective-permute-start | bytes 393224 | tf_op jit(solution)/shard_map/ppermute | solution.py:250
  10.3 3.4 %collective-permute-start.3 = (bf16[128,256]{1,0:T(8,128)(2,1)S(1)}, bf16[128,256]{1,0:T(8,128)(2,1)S(1)}, u32[]{:S(2)}, u32[]{:S(2)}) collective-permute-start(bf16[128,256]{1,0:T(8,128)(2,1)S(1)} %get-tuple-element.18), channel_id=1, source_target_pairs={{128,256},{256,128},{129,257},{257,129},{130,258},{258,130},{131,2... | collective-permute-start | bytes 196616 | tf_op jit(solution)/shard_map/ppermute | solution.py:235
  13.7 0.4 %collective-permute-done.1 = bf16[256,256]{1,0:T(8,128)(2,1)S(1)} collective-permute-done((bf16[256,256]{1,0:T(8,128)(2,1)S(1)}, bf16[256,256]{1,0:T(8,128)(2,1)S(1)}, u32[]{:S(2)}, u32[]{:S(2)}) %collective-permute-start.1) | collective-permute-done | bytes 131104 | tf_op jit(solution)/shard_map/ppermute | solution.py:250
  14.1 0.0 collective-permute-done
  14.1 4.7 %collective-permute-start.2 = (f32[128,256]{1,0:T(8,128)S(1)}, f32[128,256]{1,0:T(8,128)S(1)}, u32[]{:S(2)}, u32[]{:S(2)}) collective-permute-start(f32[128,256]{1,0:T(8,128)S(1)} %slice.18), channel_id=1, source_target_pairs={{0,1},{1,0},{2,3},{3,2},{4,5},{5,4},{6,7},{7,6},{8,9},{9,8},{10,11... | collective-permute-start | bytes 393224 | tf_op jit(solution)/shard_map/ppermute | solution.py:254
  18.9 0.0 collective-permute-done.3
  18.9 5.8 %collective-permute-start.4 = (bf16[128,256]{1,0:T(8,128)(2,1)S(1)}, bf16[128,256]{1,0:T(8,128)(2,1)S(1)}, u32[]{:S(2)}, u32[]{:S(2)}) collective-permute-start(bf16[128,256]{1,0:T(8,128)(2,1)S(1)} %add_convert_fusion), channel_id=1, source_target_pairs={{1,2},{2,1},{3,4},{4,3},{5,6},{6,5},{7,8},{8,7},{9,10},{10,9},{11,... | collective-permute-start | bytes 196616 | tf_op jit(solution)/shard_map/ppermute | solution.py:252
  24.7 7.9 %collective-permute-done.4 = bf16[128,256]{1,0:T(8,128)(2,1)S(1)} collective-permute-done((bf16[128,256]{1,0:T(8,128)(2,1)S(1)}, bf16[128,256]{1,0:T(8,128)(2,1)S(1)}, u32[]{:S(2)}, u32[]{:S(2)}) %collective-permute-start.4) | collective-permute-done | bytes 65568 | tf_op jit(solution)/shard_map/ppermute | solution.py:252
  32.6 0.0 collective-permute-done.2
  32.6 0.7 %fusion.1 = f32[16,8,256]{2,1,0:T(8,128)} fusion(f32[128,256]{1,0:T(8,128)S(1)} %collective-permute-done.2, f32[256,256]{1,0:T(8,128)S(1)} %convert_add_fusion, bf16[128,256]{1,0:T(8,128)(2,1)S(1)} %collective-permute-done.4), kind=kLoop, calls=%fused_computation.3 | loop fusion | flops 98304 | bytes 458752 | tf_op jit(solution)/shard_map/reshape | solution.py:256
  (3 shorter events, 0.1 us)
Async XLA Ops:
  4.4 9.7 %collective-permute-start = (bf16[384,256]{1,0:T(8,128)(2,1)S(1)}, bf16[384,256]{1,0:T(8,128)(2,1)S(1)}, u32[]{:S(2)}, u32[]{:S(2)}) collective-permute-start(bf16[384,256]{1,0:T(8,128)(2,1)S(1)} %get-tuple-element.15), channel_id=1, source_target_pairs={{0,128},{128,0},{256,384},{384,256},{1,129},{129,1},{257,385},{385... | collective-permute-start | bytes 589832 | tf_op jit(solution)/shard_map/ppermute | solution.py:234
  8.4 5.7 %collective-permute-start.1 = (bf16[256,256]{1,0:T(8,128)(2,1)S(1)}, bf16[256,256]{1,0:T(8,128)(2,1)S(1)}, u32[]{:S(2)}, u32[]{:S(2)}) collective-permute-start(bf16[256,256]{1,0:T(8,128)(2,1)S(1)} %get-tuple-element.16), channel_id=1, source_target_pairs={{128,256},{256,128},{129,257},{257,129},{130,258},{258,130},{131,2... | collective-permute-start | bytes 393224 | tf_op jit(solution)/shard_map/ppermute | solution.py:250
  10.3 8.6 %collective-permute-start.3 = (bf16[128,256]{1,0:T(8,128)(2,1)S(1)}, bf16[128,256]{1,0:T(8,128)(2,1)S(1)}, u32[]{:S(2)}, u32[]{:S(2)}) collective-permute-start(bf16[128,256]{1,0:T(8,128)(2,1)S(1)} %get-tuple-element.18), channel_id=1, source_target_pairs={{128,256},{256,128},{129,257},{257,129},{130,258},{258,130},{131,2... | collective-permute-start | bytes 196616 | tf_op jit(solution)/shard_map/ppermute | solution.py:235
  14.1 18.5 %collective-permute-start.2 = (f32[128,256]{1,0:T(8,128)S(1)}, f32[128,256]{1,0:T(8,128)S(1)}, u32[]{:S(2)}, u32[]{:S(2)}) collective-permute-start(f32[128,256]{1,0:T(8,128)S(1)} %slice.18), channel_id=1, source_target_pairs={{0,1},{1,0},{2,3},{3,2},{4,5},{5,4},{6,7},{7,6},{8,9},{9,8},{10,11... | collective-permute-start | bytes 393224 | tf_op jit(solution)/shard_map/ppermute | solution.py:254
  18.9 13.7 %collective-permute-start.4 = (bf16[128,256]{1,0:T(8,128)(2,1)S(1)}, bf16[128,256]{1,0:T(8,128)(2,1)S(1)}, u32[]{:S(2)}, u32[]{:S(2)}) collective-permute-start(bf16[128,256]{1,0:T(8,128)(2,1)S(1)} %add_convert_fusion), channel_id=1, source_target_pairs={{1,2},{2,1},{3,4},{4,3},{5,6},{6,5},{7,8},{8,7},{9,10},{10,9},{11,... | collective-permute-start | bytes 196616 | tf_op jit(solution)/shard_map/ppermute | solution.py:252

commit v4 on v3

v4 whole, which is shorter than its diff:
```python
import jax
import jax.numpy as jnp
from jax import lax
from jax.experimental import pallas as pl
from jax.experimental.pallas import tpu as pltpu
from jax.sharding import PartitionSpec as P


NS = 256
NTIME = 256
PX = 16
PY = 8
DSTEP = 8
TR = 128
NH = 8
NC = 14
COLS = PX * PY
NJ = 4 * TR
NQ = (2 * PX - 1 + 2 * PY - 1) // DSTEP + 1
LEVEL = 129.0
BF = jnp.bfloat16
F32 = jnp.float32


NB = 4
NREACH = NH + NQ - 1
PICK_UNROLL = 4
ROW_X, ROW_Y, ROW_SCALE, ROW_LIVE = 0, 1, 2, 2 + NQ


def row_of(parts):
    return jnp.concatenate(parts, axis=1)


def blocks(piece):
    return row_of([piece(i, k) for i in range(2) for k in range(2)])


def down(piece, rows):
    return jnp.concatenate([piece] * (rows // 16), axis=0)


def partners():
    dx = 1 - 2 * (lax.axis_index("gx") % 2)
    dy = 1 - 2 * (lax.axis_index("gy") % 2)
    return dx, dy


def inline_distance(dx, mx):
    px = (lax.broadcasted_iota(jnp.int32, (PX, NJ), 0) + PX * dx).astype(F32)
    ax = (2.0 * jnp.abs(px - mx) - (DSTEP - 1)) * (0.5 / DSTEP)
    ax = jnp.broadcast_to(ax[:, None, :], (PX, PY, NJ)).reshape(COLS, NJ)
    return ax.astype(BF)


def crossline_distance(dy, my):
    py = (lax.broadcasted_iota(jnp.int32, (16, NJ), 0) % PY + PY * dy).astype(F32)
    return down((jnp.abs(py - my) * (1.0 / DSTEP)).astype(BF), COLS)


def class_scales(h, w, cw_ref):
    scales = []
    for q in range(NQ):
        cw = jnp.full(h.shape, cw_ref[q], F32)
        for k in range(1, NH):
            cw = jnp.where(h == k, cw_ref[k + q], cw)
        scales.append((w * cw).astype(BF).astype(F32))
    return scales


def live_row(ap_ref, dx, dy):
    entry = (dx + 1) * 3 + dy + 1
    return blocks(lambda i, k: jnp.full((1, TR), ap_ref[i, k, entry].astype(F32), F32))


def amplitude(level, scales, lives, q):
    scale = [down(jnp.broadcast_to(scales[q] * live, (16, NJ)).astype(BF), COLS) for live in lives]
    return jnp.where(level == jnp.asarray(LEVEL + q, BF), jnp.concatenate(scale, axis=0), jnp.zeros((), BF))


def stacked(tq_ref, level, scales, lives, n_q):
    out = jnp.zeros((len(lives) * COLS, NTIME), F32)
    for q in range(n_q):
        a = amplitude(level, scales, lives, q)
        out = out + jnp.dot(a, tq_ref[q * NJ : (q + 1) * NJ, :], preferred_element_type=F32)
    return out


def outer_kernel(
    traces_hbm, geom_hbm, w_hbm, tt_hbm, ap_hbm, cw_hbm,
    first_ref, corner_ref, tq_ref, table_ref,
    traces_ref, geom_ref, w_ref, tt_ref, ap_ref, cw_ref, sems, class_ref, t_ref, level_ref,
):
    pairs = (
        (traces_hbm, traces_ref), (geom_hbm, geom_ref), (tt_hbm, tt_ref),
        (w_hbm, w_ref), (cw_hbm, cw_ref), (ap_hbm, ap_ref),
    )
    copies = [pltpu.make_async_copy(a, b, sems.at[n]) for n, (a, b) in enumerate(pairs)]
    for copy in copies:
        copy.start()
    dx, dy = partners()
    for copy in copies[1:]:
        copy.wait()
    h = blocks(lambda i, k: geom_ref[i, 2, k : k + 1, :])
    mx = blocks(lambda i, k: geom_ref[i, 0, k : k + 1, :] & (PX - 1)).astype(F32)
    my = blocks(lambda i, k: geom_ref[i, 1, k : k + 1, :] & (PY - 1)).astype(F32)
    w = blocks(lambda i, k: w_ref[i, k : k + 1, :]).astype(F32)
    table_ref[ROW_X : ROW_X + 1, :] = mx
    table_ref[ROW_Y : ROW_Y + 1, :] = my
    for q, scale in enumerate(class_scales(h, w, cw_ref)):
        table_ref[ROW_SCALE + q : ROW_SCALE + q + 1, :] = scale
    tiles = outer_tiles(dx, dy)
    for n, (tx, ty) in enumerate(inner_tiles(dx, dy) + tiles):
        table_ref[ROW_LIVE + n : ROW_LIVE + n + 1, :] = live_row(ap_ref, tx, ty)
    hf = h.astype(F32)
    for b in range(NB):
        column = jnp.broadcast_to(hf[:, b * TR : (b + 1) * TR], (TR, TR)).T
        class_ref[b * TR : (b + 1) * TR, :] = jnp.concatenate([column, column], axis=1).astype(BF)
    ays = [crossline_distance(t, my) for t in (-dy, 0, dy)]
    axs = [inline_distance(t, mx) for t in (dx, -dx)]
    which = ((0, 0), (0, 1), (0, 2), (1, 0))
    for n in range(len(tiles)):
        x, y = which[n]
        level_ref[n * COLS : (n + 1) * COLS, :] = axs[x] + ays[y] + jnp.asarray(LEVEL, BF)
    copies[0].wait()
    sample = lax.broadcasted_iota(jnp.int32, (NS, NTIME), 0).astype(F32).astype(BF)
    for c in range(NREACH):
        quarter = tt_ref[c : c + 1, :]
        whole = jnp.minimum(quarter >> 2, NS).astype(F32)
        part = (quarter & 3).astype(F32) * 0.25
        whole = down(jnp.broadcast_to(whole, (16, NTIME)).astype(BF), NS)
        part = down(jnp.broadcast_to(part, (16, NTIME)).astype(BF), NS)
        away = jnp.abs((sample - whole) - part)
        interp = jnp.maximum(jnp.asarray(1.0, BF) - away, jnp.asarray(0.0, BF))
        lanes = slice(c * NTIME, (c + 1) * NTIME)
        for n in range(2):
            rows = slice(n * (NJ // 2), (n + 1) * (NJ // 2))
            t_ref[rows, lanes] = jnp.dot(traces_ref[rows, :], interp, preferred_element_type=F32).astype(BF)

    def pick(n, carry):
        rows = pl.ds(pl.multiple_of(n * 16, 16), 16)
        k = class_ref[rows, :]
        bit4 = k >= jnp.asarray(4.0, BF)
        k = jnp.where(bit4, k - jnp.asarray(4.0, BF), k)
        bit2 = k >= jnp.asarray(2.0, BF)
        k = jnp.where(bit2, k - jnp.asarray(2.0, BF), k)
        bit1 = k >= jnp.asarray(1.0, BF)
        t = [t_ref[rows, c * NTIME : (c + 1) * NTIME] for c in range(NREACH)]
        for bit, shift in ((bit1, 1), (bit2, 2), (bit4, 4)):
            t = [jnp.where(bit, t[c + shift], t[c]) for c in range(len(t) - shift)]
        for q in range(NQ):
            tq_ref[pl.ds(pl.multiple_of(q * NJ + n * 16, 16), 16), :] = t[q]
        return carry

    lax.fori_loop(0, NJ // 16, pick, 0, unroll=PICK_UNROLL)
    _, _, scales, lives = table_rows(table_ref)
    lives = lives[len(inner_tiles(dx, dy)) :]
    sums = []
    for low, high in ((0, 2), (2, 4)):
        level = level_ref[low * COLS : high * COLS, :]
        sums.append(stacked(tq_ref, level, scales, lives[low:high], NQ).astype(BF))
    first_ref[: 2 * COLS] = sums[0]
    first_ref[2 * COLS :] = sums[1][:COLS]
    corner_ref[...] = sums[1][COLS:]


def outer_tiles(dx, dy):
    return ((dx, -dy), (dx, 0), (dx, dy), (-dx, -dy))


def inner_tiles(dx, dy):
    return ((-dx, 0), (-dx, dy), (0, 0), (0, dy), (0, -dy))


def table_rows(table_ref):
    mx, my = table_ref[ROW_X : ROW_X + 1, :], table_ref[ROW_Y : ROW_Y + 1, :]
    scales = [table_ref[ROW_SCALE + q : ROW_SCALE + q + 1, :] for q in range(NQ)]
    return mx, my, scales, [table_ref[ROW_LIVE + n : ROW_LIVE + n + 1, :] for n in range(9)]


def side_kernel(tq_ref, table_ref, second_ref, slow_ref):
    dx, dy = partners()
    mx, my, scales, lives = table_rows(table_ref)
    ax = inline_distance(-dx, mx)
    levels = [ax + crossline_distance(ty, my) + jnp.asarray(LEVEL, BF) for ty in (0, dy)]
    for n, level in enumerate(levels):
        out = stacked(tq_ref, level, scales, lives[n : n + 1], NQ)
        second_ref[n * COLS : (n + 1) * COLS, :] = out.astype(BF)
    level = inline_distance(0, mx) + crossline_distance(-dy, my) + jnp.asarray(LEVEL, BF)
    slow_ref[...] = stacked(tq_ref, level, scales, lives[4:5], 4)


def own_kernel(tq_ref, table_ref, own_ref):
    _, dy = partners()
    mx, my, scales, lives = table_rows(table_ref)
    ax = inline_distance(0, mx)
    for n, ty in enumerate((0, dy)):
        level = ax + crossline_distance(ty, my) + jnp.asarray(LEVEL, BF)
        own_ref[n * COLS : (n + 1) * COLS, :] = stacked(tq_ref, level, scales, lives[2 + n : 3 + n], 3 + n)


def swaps(axis, odd):
    n = lax.axis_size(axis)
    lower = range(1 if odd else 0, n - 1, 2)
    return [p for i in lower for p in ((i, i + 1), (i + 1, i))]


HBM = pl.BlockSpec(memory_space=pltpu.HBM)
VMEM = pl.BlockSpec(memory_space=pltpu.VMEM)
LATER_COST = pl.CostEstimate(flops=2 * 7 * COLS * NJ * NTIME, bytes_accessed=1 << 21, transcendentals=0)
PARAMS = pltpu.CompilerParams(vmem_limit_bytes=24 << 20)


def in_hbm(x):
    return pltpu.with_memory_space_constraint(x, pltpu.HBM)


def later_tiles(kernel, dtypes, tq, table):
    return pl.pallas_call(
        kernel,
        out_shape=tuple(jax.ShapeDtypeStruct(((2 - n) * COLS, NTIME), t) for n, t in enumerate(dtypes)),
        in_specs=[VMEM] * 2,
        out_specs=(VMEM,) * len(dtypes),
        compiler_params=PARAMS,
        cost_estimate=LATER_COST,
    )(tq, table)


def per_device(traces, aperture, geometry, trace_weight, class_weight, traveltime):
    geom = jnp.transpose(geometry, (0, 2, 1, 3))
    first, corner, tq, table = pl.pallas_call(
        outer_kernel,
        out_shape=(
            jax.ShapeDtypeStruct((3 * COLS, NTIME), BF),
            jax.ShapeDtypeStruct((COLS, NTIME), BF),
            jax.ShapeDtypeStruct((NQ * NJ, NTIME), BF),
            jax.ShapeDtypeStruct((24, NJ), F32),
        ),
        in_specs=[HBM] * 6,
        out_specs=(VMEM,) * 4,
        scratch_shapes=[
            pltpu.VMEM((NJ, NS), BF),
            pltpu.VMEM((2, 3, 2, TR), jnp.int32),
            pltpu.VMEM((2, 2, TR), BF),
            pltpu.VMEM((NC, NTIME), jnp.int32),
            pltpu.SMEM((2, 2, 9), jnp.int32),
            pltpu.SMEM((NC,), F32),
            pltpu.SemaphoreType.DMA((6,)),
            pltpu.VMEM((NJ, NTIME), BF),
            pltpu.VMEM((NJ, NREACH * NTIME), BF),
            pltpu.VMEM((4 * COLS, NJ), BF),
        ],
        compiler_params=PARAMS,
        name="outer",
    )(*(in_hbm(x) for x in (traces.reshape(NJ, NS), geom, trace_weight, traveltime, aperture, class_weight)))
    from_first = lax.ppermute(first, "gx", swaps("gx", False))
    from_corner = lax.ppermute(corner, "gx", swaps("gx", True))
    second, slow = later_tiles(side_kernel, (BF, F32), tq, table)
    from_second = lax.ppermute(second, "gx", swaps("gx", True))
    slow = slow + from_first[:COLS].astype(F32) + from_corner.astype(F32)
    far = lax.ppermute(slow.astype(BF), "gy", swaps("gy", True))
    (own,) = later_tiles(own_kernel, (F32,), tq, table)
    own = own + from_first[COLS:].astype(F32) + from_second.astype(F32)
    near = lax.ppermute(own[COLS:], "gy", swaps("gy", False))
    image = own[:COLS] + near + far.astype(F32)
    return image.reshape(PX, PY, NTIME)


def solution(mesh):
    return jax.shard_map(
        per_device,
        mesh=mesh,
        in_specs=(
            P("gx", "gy", None, None),
            P("gx", "gy", None),
            P("gx", "gy", None, None),
            P("gx", "gy", None),
            P(),
            P(),
        ),
        out_specs=P("gx", "gy", None),
        check_vma=False,
    )
```

time: 33.6 us -> 32.5 us (0.967)
  Pallas kernels: 5.36 us -> 4.77 us
  waiting for transfers between devices: 8.34 us -> 7.95 us
    pallas_call x1, Pallas kernels: 4.38 us -> 3.63 us  [per_device(): pl.pallas_call(outer_kernel, out_shape=(jax.ShapeDtypeStruct((3 * COLS, N...]
    ppermute x1, waiting for transfers between devices: 0.41 us -> 0.01 us  [per_device(): from_second = lax.ppermute(second, 'gx', swaps('gx', True))]
    pallas_call x1 -> x2, Pallas kernels: 0.98 us -> 1.14 us  [later_tiles(): pl.pallas_call(kernel, out_shape=tuple((jax.ShapeDtypeStruct(((2 - n) * C...]
  transfers between devices with their start and end apart: 5 -> 5, of which waited for: 2 -> 1; matrix products, arithmetic and copies ran while one was open for 0% -> 0% of each run, Pallas kernels for 3% -> 4%
where the time goes in v4:
time: 32.5 us; the launch traced here: 32.3 us
  starting transfers between devices  18.7 us (58%)
  waiting for transfers between devices  7.95 us (24%)
  Pallas kernels  4.77 us (15%)
  other arithmetic  0.74 us (2%)
    ppermute x1, waiting for transfers between devices, per_device(): far = lax.ppermute(slow.astype(BF), 'gy', swaps('gy', True))  7.94 us
    ppermute x1, starting transfers between devices, per_device(): far = lax.ppermute(slow.astype(BF), 'gy', swaps('gy', True))  5.76 us
    ppermute x1, starting transfers between devices, per_device(): near = lax.ppermute(own[COLS:], 'gy', swaps('gy', False))  4.68 us
    pallas_call x1, Pallas kernels, per_device(): pl.pallas_call(outer_kernel, out_shape=(jax.ShapeDtypeStruct((3 * COLS, N...  3.63 us
    ppermute x1, starting transfers between devices, per_device(): from_corner = lax.ppermute(corner, 'gx', swaps('gx', True))  3.36 us
    ppermute x1, starting transfers between devices, per_device(): from_first = lax.ppermute(first, 'gx', swaps('gx', False))  2.98 us
    ppermute x1, starting transfers between devices, per_device(): from_second = lax.ppermute(second, 'gx', swaps('gx', True))  1.92 us
    pallas_call x2, Pallas kernels, later_tiles(): pl.pallas_call(kernel, out_shape=tuple((jax.ShapeDtypeStruct(((2 - n) * C...  1.14 us
  transfers between devices with their start and end apart: 5, of which 1 were waited for; matrix products, arithmetic and copies ran while one was open for 0% of the time, Pallas kernels for 4%

profile of v4, /device:TPU:239, one launch (start us, length us, event | category | flops | bytes accessed | tf_op | source)
XLA Modules:
  0.0 32.3 jit_solution(16110244293376955302)
XLA Ops:
  0.0 3.6 %outer.1 = (bf16[384,256]{1,0:T(8,128)(2,1)S(1)}, bf16[128,256]{1,0:T(8,128)(2,1)S(1)}, bf16[3072,256]{1,0:T(8,128)(2,1)S(1)}, f32[24,512]{1,0:T(8,128)S(1)}) custom-call(bf16[512,256]{1,0:T(8,128)(2,1)} %bitcast.4, s32[2,3,2,128]{3,2,1,0:T(2,128)} %bitcast.5, bf16[2,2,128]{2,1,0:T(2,128)(2,1)} %w_hbm.1, s32[14,256]{1,0:T(8,128)} %tt_hbm.1, ...), custom_call_target="tpu_custom_call" | custom-call | tf_op jit(solution)/shard_map/outer/pallas_call | solution.py:231
  3.6 3.0 %collective-permute-start = (bf16[384,256]{1,0:T(8,128)(2,1)S(1)}, bf16[384,256]{1,0:T(8,128)(2,1)S(1)}, u32[]{:S(2)}, u32[]{:S(2)}) collective-permute-start(bf16[384,256]{1,0:T(8,128)(2,1)S(1)} %get-tuple-element.13), channel_id=1, source_target_pairs={{0,128},{128,0},{256,384},{384,256},{1,129},{129,1},{257,385},{385... | collective-permute-start | bytes 589832 | tf_op jit(solution)/shard_map/ppermute | solution.py:256
  6.6 0.7 %shard_map.65 = (bf16[256,256]{1,0:T(8,128)(2,1)S(1)}, f32[128,256]{1,0:T(8,128)S(1)}) custom-call(bf16[3072,256]{1,0:T(8,128)(2,1)S(1)} %get-tuple-element.11.tq_ref, f32[24,512]{1,0:T(8,128)S(1)} %get-tuple-element.12.table_ref), custom_call_target="tpu_custom_call" | custom-call | flops 234881024 | bytes 2097152 | tf_op jit(solution)/shard_map/pallas_call | solution.py:219
  7.4 1.9 %collective-permute-start.1 = (bf16[256,256]{1,0:T(8,128)(2,1)S(1)}, bf16[256,256]{1,0:T(8,128)(2,1)S(1)}, u32[]{:S(2)}, u32[]{:S(2)}) collective-permute-start(bf16[256,256]{1,0:T(8,128)(2,1)S(1)} %get-tuple-element.14), channel_id=1, source_target_pairs={{128,256},{256,128},{129,257},{257,129},{130,258},{258,130},{131,2... | collective-permute-start | bytes 393224 | tf_op jit(solution)/shard_map/ppermute | solution.py:259
  9.3 3.4 %collective-permute-start.3 = (bf16[128,256]{1,0:T(8,128)(2,1)S(1)}, bf16[128,256]{1,0:T(8,128)(2,1)S(1)}, u32[]{:S(2)}, u32[]{:S(2)}) collective-permute-start(bf16[128,256]{1,0:T(8,128)(2,1)S(1)} %get-tuple-element.16), channel_id=1, source_target_pairs={{128,256},{256,128},{129,257},{257,129},{130,258},{258,130},{131,2... | collective-permute-start | bytes 196616 | tf_op jit(solution)/shard_map/ppermute | solution.py:257
  12.7 0.4 %shard_map.64 = f32[256,256]{1,0:T(8,128)S(1)} custom-call(bf16[3072,256]{1,0:T(8,128)(2,1)S(1)} %get-tuple-element.11.tq_ref, f32[24,512]{1,0:T(8,128)S(1)} %get-tuple-element.12.table_ref), custom_call_target="tpu_custom_call" | custom-call | flops 234881024 | bytes 2097152 | tf_op jit(solution)/shard_map/pallas_call | solution.py:219
  13.1 0.0 collective-permute-done.1
  13.1 0.0 collective-permute-done
  13.2 4.7 %collective-permute-start.2 = (f32[128,256]{1,0:T(8,128)S(1)}, f32[128,256]{1,0:T(8,128)S(1)}, u32[]{:S(2)}, u32[]{:S(2)}) collective-permute-start(f32[128,256]{1,0:T(8,128)S(1)} %slice.18), channel_id=1, source_target_pairs={{0,1},{1,0},{2,3},{3,2},{4,5},{5,4},{6,7},{7,6},{8,9},{9,8},{10,11... | collective-permute-start | bytes 393224 | tf_op jit(solution)/shard_map/ppermute | solution.py:264
  17.9 0.0 collective-permute-done.3
  17.9 5.8 %collective-permute-start.4 = (bf16[128,256]{1,0:T(8,128)(2,1)S(1)}, bf16[128,256]{1,0:T(8,128)(2,1)S(1)}, u32[]{:S(2)}, u32[]{:S(2)}) collective-permute-start(bf16[128,256]{1,0:T(8,128)(2,1)S(1)} %add_convert_fusion), channel_id=1, source_target_pairs={{1,2},{2,1},{3,4},{4,3},{5,6},{6,5},{7,8},{8,7},{9,10},{10,9},{11,... | collective-permute-start | bytes 196616 | tf_op jit(solution)/shard_map/ppermute | solution.py:261
  23.7 7.9 %collective-permute-done.4 = bf16[128,256]{1,0:T(8,128)(2,1)S(1)} collective-permute-done((bf16[128,256]{1,0:T(8,128)(2,1)S(1)}, bf16[128,256]{1,0:T(8,128)(2,1)S(1)}, u32[]{:S(2)}, u32[]{:S(2)}) %collective-permute-start.4) | collective-permute-done | bytes 65568 | tf_op jit(solution)/shard_map/ppermute | solution.py:261
  31.6 0.0 collective-permute-done.2
  31.6 0.7 %fusion.1 = f32[16,8,256]{2,1,0:T(8,128)} fusion(f32[128,256]{1,0:T(8,128)S(1)} %collective-permute-done.2, f32[256,256]{1,0:T(8,128)S(1)} %convert_add_fusion, bf16[128,256]{1,0:T(8,128)(2,1)S(1)} %collective-permute-done.4), kind=kLoop, calls=%fused_computation.3 | loop fusion | flops 98304 | bytes 458752 | tf_op jit(solution)/shard_map/reshape | solution.py:266
  (3 shorter events, 0.1 us)
Async XLA Ops:
  3.6 9.5 %collective-permute-start = (bf16[384,256]{1,0:T(8,128)(2,1)S(1)}, bf16[384,256]{1,0:T(8,128)(2,1)S(1)}, u32[]{:S(2)}, u32[]{:S(2)}) collective-permute-start(bf16[384,256]{1,0:T(8,128)(2,1)S(1)} %get-tuple-element.13), channel_id=1, source_target_pairs={{0,128},{128,0},{256,384},{384,256},{1,129},{129,1},{257,385},{385... | collective-permute-start | bytes 589832 | tf_op jit(solution)/shard_map/ppermute | solution.py:256
  7.4 5.7 %collective-permute-start.1 = (bf16[256,256]{1,0:T(8,128)(2,1)S(1)}, bf16[256,256]{1,0:T(8,128)(2,1)S(1)}, u32[]{:S(2)}, u32[]{:S(2)}) collective-permute-start(bf16[256,256]{1,0:T(8,128)(2,1)S(1)} %get-tuple-element.14), channel_id=1, source_target_pairs={{128,256},{256,128},{129,257},{257,129},{130,258},{258,130},{131,2... | collective-permute-start | bytes 393224 | tf_op jit(solution)/shard_map/ppermute | solution.py:259
  9.3 8.6 %collective-permute-start.3 = (bf16[128,256]{1,0:T(8,128)(2,1)S(1)}, bf16[128,256]{1,0:T(8,128)(2,1)S(1)}, u32[]{:S(2)}, u32[]{:S(2)}) collective-permute-start(bf16[128,256]{1,0:T(8,128)(2,1)S(1)} %get-tuple-element.16), channel_id=1, source_target_pairs={{128,256},{256,128},{129,257},{257,129},{130,258},{258,130},{131,2... | collective-permute-start | bytes 196616 | tf_op jit(solution)/shard_map/ppermute | solution.py:257
  13.2 18.4 %collective-permute-start.2 = (f32[128,256]{1,0:T(8,128)S(1)}, f32[128,256]{1,0:T(8,128)S(1)}, u32[]{:S(2)}, u32[]{:S(2)}) collective-permute-start(f32[128,256]{1,0:T(8,128)S(1)} %slice.18), channel_id=1, source_target_pairs={{0,1},{1,0},{2,3},{3,2},{4,5},{5,4},{6,7},{7,6},{8,9},{9,8},{10,11... | collective-permute-start | bytes 393224 | tf_op jit(solution)/shard_map/ppermute | solution.py:264
  17.9 13.7 %collective-permute-start.4 = (bf16[128,256]{1,0:T(8,128)(2,1)S(1)}, bf16[128,256]{1,0:T(8,128)(2,1)S(1)}, u32[]{:S(2)}, u32[]{:S(2)}) collective-permute-start(bf16[128,256]{1,0:T(8,128)(2,1)S(1)} %add_convert_fusion), channel_id=1, source_target_pairs={{1,2},{2,1},{3,4},{4,3},{5,6},{6,5},{7,8},{8,7},{9,10},{10,9},{11,... | collective-permute-start | bytes 196616 | tf_op jit(solution)/shard_map/ppermute | solution.py:261

commit v5 on v4

--- a/solution.py
+++ b/solution.py
@@ -41,7 +41,7 @@
 
 
 def partners():
-    dx = 1 - 2 * (lax.axis_index("gx") % 2)
+    dx = 1
     dy = 1 - 2 * (lax.axis_index("gy") % 2)
     return dx, dy
 
@@ -199,6 +199,11 @@
         own_ref[n * COLS : (n + 1) * COLS, :] = stacked(tq_ref, level, scales, lives[2 + n : 3 + n], 3 + n)
 
 
+def shifts(axis, up):
+    n = lax.axis_size(axis)
+    return [(i, i + 1) if up else (i + 1, i) for i in range(n - 1)]
+
+
 def swaps(axis, odd):
     n = lax.axis_size(axis)
     lower = range(1 if odd else 0, n - 1, 2)
@@ -253,10 +258,10 @@
         compiler_params=PARAMS,
         name="outer",
     )(*(in_hbm(x) for x in (traces.reshape(NJ, NS), geom, trace_weight, traveltime, aperture, class_weight)))
-    from_first = lax.ppermute(first, "gx", swaps("gx", False))
-    from_corner = lax.ppermute(corner, "gx", swaps("gx", True))
+    from_first = lax.ppermute(first, "gx", shifts("gx", True))
+    from_corner = lax.ppermute(corner, "gx", shifts("gx", False))
     second, slow = later_tiles(side_kernel, (BF, F32), tq, table)
-    from_second = lax.ppermute(second, "gx", swaps("gx", True))
+    from_second = lax.ppermute(second, "gx", shifts("gx", False))
     slow = slow + from_first[:COLS].astype(F32) + from_corner.astype(F32)
     far = lax.ppermute(slow.astype(BF), "gy", swaps("gy", True))
     (own,) = later_tiles(own_kernel, (F32,), tq, table)

time: 32.5 us -> 32.8 us (level)
  the two profiles are of different devices: /device:TPU:239 before, /device:TPU:264 now
where the time goes in v5:
time: 32.8 us; the launch traced here: 32.5 us
  starting transfers between devices  16.3 us (50%)
  waiting for transfers between devices  10.6 us (32%)
  Pallas kernels  4.76 us (15%)
  other arithmetic  0.74 us (2%)
    ppermute x1, waiting for transfers between devices, per_device(): far = lax.ppermute(slow.astype(BF), 'gy', swaps('gy', True))  7.79 us
    ppermute x1, starting transfers between devices, per_device(): far = lax.ppermute(slow.astype(BF), 'gy', swaps('gy', True))  6.62 us
    pallas_call x1, Pallas kernels, per_device(): pl.pallas_call(outer_kernel, out_shape=(jax.ShapeDtypeStruct((3 * COLS, N...  3.61 us
    ppermute x1, starting transfers between devices, per_device(): from_first = lax.ppermute(first, 'gx', shifts('gx', True))  3.48 us
    ppermute x1, waiting for transfers between devices, per_device(): from_second = lax.ppermute(second, 'gx', shifts('gx', False))  2.83 us
    ppermute x1, starting transfers between devices, per_device(): from_second = lax.ppermute(second, 'gx', shifts('gx', False))  2.37 us
    ppermute x1, starting transfers between devices, per_device(): near = lax.ppermute(own[COLS:], 'gy', swaps('gy', False))  1.92 us
    ppermute x1, starting transfers between devices, per_device(): from_corner = lax.ppermute(corner, 'gx', shifts('gx', False))  1.92 us
  transfers between devices with their start and end apart: 5, of which 2 were waited for; matrix products, arithmetic and copies ran while one was open for 0% of the time, Pallas kernels for 4%

profile of v5, /device:TPU:264, one launch (start us, length us, event | category | flops | bytes accessed | tf_op | source)
XLA Modules:
  0.0 32.5 jit_solution(11008550964891921269)
XLA Ops:
  0.0 3.6 %outer.1 = (bf16[384,256]{1,0:T(8,128)(2,1)S(1)}, bf16[128,256]{1,0:T(8,128)(2,1)S(1)}, bf16[3072,256]{1,0:T(8,128)(2,1)S(1)}, f32[24,512]{1,0:T(8,128)S(1)}) custom-call(bf16[512,256]{1,0:T(8,128)(2,1)} %bitcast.4, s32[2,3,2,128]{3,2,1,0:T(2,128)} %bitcast.5, bf16[2,2,128]{2,1,0:T(2,128)(2,1)} %w_hbm.1, s32[14,256]{1,0:T(8,128)} %tt_hbm.1, ...), custom_call_target="tpu_custom_call" | custom-call | tf_op jit(solution)/shard_map/outer/pallas_call | solution.py:236
  3.6 3.5 %collective-permute-start = (bf16[384,256]{1,0:T(8,128)(2,1)S(1)}, bf16[384,256]{1,0:T(8,128)(2,1)S(1)}, u32[]{:S(2)}, u32[]{:S(2)}) collective-permute-start(bf16[384,256]{1,0:T(8,128)(2,1)S(1)} %get-tuple-element.13), channel_id=1, source_target_pairs={{0,128},{128,256},{256,384},{1,129},{129,257},{257,385},{2,130},{1... | collective-permute-start | bytes 589832 | tf_op jit(solution)/shard_map/ppermute | solution.py:261
  7.1 0.7 %shard_map.65 = (bf16[256,256]{1,0:T(8,128)(2,1)S(1)}, f32[128,256]{1,0:T(8,128)S(1)}) custom-call(bf16[3072,256]{1,0:T(8,128)(2,1)S(1)} %get-tuple-element.11.tq_ref, f32[24,512]{1,0:T(8,128)S(1)} %get-tuple-element.12.table_ref), custom_call_target="tpu_custom_call" | custom-call | flops 234881024 | bytes 2097152 | tf_op jit(solution)/shard_map/pallas_call | solution.py:224
  7.8 2.4 %collective-permute-start.1 = (bf16[256,256]{1,0:T(8,128)(2,1)S(1)}, bf16[256,256]{1,0:T(8,128)(2,1)S(1)}, u32[]{:S(2)}, u32[]{:S(2)}) collective-permute-start(bf16[256,256]{1,0:T(8,128)(2,1)S(1)} %get-tuple-element.14), channel_id=1, source_target_pairs={{128,0},{256,128},{384,256},{129,1},{257,129},{385,257},{130,2},{2... | collective-permute-start | bytes 393224 | tf_op jit(solution)/shard_map/ppermute | solution.py:264
  10.2 1.9 %collective-permute-start.3 = (bf16[128,256]{1,0:T(8,128)(2,1)S(1)}, bf16[128,256]{1,0:T(8,128)(2,1)S(1)}, u32[]{:S(2)}, u32[]{:S(2)}) collective-permute-start(bf16[128,256]{1,0:T(8,128)(2,1)S(1)} %get-tuple-element.16), channel_id=1, source_target_pairs={{128,0},{256,128},{384,256},{129,1},{257,129},{385,257},{130,2},{2... | collective-permute-start | bytes 196616 | tf_op jit(solution)/shard_map/ppermute | solution.py:262
  12.2 0.4 %shard_map.64 = f32[256,256]{1,0:T(8,128)S(1)} custom-call(bf16[3072,256]{1,0:T(8,128)(2,1)S(1)} %get-tuple-element.11.tq_ref, f32[24,512]{1,0:T(8,128)S(1)} %get-tuple-element.12.table_ref), custom_call_target="tpu_custom_call" | custom-call | flops 234881024 | bytes 2097152 | tf_op jit(solution)/shard_map/pallas_call | solution.py:224
  12.6 2.8 %collective-permute-done.1 = bf16[256,256]{1,0:T(8,128)(2,1)S(1)} collective-permute-done((bf16[256,256]{1,0:T(8,128)(2,1)S(1)}, bf16[256,256]{1,0:T(8,128)(2,1)S(1)}, u32[]{:S(2)}, u32[]{:S(2)}) %collective-permute-start.1) | collective-permute-done | bytes 131104 | tf_op jit(solution)/shard_map/ppermute | solution.py:264
  15.4 0.0 collective-permute-done
  15.5 1.9 %collective-permute-start.2 = (f32[128,256]{1,0:T(8,128)S(1)}, f32[128,256]{1,0:T(8,128)S(1)}, u32[]{:S(2)}, u32[]{:S(2)}) collective-permute-start(f32[128,256]{1,0:T(8,128)S(1)} %slice.18), channel_id=1, source_target_pairs={{0,1},{1,0},{2,3},{3,2},{4,5},{5,4},{6,7},{7,6},{8,9},{9,8},{10,11... | collective-permute-start | bytes 393224 | tf_op jit(solution)/shard_map/ppermute | solution.py:269
  17.4 0.0 collective-permute-done.3
  17.4 6.6 %collective-permute-start.4 = (bf16[128,256]{1,0:T(8,128)(2,1)S(1)}, bf16[128,256]{1,0:T(8,128)(2,1)S(1)}, u32[]{:S(2)}, u32[]{:S(2)}) collective-permute-start(bf16[128,256]{1,0:T(8,128)(2,1)S(1)} %add_convert_fusion), channel_id=1, source_target_pairs={{1,2},{2,1},{3,4},{4,3},{5,6},{6,5},{7,8},{8,7},{9,10},{10,9},{11,... | collective-permute-start | bytes 196616 | tf_op jit(solution)/shard_map/ppermute | solution.py:266
  24.1 7.8 %collective-permute-done.4 = bf16[128,256]{1,0:T(8,128)(2,1)S(1)} collective-permute-done((bf16[128,256]{1,0:T(8,128)(2,1)S(1)}, bf16[128,256]{1,0:T(8,128)(2,1)S(1)}, u32[]{:S(2)}, u32[]{:S(2)}) %collective-permute-start.4) | collective-permute-done | bytes 65568 | tf_op jit(solution)/shard_map/ppermute | solution.py:266
  31.9 0.0 collective-permute-done.2
  31.9 0.7 %fusion.1 = f32[16,8,256]{2,1,0:T(8,128)} fusion(f32[128,256]{1,0:T(8,128)S(1)} %collective-permute-done.2, f32[256,256]{1,0:T(8,128)S(1)} %convert_add_fusion, bf16[128,256]{1,0:T(8,128)(2,1)S(1)} %collective-permute-done.4), kind=kLoop, calls=%fused_computation.3 | loop fusion | flops 98304 | bytes 458752 | tf_op jit(solution)/shard_map/reshape | solution.py:271
  (3 shorter events, 0.1 us)
Async XLA Ops:
  3.6 11.8 %collective-permute-start = (bf16[384,256]{1,0:T(8,128)(2,1)S(1)}, bf16[384,256]{1,0:T(8,128)(2,1)S(1)}, u32[]{:S(2)}, u32[]{:S(2)}) collective-permute-start(bf16[384,256]{1,0:T(8,128)(2,1)S(1)} %get-tuple-element.13), channel_id=1, source_target_pairs={{0,128},{128,256},{256,384},{1,129},{129,257},{257,385},{2,130},{1... | collective-permute-start | bytes 589832 | tf_op jit(solution)/shard_map/ppermute | solution.py:261
  7.8 7.6 %collective-permute-start.1 = (bf16[256,256]{1,0:T(8,128)(2,1)S(1)}, bf16[256,256]{1,0:T(8,128)(2,1)S(1)}, u32[]{:S(2)}, u32[]{:S(2)}) collective-permute-start(bf16[256,256]{1,0:T(8,128)(2,1)S(1)} %get-tuple-element.14), channel_id=1, source_target_pairs={{128,0},{256,128},{384,256},{129,1},{257,129},{385,257},{130,2},{2... | collective-permute-start | bytes 393224 | tf_op jit(solution)/shard_map/ppermute | solution.py:264
  10.2 7.2 %collective-permute-start.3 = (bf16[128,256]{1,0:T(8,128)(2,1)S(1)}, bf16[128,256]{1,0:T(8,128)(2,1)S(1)}, u32[]{:S(2)}, u32[]{:S(2)}) collective-permute-start(bf16[128,256]{1,0:T(8,128)(2,1)S(1)} %get-tuple-element.16), channel_id=1, source_target_pairs={{128,0},{256,128},{384,256},{129,1},{257,129},{385,257},{130,2},{2... | collective-permute-start | bytes 196616 | tf_op jit(solution)/shard_map/ppermute | solution.py:262
  15.5 16.4 %collective-permute-start.2 = (f32[128,256]{1,0:T(8,128)S(1)}, f32[128,256]{1,0:T(8,128)S(1)}, u32[]{:S(2)}, u32[]{:S(2)}) collective-permute-start(f32[128,256]{1,0:T(8,128)S(1)} %slice.18), channel_id=1, source_target_pairs={{0,1},{1,0},{2,3},{3,2},{4,5},{5,4},{6,7},{7,6},{8,9},{9,8},{10,11... | collective-permute-start | bytes 393224 | tf_op jit(solution)/shard_map/ppermute | solution.py:269
  17.4 14.4 %collective-permute-start.4 = (bf16[128,256]{1,0:T(8,128)(2,1)S(1)}, bf16[128,256]{1,0:T(8,128)(2,1)S(1)}, u32[]{:S(2)}, u32[]{:S(2)}) collective-permute-start(bf16[128,256]{1,0:T(8,128)(2,1)S(1)} %add_convert_fusion), channel_id=1, source_target_pairs={{1,2},{2,1},{3,4},{4,3},{5,6},{6,5},{7,8},{8,7},{9,10},{10,9},{11,... | collective-permute-start | bytes 196616 | tf_op jit(solution)/shard_map/ppermute | solution.py:266

commit v6 on v5

--- a/solution.py
+++ b/solution.py
@@ -23,6 +23,7 @@
 
 
 NB = 4
+HALF = COLS // 2
 NREACH = NH + NQ - 1
 PICK_UNROLL = 4
 ROW_X, ROW_Y, ROW_SCALE, ROW_LIVE = 0, 1, 2, 2 + NQ
@@ -46,16 +47,22 @@
     return dx, dy
 
 
-def inline_distance(dx, mx):
-    px = (lax.broadcasted_iota(jnp.int32, (PX, NJ), 0) + PX * dx).astype(F32)
+def inline_distance(first, last, mx):
+    px = (lax.broadcasted_iota(jnp.int32, (last - first, NJ), 0) + first).astype(F32)
     ax = (2.0 * jnp.abs(px - mx) - (DSTEP - 1)) * (0.5 / DSTEP)
-    ax = jnp.broadcast_to(ax[:, None, :], (PX, PY, NJ)).reshape(COLS, NJ)
+    ax = jnp.broadcast_to(ax[:, None, :], (last - first, PY, NJ)).reshape((last - first) * PY, NJ)
     return ax.astype(BF)
+
+
+def near_and_far(dx, mx):
+    low = inline_distance(PX * dx, PX * dx + PX // 2, mx)
+    high = inline_distance(PX * dx + PX // 2, PX * dx + PX, mx)
+    return (low, high) if dx > 0 else (high, low)
 
 
 def crossline_distance(dy, my):
     py = (lax.broadcasted_iota(jnp.int32, (16, NJ), 0) % PY + PY * dy).astype(F32)
-    return down((jnp.abs(py - my) * (1.0 / DSTEP)).astype(BF), COLS)
+    return (jnp.abs(py - my) * (1.0 / DSTEP)).astype(BF)
 
 
 def class_scales(h, w, cw_ref):
@@ -74,16 +81,21 @@
 
 
 def amplitude(level, scales, lives, q):
-    scale = [down(jnp.broadcast_to(scales[q] * live, (16, NJ)).astype(BF), COLS) for live in lives]
+    rows = level.shape[0] // len(lives)
+    scale = [down(jnp.broadcast_to(scales[q] * live, (16, NJ)).astype(BF), rows) for live in lives]
     return jnp.where(level == jnp.asarray(LEVEL + q, BF), jnp.concatenate(scale, axis=0), jnp.zeros((), BF))
 
 
-def stacked(tq_ref, level, scales, lives, n_q):
-    out = jnp.zeros((len(lives) * COLS, NTIME), F32)
-    for q in range(n_q):
+def stacked(tq_ref, level, scales, lives, reach):
+    out = jnp.zeros((level.shape[0], NTIME), F32)
+    for q in reach:
         a = amplitude(level, scales, lives, q)
         out = out + jnp.dot(a, tq_ref[q * NJ : (q + 1) * NJ, :], preferred_element_type=F32)
     return out
+
+
+def levels(ax, ay):
+    return ax + down(ay, ax.shape[0]) + jnp.asarray(LEVEL, BF)
 
 
 def outer_kernel(
@@ -117,11 +129,12 @@
         column = jnp.broadcast_to(hf[:, b * TR : (b + 1) * TR], (TR, TR)).T
         class_ref[b * TR : (b + 1) * TR, :] = jnp.concatenate([column, column], axis=1).astype(BF)
     ays = [crossline_distance(t, my) for t in (-dy, 0, dy)]
-    axs = [inline_distance(t, mx) for t in (dx, -dx)]
+    axs = [near_and_far(t, mx) for t in (dx, -dx)]
     which = ((0, 0), (0, 1), (0, 2), (1, 0))
-    for n in range(len(tiles)):
-        x, y = which[n]
-        level_ref[n * COLS : (n + 1) * COLS, :] = axs[x] + ays[y] + jnp.asarray(LEVEL, BF)
+    for half in range(2):
+        for n, (x, y) in enumerate(which):
+            at = (4 * half + n) * HALF
+            level_ref[at : at + HALF, :] = levels(axs[x][half], ays[y])
     copies[0].wait()
     sample = lax.broadcasted_iota(jnp.int32, (NS, NTIME), 0).astype(F32).astype(BF)
     for c in range(NREACH):
@@ -155,13 +168,14 @@
     lax.fori_loop(0, NJ // 16, pick, 0, unroll=PICK_UNROLL)
     _, _, scales, lives = table_rows(table_ref)
     lives = lives[len(inner_tiles(dx, dy)) :]
-    sums = []
-    for low, high in ((0, 2), (2, 4)):
-        level = level_ref[low * COLS : high * COLS, :]
-        sums.append(stacked(tq_ref, level, scales, lives[low:high], NQ).astype(BF))
-    first_ref[: 2 * COLS] = sums[0]
-    first_ref[2 * COLS :] = sums[1][:COLS]
-    corner_ref[...] = sums[1][COLS:]
+    near = stacked(tq_ref, level_ref[: 4 * HALF, :], scales, lives, range(NQ - 1)).astype(BF)
+    far = stacked(tq_ref, level_ref[4 * HALF :, :], scales, lives, range(1, NQ)).astype(BF)
+    for n in range(3):
+        rows = slice(n * HALF, (n + 1) * HALF)
+        first_ref[n * COLS : n * COLS + HALF, :] = near[rows]
+        first_ref[n * COLS + HALF : (n + 1) * COLS, :] = far[rows]
+    corner_ref[:HALF, :] = far[3 * HALF :]
+    corner_ref[HALF:, :] = near[3 * HALF :]
 
 
 def outer_tiles(dx, dy):
@@ -181,22 +195,25 @@
 def side_kernel(tq_ref, table_ref, second_ref, slow_ref):
     dx, dy = partners()
     mx, my, scales, lives = table_rows(table_ref)
-    ax = inline_distance(-dx, mx)
-    levels = [ax + crossline_distance(ty, my) + jnp.asarray(LEVEL, BF) for ty in (0, dy)]
-    for n, level in enumerate(levels):
-        out = stacked(tq_ref, level, scales, lives[n : n + 1], NQ)
-        second_ref[n * COLS : (n + 1) * COLS, :] = out.astype(BF)
-    level = inline_distance(0, mx) + crossline_distance(-dy, my) + jnp.asarray(LEVEL, BF)
-    slow_ref[...] = stacked(tq_ref, level, scales, lives[4:5], 4)
+    halves = near_and_far(-dx, mx)
+    ays = [crossline_distance(ty, my) for ty in (0, dy)]
+    for half, reach in enumerate((range(NQ - 1), range(1, NQ))):
+        level = jnp.concatenate([levels(halves[half], ay) for ay in ays], axis=0)
+        out = stacked(tq_ref, level, scales, lives[:2], reach).astype(BF)
+        for n in range(2):
+            at = n * COLS + (1 - half) * HALF
+            second_ref[at : at + HALF, :] = out[n * HALF : (n + 1) * HALF]
+    level = levels(inline_distance(0, PX, mx), crossline_distance(-dy, my))
+    slow_ref[...] = stacked(tq_ref, level, scales, lives[4:5], range(4))
 
 
 def own_kernel(tq_ref, table_ref, own_ref):
     _, dy = partners()
     mx, my, scales, lives = table_rows(table_ref)
-    ax = inline_distance(0, mx)
+    ax = inline_distance(0, PX, mx)
     for n, ty in enumerate((0, dy)):
-        level = ax + crossline_distance(ty, my) + jnp.asarray(LEVEL, BF)
-        own_ref[n * COLS : (n + 1) * COLS, :] = stacked(tq_ref, level, scales, lives[2 + n : 3 + n], 3 + n)
+        level = levels(ax, crossline_distance(ty, my))
+        own_ref[n * COLS : (n + 1) * COLS, :] = stacked(tq_ref, level, scales, lives[2 + n : 3 + n], range(3 + n))
 
 
 def shifts(axis, up):

time: 32.8 us -> 32.5 us (level)
  transfers between devices with their start and end apart: 5 -> 5, of which waited for: 2 -> 2; matrix products, arithmetic and copies ran while one was open for 0% -> 0% of each run, Pallas kernels for 4% -> 3%
where the time goes in v6:
time: 32.5 us; the launch traced here: 32.3 us
  starting transfers between devices  16.3 us (50%)
  waiting for transfers between devices  10.6 us (33%)
  Pallas kernels  4.54 us (14%)
  other arithmetic  0.74 us (2%)
    ppermute x1, waiting for transfers between devices, per_device(): far = lax.ppermute(slow.astype(BF), 'gy', swaps('gy', True))  7.78 us
    ppermute x1, starting transfers between devices, per_device(): far = lax.ppermute(slow.astype(BF), 'gy', swaps('gy', True))  6.63 us
    ppermute x1, starting transfers between devices, per_device(): from_first = lax.ppermute(first, 'gx', shifts('gx', True))  3.49 us
    pallas_call x1, Pallas kernels, per_device(): pl.pallas_call(outer_kernel, out_shape=(jax.ShapeDtypeStruct((3 * COLS, N...  3.48 us
    ppermute x1, waiting for transfers between devices, per_device(): from_second = lax.ppermute(second, 'gx', shifts('gx', False))  2.84 us
    ppermute x1, starting transfers between devices, per_device(): from_second = lax.ppermute(second, 'gx', shifts('gx', False))  2.36 us
    ppermute x1, starting transfers between devices, per_device(): from_corner = lax.ppermute(corner, 'gx', shifts('gx', False))  1.92 us
    ppermute x1, starting transfers between devices, per_device(): near = lax.ppermute(own[COLS:], 'gy', swaps('gy', False))  1.92 us
  transfers between devices with their start and end apart: 5, of which 2 were waited for; matrix products, arithmetic and copies ran while one was open for 0% of the time, Pallas kernels for 3%

profile of v6, /device:TPU:264, one launch (start us, length us, event | category | flops | bytes accessed | tf_op | source)
XLA Modules:
  0.0 32.3 jit_solution(16234222182481604922)
XLA Ops:
  0.0 3.5 %outer.1 = (bf16[384,256]{1,0:T(8,128)(2,1)S(1)}, bf16[128,256]{1,0:T(8,128)(2,1)S(1)}, bf16[3072,256]{1,0:T(8,128)(2,1)S(1)}, f32[24,512]{1,0:T(8,128)S(1)}) custom-call(bf16[512,256]{1,0:T(8,128)(2,1)} %bitcast.4, s32[2,3,2,128]{3,2,1,0:T(2,128)} %bitcast.5, bf16[2,2,128]{2,1,0:T(2,128)(2,1)} %w_hbm.1, s32[14,256]{1,0:T(8,128)} %tt_hbm.1, ...), custom_call_target="tpu_custom_call" | custom-call | tf_op jit(solution)/shard_map/outer/pallas_call | solution.py:253
  3.5 3.5 %collective-permute-start = (bf16[384,256]{1,0:T(8,128)(2,1)S(1)}, bf16[384,256]{1,0:T(8,128)(2,1)S(1)}, u32[]{:S(2)}, u32[]{:S(2)}) collective-permute-start(bf16[384,256]{1,0:T(8,128)(2,1)S(1)} %get-tuple-element.13), channel_id=1, source_target_pairs={{0,128},{128,256},{256,384},{1,129},{129,257},{257,385},{2,130},{1... | collective-permute-start | bytes 589832 | tf_op jit(solution)/shard_map/ppermute | solution.py:278
  7.0 0.7 %shard_map.65 = (bf16[256,256]{1,0:T(8,128)(2,1)S(1)}, f32[128,256]{1,0:T(8,128)S(1)}) custom-call(bf16[3072,256]{1,0:T(8,128)(2,1)S(1)} %get-tuple-element.11.tq_ref, f32[24,512]{1,0:T(8,128)S(1)} %get-tuple-element.12.table_ref), custom_call_target="tpu_custom_call" | custom-call | flops 234881024 | bytes 2097152 | tf_op jit(solution)/shard_map/pallas_call | solution.py:241
  7.6 2.4 %collective-permute-start.1 = (bf16[256,256]{1,0:T(8,128)(2,1)S(1)}, bf16[256,256]{1,0:T(8,128)(2,1)S(1)}, u32[]{:S(2)}, u32[]{:S(2)}) collective-permute-start(bf16[256,256]{1,0:T(8,128)(2,1)S(1)} %get-tuple-element.14), channel_id=1, source_target_pairs={{128,0},{256,128},{384,256},{129,1},{257,129},{385,257},{130,2},{2... | collective-permute-start | bytes 393224 | tf_op jit(solution)/shard_map/ppermute | solution.py:281
  10.0 1.9 %collective-permute-start.3 = (bf16[128,256]{1,0:T(8,128)(2,1)S(1)}, bf16[128,256]{1,0:T(8,128)(2,1)S(1)}, u32[]{:S(2)}, u32[]{:S(2)}) collective-permute-start(bf16[128,256]{1,0:T(8,128)(2,1)S(1)} %get-tuple-element.16), channel_id=1, source_target_pairs={{128,0},{256,128},{384,256},{129,1},{257,129},{385,257},{130,2},{2... | collective-permute-start | bytes 196616 | tf_op jit(solution)/shard_map/ppermute | solution.py:279
  11.9 0.4 %shard_map.64 = f32[256,256]{1,0:T(8,128)S(1)} custom-call(bf16[3072,256]{1,0:T(8,128)(2,1)S(1)} %get-tuple-element.11.tq_ref, f32[24,512]{1,0:T(8,128)S(1)} %get-tuple-element.12.table_ref), custom_call_target="tpu_custom_call" | custom-call | flops 234881024 | bytes 2097152 | tf_op jit(solution)/shard_map/pallas_call | solution.py:241
  12.4 2.8 %collective-permute-done.1 = bf16[256,256]{1,0:T(8,128)(2,1)S(1)} collective-permute-done((bf16[256,256]{1,0:T(8,128)(2,1)S(1)}, bf16[256,256]{1,0:T(8,128)(2,1)S(1)}, u32[]{:S(2)}, u32[]{:S(2)}) %collective-permute-start.1) | collective-permute-done | bytes 131104 | tf_op jit(solution)/shard_map/ppermute | solution.py:281
  15.2 0.0 collective-permute-done
  15.3 1.9 %collective-permute-start.2 = (f32[128,256]{1,0:T(8,128)S(1)}, f32[128,256]{1,0:T(8,128)S(1)}, u32[]{:S(2)}, u32[]{:S(2)}) collective-permute-start(f32[128,256]{1,0:T(8,128)S(1)} %slice.18), channel_id=1, source_target_pairs={{0,1},{1,0},{2,3},{3,2},{4,5},{5,4},{6,7},{7,6},{8,9},{9,8},{10,11... | collective-permute-start | bytes 393224 | tf_op jit(solution)/shard_map/ppermute | solution.py:286
  17.2 0.0 collective-permute-done.3
  17.2 6.6 %collective-permute-start.4 = (bf16[128,256]{1,0:T(8,128)(2,1)S(1)}, bf16[128,256]{1,0:T(8,128)(2,1)S(1)}, u32[]{:S(2)}, u32[]{:S(2)}) collective-permute-start(bf16[128,256]{1,0:T(8,128)(2,1)S(1)} %add_convert_fusion), channel_id=1, source_target_pairs={{1,2},{2,1},{3,4},{4,3},{5,6},{6,5},{7,8},{8,7},{9,10},{10,9},{11,... | collective-permute-start | bytes 196616 | tf_op jit(solution)/shard_map/ppermute | solution.py:283
  23.9 7.8 %collective-permute-done.4 = bf16[128,256]{1,0:T(8,128)(2,1)S(1)} collective-permute-done((bf16[128,256]{1,0:T(8,128)(2,1)S(1)}, bf16[128,256]{1,0:T(8,128)(2,1)S(1)}, u32[]{:S(2)}, u32[]{:S(2)}) %collective-permute-start.4) | collective-permute-done | bytes 65568 | tf_op jit(solution)/shard_map/ppermute | solution.py:283
  31.6 0.0 collective-permute-done.2
  31.7 0.7 %fusion.1 = f32[16,8,256]{2,1,0:T(8,128)} fusion(f32[128,256]{1,0:T(8,128)S(1)} %collective-permute-done.2, f32[256,256]{1,0:T(8,128)S(1)} %convert_add_fusion, bf16[128,256]{1,0:T(8,128)(2,1)S(1)} %collective-permute-done.4), kind=kLoop, calls=%fused_computation.3 | loop fusion | flops 98304 | bytes 458752 | tf_op jit(solution)/shard_map/reshape | solution.py:288
  (3 shorter events, 0.1 us)
Async XLA Ops:
  3.5 11.7 %collective-permute-start = (bf16[384,256]{1,0:T(8,128)(2,1)S(1)}, bf16[384,256]{1,0:T(8,128)(2,1)S(1)}, u32[]{:S(2)}, u32[]{:S(2)}) collective-permute-start(bf16[384,256]{1,0:T(8,128)(2,1)S(1)} %get-tuple-element.13), channel_id=1, source_target_pairs={{0,128},{128,256},{256,384},{1,129},{129,257},{257,385},{2,130},{1... | collective-permute-start | bytes 589832 | tf_op jit(solution)/shard_map/ppermute | solution.py:278
  7.6 7.6 %collective-permute-start.1 = (bf16[256,256]{1,0:T(8,128)(2,1)S(1)}, bf16[256,256]{1,0:T(8,128)(2,1)S(1)}, u32[]{:S(2)}, u32[]{:S(2)}) collective-permute-start(bf16[256,256]{1,0:T(8,128)(2,1)S(1)} %get-tuple-element.14), channel_id=1, source_target_pairs={{128,0},{256,128},{384,256},{129,1},{257,129},{385,257},{130,2},{2... | collective-permute-start | bytes 393224 | tf_op jit(solution)/shard_map/ppermute | solution.py:281
  10.0 7.2 %collective-permute-start.3 = (bf16[128,256]{1,0:T(8,128)(2,1)S(1)}, bf16[128,256]{1,0:T(8,128)(2,1)S(1)}, u32[]{:S(2)}, u32[]{:S(2)}) collective-permute-start(bf16[128,256]{1,0:T(8,128)(2,1)S(1)} %get-tuple-element.16), channel_id=1, source_target_pairs={{128,0},{256,128},{384,256},{129,1},{257,129},{385,257},{130,2},{2... | collective-permute-start | bytes 196616 | tf_op jit(solution)/shard_map/ppermute | solution.py:279
  15.3 16.4 %collective-permute-start.2 = (f32[128,256]{1,0:T(8,128)S(1)}, f32[128,256]{1,0:T(8,128)S(1)}, u32[]{:S(2)}, u32[]{:S(2)}) collective-permute-start(f32[128,256]{1,0:T(8,128)S(1)} %slice.18), channel_id=1, source_target_pairs={{0,1},{1,0},{2,3},{3,2},{4,5},{5,4},{6,7},{7,6},{8,9},{9,8},{10,11... | collective-permute-start | bytes 393224 | tf_op jit(solution)/shard_map/ppermute | solution.py:286
  17.2 14.4 %collective-permute-start.4 = (bf16[128,256]{1,0:T(8,128)(2,1)S(1)}, bf16[128,256]{1,0:T(8,128)(2,1)S(1)}, u32[]{:S(2)}, u32[]{:S(2)}) collective-permute-start(bf16[128,256]{1,0:T(8,128)(2,1)S(1)} %add_convert_fusion), channel_id=1, source_target_pairs={{1,2},{2,1},{3,4},{4,3},{5,6},{6,5},{7,8},{8,7},{9,10},{10,9},{11,... | collective-permute-start | bytes 196616 | tf_op jit(solution)/shard_map/ppermute | solution.py:283

commit v7 on v6

--- a/solution.py
+++ b/solution.py
@@ -42,22 +42,29 @@
 
 
 def partners():
-    dx = 1
+    dx = 1 - 2 * (lax.axis_index("gx") % 2)
     dy = 1 - 2 * (lax.axis_index("gy") % 2)
     return dx, dy
 
 
-def inline_distance(first, last, mx):
-    px = (lax.broadcasted_iota(jnp.int32, (last - first, NJ), 0) + first).astype(F32)
+def inline_distance(first, count, mx):
+    px = (lax.broadcasted_iota(jnp.int32, (count, NJ), 0) + first).astype(F32)
     ax = (2.0 * jnp.abs(px - mx) - (DSTEP - 1)) * (0.5 / DSTEP)
-    ax = jnp.broadcast_to(ax[:, None, :], (last - first, PY, NJ)).reshape((last - first) * PY, NJ)
+    ax = jnp.broadcast_to(ax[:, None, :], (count, PY, NJ)).reshape(count * PY, NJ)
     return ax.astype(BF)
 
 
+def halves(dx):
+    near = (PX // 4) * (1 - dx)
+    return near, PX // 2 - near
+
+
 def near_and_far(dx, mx):
-    low = inline_distance(PX * dx, PX * dx + PX // 2, mx)
-    high = inline_distance(PX * dx + PX // 2, PX * dx + PX, mx)
-    return (low, high) if dx > 0 else (high, low)
+    return [inline_distance(PX * dx + half, PX // 2, mx) for half in halves(dx)]
+
+
+def half_rows(n, half):
+    return pl.ds(pl.multiple_of(n * COLS + half * PY, HALF), HALF)
 
 
 def crossline_distance(dy, my):
@@ -170,12 +177,11 @@
     lives = lives[len(inner_tiles(dx, dy)) :]
     near = stacked(tq_ref, level_ref[: 4 * HALF, :], scales, lives, range(NQ - 1)).astype(BF)
     far = stacked(tq_ref, level_ref[4 * HALF :, :], scales, lives, range(1, NQ)).astype(BF)
-    for n in range(3):
-        rows = slice(n * HALF, (n + 1) * HALF)
-        first_ref[n * COLS : n * COLS + HALF, :] = near[rows]
-        first_ref[n * COLS + HALF : (n + 1) * COLS, :] = far[rows]
-    corner_ref[:HALF, :] = far[3 * HALF :]
-    corner_ref[HALF:, :] = near[3 * HALF :]
+    for out, half in zip((near, far), halves(dx), strict=True):
+        for n in range(3):
+            first_ref[half_rows(n, half), :] = out[n * HALF : (n + 1) * HALF]
+    for out, half in zip((near, far), halves(-dx), strict=True):
+        corner_ref[half_rows(0, half), :] = out[3 * HALF :]
 
 
 def outer_tiles(dx, dy):
@@ -195,14 +201,13 @@
 def side_kernel(tq_ref, table_ref, second_ref, slow_ref):
     dx, dy = partners()
     mx, my, scales, lives = table_rows(table_ref)
-    halves = near_and_far(-dx, mx)
+    axs = near_and_far(-dx, mx)
     ays = [crossline_distance(ty, my) for ty in (0, dy)]
-    for half, reach in enumerate((range(NQ - 1), range(1, NQ))):
-        level = jnp.concatenate([levels(halves[half], ay) for ay in ays], axis=0)
+    for ax, half, reach in zip(axs, halves(-dx), (range(NQ - 1), range(1, NQ)), strict=True):
+        level = jnp.concatenate([levels(ax, ay) for ay in ays], axis=0)
         out = stacked(tq_ref, level, scales, lives[:2], reach).astype(BF)
         for n in range(2):
-            at = n * COLS + (1 - half) * HALF
-            second_ref[at : at + HALF, :] = out[n * HALF : (n + 1) * HALF]
+            second_ref[half_rows(n, half), :] = out[n * HALF : (n + 1) * HALF]
     level = levels(inline_distance(0, PX, mx), crossline_distance(-dy, my))
     slow_ref[...] = stacked(tq_ref, level, scales, lives[4:5], range(4))
 
@@ -214,11 +219,6 @@
     for n, ty in enumerate((0, dy)):
         level = levels(ax, crossline_distance(ty, my))
         own_ref[n * COLS : (n + 1) * COLS, :] = stacked(tq_ref, level, scales, lives[2 + n : 3 + n], range(3 + n))
-
-
-def shifts(axis, up):
-    n = lax.axis_size(axis)
-    return [(i, i + 1) if up else (i + 1, i) for i in range(n - 1)]
 
 
 def swaps(axis, odd):
@@ -275,10 +275,10 @@
         compiler_params=PARAMS,
         name="outer",
     )(*(in_hbm(x) for x in (traces.reshape(NJ, NS), geom, trace_weight, traveltime, aperture, class_weight)))
-    from_first = lax.ppermute(first, "gx", shifts("gx", True))
-    from_corner = lax.ppermute(corner, "gx", shifts("gx", False))
+    from_first = lax.ppermute(first, "gx", swaps("gx", False))
+    from_corner = lax.ppermute(corner, "gx", swaps("gx", True))
     second, slow = later_tiles(side_kernel, (BF, F32), tq, table)
-    from_second = lax.ppermute(second, "gx", shifts("gx", False))
+    from_second = lax.ppermute(second, "gx", swaps("gx", True))
     slow = slow + from_first[:COLS].astype(F32) + from_corner.astype(F32)
     far = lax.ppermute(slow.astype(BF), "gy", swaps("gy", True))
     (own,) = later_tiles(own_kernel, (F32,), tq, table)

time: 32.5 us -> 32.3 us (level)
  the two profiles are of different devices: /device:TPU:264 before, /device:TPU:239 now
where the time goes in v7:
time: 32.3 us; the launch traced here: 32.1 us
  starting transfers between devices  18.7 us (58%)
  waiting for transfers between devices  7.93 us (25%)
  Pallas kernels  4.55 us (14%)
  other arithmetic  0.74 us (2%)
    ppermute x1, waiting for transfers between devices, per_device(): far = lax.ppermute(slow.astype(BF), 'gy', swaps('gy', True))  7.92 us
    ppermute x1, starting transfers between devices, per_device(): far = lax.ppermute(slow.astype(BF), 'gy', swaps('gy', True))  5.78 us
    ppermute x1, starting transfers between devices, per_device(): near = lax.ppermute(own[COLS:], 'gy', swaps('gy', False))  4.68 us
    pallas_call x1, Pallas kernels, per_device(): pl.pallas_call(outer_kernel, out_shape=(jax.ShapeDtypeStruct((3 * COLS, N...  3.48 us
    ppermute x1, starting transfers between devices, per_device(): from_corner = lax.ppermute(corner, 'gx', swaps('gx', True))  3.36 us
    ppermute x1, starting transfers between devices, per_device(): from_first = lax.ppermute(first, 'gx', swaps('gx', False))  2.98 us
    ppermute x1, starting transfers between devices, per_device(): from_second = lax.ppermute(second, 'gx', swaps('gx', True))  1.92 us
    pallas_call x2, Pallas kernels, later_tiles(): pl.pallas_call(kernel, out_shape=tuple((jax.ShapeDtypeStruct(((2 - n) * C...  1.07 us
  transfers between devices with their start and end apart: 5, of which 1 were waited for; matrix products, arithmetic and copies ran while one was open for 0% of the time, Pallas kernels for 3%

profile of v7, /device:TPU:239, one launch (start us, length us, event | category | flops | bytes accessed | tf_op | source)
XLA Modules:
  0.0 32.1 jit_solution(8923624116028826398)
XLA Ops:
  0.0 3.5 %outer.1 = (bf16[384,256]{1,0:T(8,128)(2,1)S(1)}, bf16[128,256]{1,0:T(8,128)(2,1)S(1)}, bf16[3072,256]{1,0:T(8,128)(2,1)S(1)}, f32[24,512]{1,0:T(8,128)S(1)}) custom-call(bf16[512,256]{1,0:T(8,128)(2,1)} %bitcast.4, s32[2,3,2,128]{3,2,1,0:T(2,128)} %bitcast.5, bf16[2,2,128]{2,1,0:T(2,128)(2,1)} %w_hbm.1, s32[14,256]{1,0:T(8,128)} %tt_hbm.1, ...), custom_call_target="tpu_custom_call" | custom-call | tf_op jit(solution)/shard_map/outer/pallas_call | solution.py:253
  3.5 3.0 %collective-permute-start = (bf16[384,256]{1,0:T(8,128)(2,1)S(1)}, bf16[384,256]{1,0:T(8,128)(2,1)S(1)}, u32[]{:S(2)}, u32[]{:S(2)}) collective-permute-start(bf16[384,256]{1,0:T(8,128)(2,1)S(1)} %get-tuple-element.13), channel_id=1, source_target_pairs={{0,128},{128,0},{256,384},{384,256},{1,129},{129,1},{257,385},{385... | collective-permute-start | bytes 589832 | tf_op jit(solution)/shard_map/ppermute | solution.py:278
  6.5 0.7 %shard_map.65 = (bf16[256,256]{1,0:T(8,128)(2,1)S(1)}, f32[128,256]{1,0:T(8,128)S(1)}) custom-call(bf16[3072,256]{1,0:T(8,128)(2,1)S(1)} %get-tuple-element.11.tq_ref, f32[24,512]{1,0:T(8,128)S(1)} %get-tuple-element.12.table_ref), custom_call_target="tpu_custom_call" | custom-call | flops 234881024 | bytes 2097152 | tf_op jit(solution)/shard_map/pallas_call | solution.py:241
  7.1 1.9 %collective-permute-start.1 = (bf16[256,256]{1,0:T(8,128)(2,1)S(1)}, bf16[256,256]{1,0:T(8,128)(2,1)S(1)}, u32[]{:S(2)}, u32[]{:S(2)}) collective-permute-start(bf16[256,256]{1,0:T(8,128)(2,1)S(1)} %get-tuple-element.14), channel_id=1, source_target_pairs={{128,256},{256,128},{129,257},{257,129},{130,258},{258,130},{131,2... | collective-permute-start | bytes 393224 | tf_op jit(solution)/shard_map/ppermute | solution.py:281
  9.1 3.4 %collective-permute-start.3 = (bf16[128,256]{1,0:T(8,128)(2,1)S(1)}, bf16[128,256]{1,0:T(8,128)(2,1)S(1)}, u32[]{:S(2)}, u32[]{:S(2)}) collective-permute-start(bf16[128,256]{1,0:T(8,128)(2,1)S(1)} %get-tuple-element.16), channel_id=1, source_target_pairs={{128,256},{256,128},{129,257},{257,129},{130,258},{258,130},{131,2... | collective-permute-start | bytes 196616 | tf_op jit(solution)/shard_map/ppermute | solution.py:279
  12.4 0.4 %shard_map.64 = f32[256,256]{1,0:T(8,128)S(1)} custom-call(bf16[3072,256]{1,0:T(8,128)(2,1)S(1)} %get-tuple-element.11.tq_ref, f32[24,512]{1,0:T(8,128)S(1)} %get-tuple-element.12.table_ref), custom_call_target="tpu_custom_call" | custom-call | flops 234881024 | bytes 2097152 | tf_op jit(solution)/shard_map/pallas_call | solution.py:241
  12.9 0.0 collective-permute-done.1
  12.9 0.0 collective-permute-done
  12.9 4.7 %collective-permute-start.2 = (f32[128,256]{1,0:T(8,128)S(1)}, f32[128,256]{1,0:T(8,128)S(1)}, u32[]{:S(2)}, u32[]{:S(2)}) collective-permute-start(f32[128,256]{1,0:T(8,128)S(1)} %slice.18), channel_id=1, source_target_pairs={{0,1},{1,0},{2,3},{3,2},{4,5},{5,4},{6,7},{7,6},{8,9},{9,8},{10,11... | collective-permute-start | bytes 393224 | tf_op jit(solution)/shard_map/ppermute | solution.py:286
  17.6 0.0 collective-permute-done.3
  17.7 5.8 %collective-permute-start.4 = (bf16[128,256]{1,0:T(8,128)(2,1)S(1)}, bf16[128,256]{1,0:T(8,128)(2,1)S(1)}, u32[]{:S(2)}, u32[]{:S(2)}) collective-permute-start(bf16[128,256]{1,0:T(8,128)(2,1)S(1)} %add_convert_fusion), channel_id=1, source_target_pairs={{1,2},{2,1},{3,4},{4,3},{5,6},{6,5},{7,8},{8,7},{9,10},{10,9},{11,... | collective-permute-start | bytes 196616 | tf_op jit(solution)/shard_map/ppermute | solution.py:283
  23.5 7.9 %collective-permute-done.4 = bf16[128,256]{1,0:T(8,128)(2,1)S(1)} collective-permute-done((bf16[128,256]{1,0:T(8,128)(2,1)S(1)}, bf16[128,256]{1,0:T(8,128)(2,1)S(1)}, u32[]{:S(2)}, u32[]{:S(2)}) %collective-permute-start.4) | collective-permute-done | bytes 65568 | tf_op jit(solution)/shard_map/ppermute | solution.py:283
  31.4 0.0 collective-permute-done.2
  31.4 0.7 %fusion.1 = f32[16,8,256]{2,1,0:T(8,128)} fusion(f32[128,256]{1,0:T(8,128)S(1)} %collective-permute-done.2, f32[256,256]{1,0:T(8,128)S(1)} %convert_add_fusion, bf16[128,256]{1,0:T(8,128)(2,1)S(1)} %collective-permute-done.4), kind=kLoop, calls=%fused_computation.3 | loop fusion | flops 98304 | bytes 458752 | tf_op jit(solution)/shard_map/reshape | solution.py:288
  (3 shorter events, 0.1 us)
Async XLA Ops:
  3.5 9.4 %collective-permute-start = (bf16[384,256]{1,0:T(8,128)(2,1)S(1)}, bf16[384,256]{1,0:T(8,128)(2,1)S(1)}, u32[]{:S(2)}, u32[]{:S(2)}) collective-permute-start(bf16[384,256]{1,0:T(8,128)(2,1)S(1)} %get-tuple-element.13), channel_id=1, source_target_pairs={{0,128},{128,0},{256,384},{384,256},{1,129},{129,1},{257,385},{385... | collective-permute-start | bytes 589832 | tf_op jit(solution)/shard_map/ppermute | solution.py:278
  7.1 5.7 %collective-permute-start.1 = (bf16[256,256]{1,0:T(8,128)(2,1)S(1)}, bf16[256,256]{1,0:T(8,128)(2,1)S(1)}, u32[]{:S(2)}, u32[]{:S(2)}) collective-permute-start(bf16[256,256]{1,0:T(8,128)(2,1)S(1)} %get-tuple-element.14), channel_id=1, source_target_pairs={{128,256},{256,128},{129,257},{257,129},{130,258},{258,130},{131,2... | collective-permute-start | bytes 393224 | tf_op jit(solution)/shard_map/ppermute | solution.py:281
  9.1 8.6 %collective-permute-start.3 = (bf16[128,256]{1,0:T(8,128)(2,1)S(1)}, bf16[128,256]{1,0:T(8,128)(2,1)S(1)}, u32[]{:S(2)}, u32[]{:S(2)}) collective-permute-start(bf16[128,256]{1,0:T(8,128)(2,1)S(1)} %get-tuple-element.16), channel_id=1, source_target_pairs={{128,256},{256,128},{129,257},{257,129},{130,258},{258,130},{131,2... | collective-permute-start | bytes 196616 | tf_op jit(solution)/shard_map/ppermute | solution.py:279
  12.9 18.4 %collective-permute-start.2 = (f32[128,256]{1,0:T(8,128)S(1)}, f32[128,256]{1,0:T(8,128)S(1)}, u32[]{:S(2)}, u32[]{:S(2)}) collective-permute-start(f32[128,256]{1,0:T(8,128)S(1)} %slice.18), channel_id=1, source_target_pairs={{0,1},{1,0},{2,3},{3,2},{4,5},{5,4},{6,7},{7,6},{8,9},{9,8},{10,11... | collective-permute-start | bytes 393224 | tf_op jit(solution)/shard_map/ppermute | solution.py:286
  17.7 13.7 %collective-permute-start.4 = (bf16[128,256]{1,0:T(8,128)(2,1)S(1)}, bf16[128,256]{1,0:T(8,128)(2,1)S(1)}, u32[]{:S(2)}, u32[]{:S(2)}) collective-permute-start(bf16[128,256]{1,0:T(8,128)(2,1)S(1)} %add_convert_fusion), channel_id=1, source_target_pairs={{1,2},{2,1},{3,4},{4,3},{5,6},{6,5},{7,8},{8,7},{9,10},{10,9},{11,... | collective-permute-start | bytes 196616 | tf_op jit(solution)/shard_map/ppermute | solution.py:283

commit v8 on v7

--- a/solution.py
+++ b/solution.py
@@ -25,7 +25,7 @@
 NB = 4
 HALF = COLS // 2
 NREACH = NH + NQ - 1
-PICK_UNROLL = 4
+PICK_UNROLL = 8
 ROW_X, ROW_Y, ROW_SCALE, ROW_LIVE = 0, 1, 2, 2 + NQ
 
 
@@ -175,13 +175,28 @@
     lax.fori_loop(0, NJ // 16, pick, 0, unroll=PICK_UNROLL)
     _, _, scales, lives = table_rows(table_ref)
     lives = lives[len(inner_tiles(dx, dy)) :]
-    near = stacked(tq_ref, level_ref[: 4 * HALF, :], scales, lives, range(NQ - 1)).astype(BF)
-    far = stacked(tq_ref, level_ref[4 * HALF :, :], scales, lives, range(1, NQ)).astype(BF)
-    for out, half in zip((near, far), halves(dx), strict=True):
-        for n in range(3):
-            first_ref[half_rows(n, half), :] = out[n * HALF : (n + 1) * HALF]
-    for out, half in zip((near, far), halves(-dx), strict=True):
-        corner_ref[half_rows(0, half), :] = out[3 * HALF :]
+    place = lax.axis_index("gx")
+    at_end = (place == 0) | (place == lax.axis_size("gx") - 1)
+
+    def stack(count):
+        near = stacked(tq_ref, level_ref[: count * HALF, :], scales, lives[:count], range(NQ - 1)).astype(BF)
+        far_rows = level_ref[4 * HALF : (4 + count) * HALF, :]
+        far = stacked(tq_ref, far_rows, scales, lives[:count], range(1, NQ)).astype(BF)
+        for out, half in zip((near, far), halves(dx), strict=True):
+            for n in range(3):
+                first_ref[half_rows(n, half), :] = out[n * HALF : (n + 1) * HALF]
+        if count == 4:
+            for out, half in zip((near, far), halves(-dx), strict=True):
+                corner_ref[half_rows(0, half), :] = out[3 * HALF :]
+
+    @pl.when(at_end)
+    def end():
+        stack(3)
+        corner_ref[...] = jnp.zeros_like(corner_ref)
+
+    @pl.when(jnp.logical_not(at_end))
+    def middle():
+        stack(4)
 
 
 def outer_tiles(dx, dy):

time: 32.3 us -> 32.1 us (level)
  no operation moved by 1% of the time
where the time goes in v8:
time: 32.1 us; the launch traced here: 31.9 us
  starting transfers between devices  18.5 us (58%)
  waiting for transfers between devices  7.95 us (25%)
  Pallas kernels  4.53 us (14%)
  other arithmetic  0.74 us (2%)
    ppermute x1, waiting for transfers between devices, per_device(): far = lax.ppermute(slow.astype(BF), 'gy', swaps('gy', True))  7.94 us
    ppermute x1, starting transfers between devices, per_device(): far = lax.ppermute(slow.astype(BF), 'gy', swaps('gy', True))  5.76 us
    ppermute x1, starting transfers between devices, per_device(): near = lax.ppermute(own[COLS:], 'gy', swaps('gy', False))  4.69 us
    pallas_call x1, Pallas kernels, per_device(): pl.pallas_call(outer_kernel, out_shape=(jax.ShapeDtypeStruct((3 * COLS, N...  3.45 us
    ppermute x1, starting transfers between devices, per_device(): from_corner = lax.ppermute(corner, 'gx', swaps('gx', True))  3.36 us
    ppermute x1, starting transfers between devices, per_device(): from_first = lax.ppermute(first, 'gx', swaps('gx', False))  2.81 us
    ppermute x1, starting transfers between devices, per_device(): from_second = lax.ppermute(second, 'gx', swaps('gx', True))  1.92 us
    pallas_call x2, Pallas kernels, later_tiles(): pl.pallas_call(kernel, out_shape=tuple((jax.ShapeDtypeStruct(((2 - n) * C...  1.07 us
  transfers between devices with their start and end apart: 5, of which 1 were waited for; matrix products, arithmetic and copies ran while one was open for 0% of the time, Pallas kernels for 3%

profile of v8, /device:TPU:239, one launch (start us, length us, event | category | flops | bytes accessed | tf_op | source)
XLA Modules:
  0.0 31.9 jit_solution(3419028010338220332)
XLA Ops:
  0.0 3.5 %outer.1 = (bf16[384,256]{1,0:T(8,128)(2,1)S(1)}, bf16[128,256]{1,0:T(8,128)(2,1)S(1)}, bf16[3072,256]{1,0:T(8,128)(2,1)S(1)}, f32[24,512]{1,0:T(8,128)S(1)}) custom-call(bf16[512,256]{1,0:T(8,128)(2,1)} %bitcast.4, s32[2,3,2,128]{3,2,1,0:T(2,128)} %bitcast.5, bf16[2,2,128]{2,1,0:T(2,128)(2,1)} %w_hbm.1, s32[14,256]{1,0:T(8,128)} %tt_hbm.1, ...), custom_call_target="tpu_custom_call" | custom-call | tf_op jit(solution)/shard_map/outer/pallas_call | solution.py:268
  3.5 2.8 %collective-permute-start = (bf16[384,256]{1,0:T(8,128)(2,1)S(1)}, bf16[384,256]{1,0:T(8,128)(2,1)S(1)}, u32[]{:S(2)}, u32[]{:S(2)}) collective-permute-start(bf16[384,256]{1,0:T(8,128)(2,1)S(1)} %get-tuple-element.13), channel_id=1, source_target_pairs={{0,128},{128,0},{256,384},{384,256},{1,129},{129,1},{257,385},{385... | collective-permute-start | bytes 589832 | tf_op jit(solution)/shard_map/ppermute | solution.py:293
  6.3 0.7 %shard_map.65 = (bf16[256,256]{1,0:T(8,128)(2,1)S(1)}, f32[128,256]{1,0:T(8,128)S(1)}) custom-call(bf16[3072,256]{1,0:T(8,128)(2,1)S(1)} %get-tuple-element.11.tq_ref, f32[24,512]{1,0:T(8,128)S(1)} %get-tuple-element.12.table_ref), custom_call_target="tpu_custom_call" | custom-call | flops 234881024 | bytes 2097152 | tf_op jit(solution)/shard_map/pallas_call | solution.py:256
  6.9 1.9 %collective-permute-start.1 = (bf16[256,256]{1,0:T(8,128)(2,1)S(1)}, bf16[256,256]{1,0:T(8,128)(2,1)S(1)}, u32[]{:S(2)}, u32[]{:S(2)}) collective-permute-start(bf16[256,256]{1,0:T(8,128)(2,1)S(1)} %get-tuple-element.14), channel_id=1, source_target_pairs={{128,256},{256,128},{129,257},{257,129},{130,258},{258,130},{131,2... | collective-permute-start | bytes 393224 | tf_op jit(solution)/shard_map/ppermute | solution.py:296
  8.9 3.4 %collective-permute-start.3 = (bf16[128,256]{1,0:T(8,128)(2,1)S(1)}, bf16[128,256]{1,0:T(8,128)(2,1)S(1)}, u32[]{:S(2)}, u32[]{:S(2)}) collective-permute-start(bf16[128,256]{1,0:T(8,128)(2,1)S(1)} %get-tuple-element.16), channel_id=1, source_target_pairs={{128,256},{256,128},{129,257},{257,129},{130,258},{258,130},{131,2... | collective-permute-start | bytes 196616 | tf_op jit(solution)/shard_map/ppermute | solution.py:294
  12.2 0.4 %shard_map.64 = f32[256,256]{1,0:T(8,128)S(1)} custom-call(bf16[3072,256]{1,0:T(8,128)(2,1)S(1)} %get-tuple-element.11.tq_ref, f32[24,512]{1,0:T(8,128)S(1)} %get-tuple-element.12.table_ref), custom_call_target="tpu_custom_call" | custom-call | flops 234881024 | bytes 2097152 | tf_op jit(solution)/shard_map/pallas_call | solution.py:256
  12.7 0.0 collective-permute-done.1
  12.7 0.0 collective-permute-done
  12.8 4.7 %collective-permute-start.2 = (f32[128,256]{1,0:T(8,128)S(1)}, f32[128,256]{1,0:T(8,128)S(1)}, u32[]{:S(2)}, u32[]{:S(2)}) collective-permute-start(f32[128,256]{1,0:T(8,128)S(1)} %slice.18), channel_id=1, source_target_pairs={{0,1},{1,0},{2,3},{3,2},{4,5},{5,4},{6,7},{7,6},{8,9},{9,8},{10,11... | collective-permute-start | bytes 393224 | tf_op jit(solution)/shard_map/ppermute | solution.py:301
  17.4 0.0 collective-permute-done.3
  17.5 5.8 %collective-permute-start.4 = (bf16[128,256]{1,0:T(8,128)(2,1)S(1)}, bf16[128,256]{1,0:T(8,128)(2,1)S(1)}, u32[]{:S(2)}, u32[]{:S(2)}) collective-permute-start(bf16[128,256]{1,0:T(8,128)(2,1)S(1)} %add_convert_fusion), channel_id=1, source_target_pairs={{1,2},{2,1},{3,4},{4,3},{5,6},{6,5},{7,8},{8,7},{9,10},{10,9},{11,... | collective-permute-start | bytes 196616 | tf_op jit(solution)/shard_map/ppermute | solution.py:298
  23.3 7.9 %collective-permute-done.4 = bf16[128,256]{1,0:T(8,128)(2,1)S(1)} collective-permute-done((bf16[128,256]{1,0:T(8,128)(2,1)S(1)}, bf16[128,256]{1,0:T(8,128)(2,1)S(1)}, u32[]{:S(2)}, u32[]{:S(2)}) %collective-permute-start.4) | collective-permute-done | bytes 65568 | tf_op jit(solution)/shard_map/ppermute | solution.py:298
  31.2 0.0 collective-permute-done.2
  31.2 0.7 %fusion.1 = f32[16,8,256]{2,1,0:T(8,128)} fusion(f32[128,256]{1,0:T(8,128)S(1)} %collective-permute-done.2, f32[256,256]{1,0:T(8,128)S(1)} %convert_add_fusion, bf16[128,256]{1,0:T(8,128)(2,1)S(1)} %collective-permute-done.4), kind=kLoop, calls=%fused_computation.3 | loop fusion | flops 98304 | bytes 458752 | tf_op jit(solution)/shard_map/reshape | solution.py:303
  (3 shorter events, 0.1 us)
Async XLA Ops:
  3.5 9.2 %collective-permute-start = (bf16[384,256]{1,0:T(8,128)(2,1)S(1)}, bf16[384,256]{1,0:T(8,128)(2,1)S(1)}, u32[]{:S(2)}, u32[]{:S(2)}) collective-permute-start(bf16[384,256]{1,0:T(8,128)(2,1)S(1)} %get-tuple-element.13), channel_id=1, source_target_pairs={{0,128},{128,0},{256,384},{384,256},{1,129},{129,1},{257,385},{385... | collective-permute-start | bytes 589832 | tf_op jit(solution)/shard_map/ppermute | solution.py:293
  6.9 5.7 %collective-permute-start.1 = (bf16[256,256]{1,0:T(8,128)(2,1)S(1)}, bf16[256,256]{1,0:T(8,128)(2,1)S(1)}, u32[]{:S(2)}, u32[]{:S(2)}) collective-permute-start(bf16[256,256]{1,0:T(8,128)(2,1)S(1)} %get-tuple-element.14), channel_id=1, source_target_pairs={{128,256},{256,128},{129,257},{257,129},{130,258},{258,130},{131,2... | collective-permute-start | bytes 393224 | tf_op jit(solution)/shard_map/ppermute | solution.py:296
  8.9 8.6 %collective-permute-start.3 = (bf16[128,256]{1,0:T(8,128)(2,1)S(1)}, bf16[128,256]{1,0:T(8,128)(2,1)S(1)}, u32[]{:S(2)}, u32[]{:S(2)}) collective-permute-start(bf16[128,256]{1,0:T(8,128)(2,1)S(1)} %get-tuple-element.16), channel_id=1, source_target_pairs={{128,256},{256,128},{129,257},{257,129},{130,258},{258,130},{131,2... | collective-permute-start | bytes 196616 | tf_op jit(solution)/shard_map/ppermute | solution.py:294
  12.8 18.5 %collective-permute-start.2 = (f32[128,256]{1,0:T(8,128)S(1)}, f32[128,256]{1,0:T(8,128)S(1)}, u32[]{:S(2)}, u32[]{:S(2)}) collective-permute-start(f32[128,256]{1,0:T(8,128)S(1)} %slice.18), channel_id=1, source_target_pairs={{0,1},{1,0},{2,3},{3,2},{4,5},{5,4},{6,7},{7,6},{8,9},{9,8},{10,11... | collective-permute-start | bytes 393224 | tf_op jit(solution)/shard_map/ppermute | solution.py:301
  17.5 13.7 %collective-permute-start.4 = (bf16[128,256]{1,0:T(8,128)(2,1)S(1)}, bf16[128,256]{1,0:T(8,128)(2,1)S(1)}, u32[]{:S(2)}, u32[]{:S(2)}) collective-permute-start(bf16[128,256]{1,0:T(8,128)(2,1)S(1)} %add_convert_fusion), channel_id=1, source_target_pairs={{1,2},{2,1},{3,4},{4,3},{5,6},{6,5},{7,8},{8,7},{9,10},{10,9},{11,... | collective-permute-start | bytes 196616 | tf_op jit(solution)/shard_map/ppermute | solution.py:298

commit v9 on v8

--- a/solution.py
+++ b/solution.py
@@ -107,7 +107,7 @@
 
 def outer_kernel(
     traces_hbm, geom_hbm, w_hbm, tt_hbm, ap_hbm, cw_hbm,
-    first_ref, corner_ref, tq_ref, table_ref,
+    first_ref, corner_ref, second_ref, tq_ref, table_ref,
     traces_ref, geom_ref, w_ref, tt_ref, ap_ref, cw_ref, sems, class_ref, t_ref, level_ref,
 ):
     pairs = (
@@ -193,10 +193,12 @@
     def end():
         stack(3)
         corner_ref[...] = jnp.zeros_like(corner_ref)
+        second_ref[...] = jnp.zeros_like(second_ref)
 
     @pl.when(jnp.logical_not(at_end))
     def middle():
         stack(4)
+        side_tiles(tq_ref, table_ref, second_ref)
 
 
 def outer_tiles(dx, dy):
@@ -213,7 +215,7 @@
     return mx, my, scales, [table_ref[ROW_LIVE + n : ROW_LIVE + n + 1, :] for n in range(9)]
 
 
-def side_kernel(tq_ref, table_ref, second_ref, slow_ref):
+def side_tiles(tq_ref, table_ref, second_ref):
     dx, dy = partners()
     mx, my, scales, lives = table_rows(table_ref)
     axs = near_and_far(-dx, mx)
@@ -223,6 +225,11 @@
         out = stacked(tq_ref, level, scales, lives[:2], reach).astype(BF)
         for n in range(2):
             second_ref[half_rows(n, half), :] = out[n * HALF : (n + 1) * HALF]
+
+
+def slow_kernel(tq_ref, table_ref, slow_ref):
+    _, dy = partners()
+    mx, my, scales, lives = table_rows(table_ref)
     level = levels(inline_distance(0, PX, mx), crossline_distance(-dy, my))
     slow_ref[...] = stacked(tq_ref, level, scales, lives[4:5], range(4))
 
@@ -252,12 +259,12 @@
     return pltpu.with_memory_space_constraint(x, pltpu.HBM)
 
 
-def later_tiles(kernel, dtypes, tq, table):
+def later_tiles(kernel, tiles, tq, table):
     return pl.pallas_call(
         kernel,
-        out_shape=tuple(jax.ShapeDtypeStruct(((2 - n) * COLS, NTIME), t) for n, t in enumerate(dtypes)),
+        out_shape=jax.ShapeDtypeStruct((tiles * COLS, NTIME), F32),
         in_specs=[VMEM] * 2,
-        out_specs=(VMEM,) * len(dtypes),
+        out_specs=VMEM,
         compiler_params=PARAMS,
         cost_estimate=LATER_COST,
     )(tq, table)
@@ -265,16 +272,17 @@
 
 def per_device(traces, aperture, geometry, trace_weight, class_weight, traveltime):
     geom = jnp.transpose(geometry, (0, 2, 1, 3))
-    first, corner, tq, table = pl.pallas_call(
+    first, corner, second, tq, table = pl.pallas_call(
         outer_kernel,
         out_shape=(
             jax.ShapeDtypeStruct((3 * COLS, NTIME), BF),
             jax.ShapeDtypeStruct((COLS, NTIME), BF),
+            jax.ShapeDtypeStruct((2 * COLS, NTIME), BF),
             jax.ShapeDtypeStruct((NQ * NJ, NTIME), BF),
             jax.ShapeDtypeStruct((24, NJ), F32),
         ),
         in_specs=[HBM] * 6,
-        out_specs=(VMEM,) * 4,
+        out_specs=(VMEM,) * 5,
         scratch_shapes=[
             pltpu.VMEM((NJ, NS), BF),
             pltpu.VMEM((2, 3, 2, TR), jnp.int32),
@@ -292,11 +300,11 @@
     )(*(in_hbm(x) for x in (traces.reshape(NJ, NS), geom, trace_weight, traveltime, aperture, class_weight)))
     from_first = lax.ppermute(first, "gx", swaps("gx", False))
     from_corner = lax.ppermute(corner, "gx", swaps("gx", True))
-    second, slow = later_tiles(side_kernel, (BF, F32), tq, table)
+    slow = later_tiles(slow_kernel, 1, tq, table)
     from_second = lax.ppermute(second, "gx", swaps("gx", True))
     slow = slow + from_first[:COLS].astype(F32) + from_corner.astype(F32)
     far = lax.ppermute(slow.astype(BF), "gy", swaps("gy", True))
-    (own,) = later_tiles(own_kernel, (F32,), tq, table)
+    own = later_tiles(own_kernel, 2, tq, table)
     own = own + from_first[COLS:].astype(F32) + from_second.astype(F32)
     near = lax.ppermute(own[COLS:], "gy", swaps("gy", False))
     image = own[:COLS] + near + far.astype(F32)

time: 32.1 us -> 31.4 us (0.978)
  starting transfers between devices: 18.5 us -> 17.9 us
    pallas_call x1, Pallas kernels: 3.45 us -> 3.8 us  [per_device(): pl.pallas_call(outer_kernel, out_shape=(jax.ShapeDtypeStruct((3 * COLS, N...]
    ppermute x1, starting transfers between devices: 2.81 us -> 2.47 us  [per_device(): from_first = lax.ppermute(first, 'gx', swaps('gx', False))]
    pallas_call x2, Pallas kernels: 1.07 us -> 0.74 us  [later_tiles(): pl.pallas_call(kernel, out_shape=jax.ShapeDtypeStruct((tiles * COLS, NTIM...]
    ppermute x1, starting transfers between devices: 4.69 us -> 4.35 us  [per_device(): near = lax.ppermute(own[COLS:], 'gy', swaps('gy', False))]
  transfers between devices with their start and end apart: 5 -> 5, of which waited for: 1 -> 1; matrix products, arithmetic and copies ran while one was open for 0% -> 0% of each run, Pallas kernels for 3% -> 2%
where the time goes in v9:
time: 31.4 us; the launch traced here: 31.2 us
  starting transfers between devices  17.9 us (57%)
  waiting for transfers between devices  7.94 us (25%)
  Pallas kernels  4.54 us (14%)
  other arithmetic  0.74 us (2%)
    ppermute x1, waiting for transfers between devices, per_device(): far = lax.ppermute(slow.astype(BF), 'gy', swaps('gy', True))  7.93 us
    ppermute x1, starting transfers between devices, per_device(): far = lax.ppermute(slow.astype(BF), 'gy', swaps('gy', True))  5.78 us
    ppermute x1, starting transfers between devices, per_device(): near = lax.ppermute(own[COLS:], 'gy', swaps('gy', False))  4.35 us
    pallas_call x1, Pallas kernels, per_device(): pl.pallas_call(outer_kernel, out_shape=(jax.ShapeDtypeStruct((3 * COLS, N...  3.8 us
    ppermute x1, starting transfers between devices, per_device(): from_corner = lax.ppermute(corner, 'gx', swaps('gx', True))  3.36 us
    ppermute x1, starting transfers between devices, per_device(): from_first = lax.ppermute(first, 'gx', swaps('gx', False))  2.47 us
    ppermute x1, starting transfers between devices, per_device(): from_second = lax.ppermute(second, 'gx', swaps('gx', True))  1.92 us
    pallas_call x2, Pallas kernels, later_tiles(): pl.pallas_call(kernel, out_shape=jax.ShapeDtypeStruct((tiles * COLS, NTIM...  0.74 us
  transfers between devices with their start and end apart: 5, of which 1 were waited for; matrix products, arithmetic and copies ran while one was open for 0% of the time, Pallas kernels for 2%

profile of v9, /device:TPU:239, one launch (start us, length us, event | category | flops | bytes accessed | tf_op | source)
XLA Modules:
  0.0 31.2 jit_solution(6515109252607184482)
XLA Ops:
  0.0 3.8 %outer.1 = (bf16[384,256]{1,0:T(8,128)(2,1)S(1)}, bf16[128,256]{1,0:T(8,128)(2,1)S(1)}, bf16[256,256]{1,0:T(8,128)(2,1)S(1)}, bf16[3072,256]{1,0:T(8,128)(2,1)S(1)}, f32[24,512]{1,0:T(8,128)S(1)}) custom-call(bf16[512,256]{1,0:T(8,128)(2,1)} %bitcast.4, s32[2,3,2,128]{3,2,1,0:T(2,128)} %bitcast.5, bf16[2,2,128]{2,1,0:T(2,128)(2,1)} %w_hbm.1, ...), custom_call_target="tpu_custom_call" | custom-call | tf_op jit(solution)/shard_map/outer/pallas_call | solution.py:275
  3.8 2.5 %collective-permute-start = (bf16[384,256]{1,0:T(8,128)(2,1)S(1)}, bf16[384,256]{1,0:T(8,128)(2,1)S(1)}, u32[]{:S(2)}, u32[]{:S(2)}) collective-permute-start(bf16[384,256]{1,0:T(8,128)(2,1)S(1)} %get-tuple-element.12), channel_id=1, source_target_pairs={{0,128},{128,0},{256,384},{384,256},{1,129},{129,1},{257,385},{385... | collective-permute-start | bytes 589832 | tf_op jit(solution)/shard_map/ppermute | solution.py:301
  6.3 1.9 %collective-permute-start.1 = (bf16[256,256]{1,0:T(8,128)(2,1)S(1)}, bf16[256,256]{1,0:T(8,128)(2,1)S(1)}, u32[]{:S(2)}, u32[]{:S(2)}) collective-permute-start(bf16[256,256]{1,0:T(8,128)(2,1)S(1)} %get-tuple-element.13), channel_id=1, source_target_pairs={{128,256},{256,128},{129,257},{257,129},{130,258},{258,130},{131,2... | collective-permute-start | bytes 393224 | tf_op jit(solution)/shard_map/ppermute | solution.py:304
  8.2 3.4 %collective-permute-start.3 = (bf16[128,256]{1,0:T(8,128)(2,1)S(1)}, bf16[128,256]{1,0:T(8,128)(2,1)S(1)}, u32[]{:S(2)}, u32[]{:S(2)}) collective-permute-start(bf16[128,256]{1,0:T(8,128)(2,1)S(1)} %get-tuple-element.14), channel_id=1, source_target_pairs={{128,256},{256,128},{129,257},{257,129},{130,258},{258,130},{131,2... | collective-permute-start | bytes 196616 | tf_op jit(solution)/shard_map/ppermute | solution.py:302
  11.6 0.3 shard_map.65
  11.9 0.4 %shard_map.64 = f32[256,256]{1,0:T(8,128)S(1)} custom-call(bf16[3072,256]{1,0:T(8,128)(2,1)S(1)} %get-tuple-element.10.tq_ref, f32[24,512]{1,0:T(8,128)S(1)} %get-tuple-element.11.table_ref), custom_call_target="tpu_custom_call" | custom-call | flops 234881024 | bytes 2097152 | tf_op jit(solution)/shard_map/pallas_call | solution.py:263
  12.3 0.0 collective-permute-done.1
  12.3 0.0 collective-permute-done
  12.4 4.4 %collective-permute-start.2 = (f32[128,256]{1,0:T(8,128)S(1)}, f32[128,256]{1,0:T(8,128)S(1)}, u32[]{:S(2)}, u32[]{:S(2)}) collective-permute-start(f32[128,256]{1,0:T(8,128)S(1)} %slice.18), channel_id=1, source_target_pairs={{0,1},{1,0},{2,3},{3,2},{4,5},{5,4},{6,7},{7,6},{8,9},{9,8},{10,11... | collective-permute-start | bytes 393224 | tf_op jit(solution)/shard_map/ppermute | solution.py:309
  16.8 0.0 collective-permute-done.3
  16.8 5.8 %collective-permute-start.4 = (bf16[128,256]{1,0:T(8,128)(2,1)S(1)}, bf16[128,256]{1,0:T(8,128)(2,1)S(1)}, u32[]{:S(2)}, u32[]{:S(2)}) collective-permute-start(bf16[128,256]{1,0:T(8,128)(2,1)S(1)} %add_convert_fusion), channel_id=1, source_target_pairs={{1,2},{2,1},{3,4},{4,3},{5,6},{6,5},{7,8},{8,7},{9,10},{10,9},{11,... | collective-permute-start | bytes 196616 | tf_op jit(solution)/shard_map/ppermute | solution.py:306
  22.6 7.9 %collective-permute-done.4 = bf16[128,256]{1,0:T(8,128)(2,1)S(1)} collective-permute-done((bf16[128,256]{1,0:T(8,128)(2,1)S(1)}, bf16[128,256]{1,0:T(8,128)(2,1)S(1)}, u32[]{:S(2)}, u32[]{:S(2)}) %collective-permute-start.4) | collective-permute-done | bytes 65568 | tf_op jit(solution)/shard_map/ppermute | solution.py:306
  30.5 0.0 collective-permute-done.2
  30.5 0.7 %fusion.1 = f32[16,8,256]{2,1,0:T(8,128)} fusion(f32[128,256]{1,0:T(8,128)S(1)} %collective-permute-done.2, f32[256,256]{1,0:T(8,128)S(1)} %convert_add_fusion, bf16[128,256]{1,0:T(8,128)(2,1)S(1)} %collective-permute-done.4), kind=kLoop, calls=%fused_computation.3 | loop fusion | flops 98304 | bytes 458752 | tf_op jit(solution)/shard_map/reshape | solution.py:311
  (3 shorter events, 0.1 us)
Async XLA Ops:
  3.8 8.5 %collective-permute-start = (bf16[384,256]{1,0:T(8,128)(2,1)S(1)}, bf16[384,256]{1,0:T(8,128)(2,1)S(1)}, u32[]{:S(2)}, u32[]{:S(2)}) collective-permute-start(bf16[384,256]{1,0:T(8,128)(2,1)S(1)} %get-tuple-element.12), channel_id=1, source_target_pairs={{0,128},{128,0},{256,384},{384,256},{1,129},{129,1},{257,385},{385... | collective-permute-start | bytes 589832 | tf_op jit(solution)/shard_map/ppermute | solution.py:301
  6.3 6.1 %collective-permute-start.1 = (bf16[256,256]{1,0:T(8,128)(2,1)S(1)}, bf16[256,256]{1,0:T(8,128)(2,1)S(1)}, u32[]{:S(2)}, u32[]{:S(2)}) collective-permute-start(bf16[256,256]{1,0:T(8,128)(2,1)S(1)} %get-tuple-element.13), channel_id=1, source_target_pairs={{128,256},{256,128},{129,257},{257,129},{130,258},{258,130},{131,2... | collective-permute-start | bytes 393224 | tf_op jit(solution)/shard_map/ppermute | solution.py:304
  8.2 8.6 %collective-permute-start.3 = (bf16[128,256]{1,0:T(8,128)(2,1)S(1)}, bf16[128,256]{1,0:T(8,128)(2,1)S(1)}, u32[]{:S(2)}, u32[]{:S(2)}) collective-permute-start(bf16[128,256]{1,0:T(8,128)(2,1)S(1)} %get-tuple-element.14), channel_id=1, source_target_pairs={{128,256},{256,128},{129,257},{257,129},{130,258},{258,130},{131,2... | collective-permute-start | bytes 196616 | tf_op jit(solution)/shard_map/ppermute | solution.py:302
  12.4 18.1 %collective-permute-start.2 = (f32[128,256]{1,0:T(8,128)S(1)}, f32[128,256]{1,0:T(8,128)S(1)}, u32[]{:S(2)}, u32[]{:S(2)}) collective-permute-start(f32[128,256]{1,0:T(8,128)S(1)} %slice.18), channel_id=1, source_target_pairs={{0,1},{1,0},{2,3},{3,2},{4,5},{5,4},{6,7},{7,6},{8,9},{9,8},{10,11... | collective-permute-start | bytes 393224 | tf_op jit(solution)/shard_map/ppermute | solution.py:309
  16.8 13.7 %collective-permute-start.4 = (bf16[128,256]{1,0:T(8,128)(2,1)S(1)}, bf16[128,256]{1,0:T(8,128)(2,1)S(1)}, u32[]{:S(2)}, u32[]{:S(2)}) collective-permute-start(bf16[128,256]{1,0:T(8,128)(2,1)S(1)} %add_convert_fusion), channel_id=1, source_target_pairs={{1,2},{2,1},{3,4},{4,3},{5,6},{6,5},{7,8},{8,7},{9,10},{10,9},{11,... | collective-permute-start | bytes 196616 | tf_op jit(solution)/shard_map/ppermute | solution.py:306
